TPU v7x, 32 devices: a whole 2x2x4 slice. The times are simulated.
32 devices in a mesh: grp: 2 (over x), row: 16 (over z, y, core).
Axes of the slice: x: 2, y: 2, z: 4, core: 2. Of those that a mesh axis runs over, the one named last changes fastest.
Arguments:
- alignment: bfloat16 [128, 128, 256], P(('grp', 'row')), parts along dimension 0, may hold values from -6 to 6
- seq_flags: int32 [128], P(('grp', 'row')), parts along dimension 0, may hold values 0 or 1
- crop_flags: int32 [256], P('grp'), parts along dimension 0, may hold values 0 or 1
- norm_gain: float32 [256], replicated, may hold values from 0.5 to 1.5
- norm_bias: float32 [256], replicated, may hold values from -3 to 3
- left_weight: bfloat16 [256, 32], replicated, may hold values from -0.375 to 0.375
- left_bias: float32 [32], replicated, may hold values from -3 to 3
- right_weight: bfloat16 [256, 32], replicated, may hold values from -0.375 to 0.375
- right_bias: float32 [32], replicated, may hold values from -3 to 3
- out_weight: bfloat16 [1024, 128], replicated, may hold values from -0.1875 to 0.1875
- out_bias: float32 [128], replicated, may hold values from -3 to 3
Outputs:
- pair_update: bfloat16 [256, 128, 128], P(('grp', 'row')), parts along dimension 0
There are 2 independent parts, one for each index of `grp`. A program takes and returns all parts, laid end to end along the dimension named above; an argument that names none is the same for every part. Nothing has to cross between parts.
All inputs are finite; a program needn't handle non-finite values. No bound on the sum of `seq_flags` on one device may be relied on, other than what follows from the above.
Results may differ from a plain program's by a relative error of at most 0.004.
Values may be sent and summed in bfloat16 or wider, within the bound.
No kernel may reach another device: no remote copies, remote signals or barrier semaphores. Data moves between devices by JAX's collectives and lax.ppermute only.
A program may use at most 128 MiB of HBM per device.

v0:
```python
import jax
import jax.numpy as jnp
from jax import lax
from jax.sharding import PartitionSpec as P


def normalize(values, norm_gain, norm_bias):
    values = values.astype(jnp.float32)
    average = jnp.mean(values, axis=-1, keepdims=True)
    variance = jnp.mean((values - average) ** 2, axis=-1, keepdims=True)
    return (values - average) * lax.rsqrt(variance + 1e-05) * norm_gain + norm_bias


def project(normed, weight, bias, scaling):
    product = jnp.einsum(
        "src,cd->srd", normed, weight.astype(jnp.float32), precision=lax.Precision.HIGHEST
    )
    return ((product + bias) * scaling).astype(jnp.bfloat16)


def pair_tile(
    left_flat, column_piece, crop_rows, crop_cols, live_count, out_weight, out_bias, channels
):
    rows_here = crop_rows.shape[0]
    width_cols = column_piece.shape[1] // channels
    sums = lax.dot_general(
        left_flat, column_piece, (((0,), (0,)), ((), ())), preferred_element_type=jnp.float32
    )
    outer_sum = sums.reshape(rows_here, channels, width_cols, channels).transpose(0, 2, 1, 3)
    outer_sum = outer_sum.reshape(rows_here * width_cols, channels * channels).astype(jnp.bfloat16)
    projected = jnp.dot(outer_sum, out_weight, preferred_element_type=jnp.float32)
    projected = projected.reshape(rows_here, width_cols, out_weight.shape[1])
    divisor = jnp.maximum(live_count * crop_rows[:, None] * crop_cols[None, :], 1.0)
    return (projected / divisor[:, :, None] + out_bias).astype(jnp.bfloat16)


def column_blocks(
    left_flat, column_piece, crop_rows, crop_cols, live_count, out_weight, out_bias, channels
):
    rows_here = crop_rows.shape[0]
    width_cols = column_piece.shape[1] // channels
    span = max(1, 2048 // rows_here)
    if width_cols > span and width_cols % span == 0:

        def one_block(block_index):
            start = block_index * span
            piece_block = lax.dynamic_slice_in_dim(
                column_piece, start * channels, span * channels, 1
            )
            crop_block = lax.dynamic_slice_in_dim(crop_cols, start, span, 0)
            return pair_tile(
                left_flat,
                piece_block,
                crop_rows,
                crop_block,
                live_count,
                out_weight,
                out_bias,
                channels,
            )

        stacked = lax.map(one_block, jnp.arange(width_cols // span, dtype=jnp.int32))
        return stacked.transpose(1, 0, 2, 3).reshape(rows_here, width_cols, out_weight.shape[1])
    return pair_tile(
        left_flat, column_piece, crop_rows, crop_cols, live_count, out_weight, out_bias, channels
    )


def per_device(
    alignment,
    seq_flags,
    crop_flags,
    norm_gain,
    norm_bias,
    left_weight,
    left_bias,
    right_weight,
    right_bias,
    out_weight,
    out_bias,
):
    channels = left_weight.shape[1]
    devices_row = lax.axis_size("row")
    residues = alignment.shape[1]
    rows_here = residues // devices_row
    crop_float = crop_flags.astype(jnp.float32)
    my_index = lax.axis_index("row")
    crop_rows = lax.dynamic_slice_in_dim(crop_float, my_index * rows_here, rows_here, 0)
    regrouped = lax.all_to_all(alignment, "row", split_axis=1, concat_axis=0, tiled=True)
    all_flags = lax.all_gather(seq_flags, "row", axis=0, tiled=True)
    flag_float = all_flags.astype(jnp.float32)
    live_count = jnp.sum(flag_float)
    normed = normalize(regrouped, norm_gain, norm_bias)
    scaling = flag_float[:, None, None] * crop_rows[None, :, None]
    left = project(normed, left_weight, left_bias, scaling)
    right = project(normed, right_weight, right_bias, scaling)
    sequences = left.shape[0]
    left_flat = left.reshape(sequences, rows_here * channels)
    right_flat = right.reshape(sequences, rows_here * channels)
    return column_blocks(
        left_flat,
        lax.all_gather(right_flat, "row", axis=1, tiled=True),
        crop_rows,
        crop_float,
        live_count,
        out_weight,
        out_bias,
        channels,
    )


def solution(mesh):
    return jax.shard_map(
        per_device,
        mesh=mesh,
        in_specs=(
            P(("grp", "row"), None, None),
            P(("grp", "row")),
            P("grp"),
            P(),
            P(),
            P(),
            P(),
            P(),
            P(),
            P(),
            P(),
        ),
        out_specs=P(("grp", "row"), None, None),
        check_vma=False,
    )
```

profile of v0, /device:TPU:0, one launch (start us, length us, event | category | flops | bytes accessed | tf_op | source)
XLA Modules:
  0.0 54.4 jit_solution(9916558976857848131)
XLA Ops:
  0.0 1.9 %copy.75 = bf16[4,128,256]{2,0,1:T(4,128)(2,1)} copy(bf16[4,128,256]{2,1,0:T(8,128)(2,1)} %param.11) | data formatting | bytes 524288 | tf_op args[0]
  1.9 7.4 %all-to-all-start = ((bf16[4,128,256]{2,0,1:T(4,128)(2,1)}), bf16[4,128,256]{2,0,1:T(4,128)(2,1)S(1)}, u32[]{:S(2)}, u32[]{:S(2)}) async-start(bf16[4,128,256]{2,0,1:T(4,128)(2,1)} %copy.75), calls=%async_computation | async-start | bytes 524288 | tf_op jit(solution)/shard_map/all_to_all | solution.py:89
  9.3 0.0 copy-start.1
  9.3 0.0 copy-start.5
  9.4 1.3 %dynamic-slice = u32[1]{0:T(128)} dynamic-slice(u32[32]{0:T(128)} %constant.24, u32[]{:T(128)S(6)} %add.58), dynamic_slice_sizes={1} | dynamic-slice | bytes 12
  11.4 0.9 %dynamic-update-slice = s32[64]{0:T(128)S(1)} dynamic-update-slice(s32[64]{0:T(128)S(1)} %broadcast.80, s32[4]{0:T(128)} %param.12, u32[]{:T(128)} %bitcast.7) | dynamic-update-slice | bytes 36
  12.2 12.4 %all-reduce = s32[64]{0:T(128)S(1)} all-reduce(s32[64]{0:T(128)S(1)} %dynamic-update-slice), channel_id=1, replica_groups=mesh['grp'=2,'row'=16] {'row'}, use_global_device_ids=true, to_apply=%add | all-reduce | flops 64 | bytes 512
  24.7 0.7 %convert_reduce_fusion = f32[]{:T(128)} fusion(s32[64]{0:T(128)S(1)} %all-reduce), kind=kLoop, calls=%fused_computation.27 | loop fusion | flops 127 | bytes 260 | tf_op jit(solution)/shard_map/reduce_sum | solution.py:92
  25.4 0.7 %convert_element_type.51 = f32[128]{0:T(128)S(1)} convert(s32[128]{0:T(128)} %param.13) | non-fusion elementwise | flops 128 | bytes 1024 | tf_op jit(solution)/shard_map/convert_element_type | solution.py:86
  26.0 0.8 %broadcast_multiply_fusion.2 = (f32[8]{0:T(128)S(1)}, f32[8]{0:T(128)S(1)}) fusion(f32[]{:T(128)} %convert_reduce_fusion, f32[128]{0:T(128)S(1)} %convert_element_type.51, s32[]{:T(128)S(6)} %select_n.3), kind=kLoop, calls=%fused_computation.26 | loop fusion | flops 8 | bytes 104 | tf_op jit(solution)/shard_map/mul | solution.py:33
  26.8 0.1 multiply_maximum_fusion
  26.9 0.1 broadcast_multiply_fusion
  26.9 0.1 fusion.10
  27.1 0.1 copy.79
  27.2 0.1 copy.81
  27.2 0.1 copy.80
  27.3 0.3 multiply_reduce_fusion
  27.6 0.1 copy.83
  27.7 0.1 copy.84
  27.9 0.0 copy-start.2
  27.9 0.0 copy-start.6
  27.9 0.2 fusion.9
  28.2 0.4 fusion.5
  28.5 0.1 copy.86
  28.7 21.0 %all_gather.7 = bf16[64,4096]{0,1:T(8,128)(2,1)S(1)} all-gather(bf16[64,256]{0,1:T(8,128)(2,1)S(1)} %bitcast.57), channel_id=1, replica_groups=mesh['grp'=2,'row'=16] {'row'}, dimensions={1}, use_global_device_ids=true | all-gather | bytes 557056 | tf_op jit(solution)/shard_map/all_gather | solution.py:102
  49.7 1.1 %copy.87 = bf16[128,32,64]{0,2,1:T(8,128)(2,1)S(1)} copy(bf16[128,32,64]{2,1,0:T(8,128)(2,1)S(1)} %bitcast.55) | data formatting | bytes 1048576 | tf_op jit(solution)/shard_map/dot_general | solution.py:26
  50.8 0.4 fusion.4
  51.2 0.1 copy.85
  51.3 0.7 %convert_bitcast_fusion = bf16[8,128,32,32]{1,2,3,0:T(8,128)(2,1)S(1)} fusion(bf16[128,32,64]{0,2,1:T(8,128)(2,1)S(1)} %copy.87, bf16[64,8,32]{0,2,1:T(8,128)(2,1)S(1)} %copy.85), kind=kOutput, calls=%fused_computation | convolution fusion | flops 135266304 | bytes 2654208 | tf_op jit(solution)/shard_map/dot_general | solution.py:26
  52.0 0.0 copy-start.7
  52.0 0.8 %copy.88 = bf16[8,128,32,32]{1,3,2,0:T(8,128)(2,1)S(1)} copy(bf16[8,128,32,32]{1,2,3,0:T(8,128)(2,1)S(1)} %convert_bitcast_fusion) | data formatting | bytes 4194304 | tf_op jit(solution)/shard_map/convert_element_type | solution.py:30
  52.9 1.5 %fusion.1 = bf16[8,128,128]{2,1,0:T(8,128)(2,1)} fusion(bf16[8,128,1024]{1,2,0:T(8,128)(2,1)S(1)} %bitcast.56, bf16[1024,128]{1,0:T(8,128)(2,1)S(1)} %copy-done, f32[128]{0:T(128)S(1)} %copy-done.7, f32[8,128]{1,0:T(8,128)S(1)} %multiply_maximum_fusion), kind=kOutput, calls=%fused_computation.3 | convolution fusion | flops 268828672 | bytes 2626048 | tf_op jit(solution)/shard_map/dot_general | solution.py:31
  (18 shorter events, 0.1 us)
Async XLA Ops:
  0.0 52.9 %copy-start = (bf16[1024,128]{1,0:T(8,128)(2,1)S(1)}, bf16[1024,128]{1,0:T(8,128)(2,1)}, u32[]{:S(2)}) copy-start(bf16[1024,128]{1,0:T(8,128)(2,1)} %param.20) | copy-start | bytes 786436
  0.0 27.9 %copy-start.4 = (f32[256]{0:T(256)S(1)}, f32[256]{0:T(256)}, u32[]{:S(2)}) copy-start(f32[256]{0:T(256)} %param.14) | copy-start | bytes 3076
  0.0 27.9 %copy-start.3 = (f32[256]{0:T(256)S(1)}, f32[256]{0:T(256)}, u32[]{:S(2)}) copy-start(f32[256]{0:T(256)} %param.15) | copy-start | bytes 3076
  1.9 25.0 %all-to-all-start = ((bf16[4,128,256]{2,0,1:T(4,128)(2,1)}), bf16[4,128,256]{2,0,1:T(4,128)(2,1)S(1)}, u32[]{:S(2)}, u32[]{:S(2)}) async-start(bf16[4,128,256]{2,0,1:T(4,128)(2,1)} %copy.75), calls=%async_computation | async-start | bytes 524288 | tf_op jit(solution)/shard_map/all_to_all | solution.py:89
  9.3 18.8 %copy-start.1 = (bf16[256,32]{0,1:T(8,128)(2,1)S(1)}, bf16[256,32]{0,1:T(8,128)(2,1)}, u32[]{:S(2)}) copy-start(bf16[256,32]{0,1:T(8,128)(2,1)} %param.18) | copy-start | bytes 49156
  9.3 18.8 %copy-start.5 = (f32[32]{0:T(128)S(1)}, f32[32]{0:T(128)}, u32[]{:S(2)}) copy-start(f32[32]{0:T(128)} %param.19) | copy-start | bytes 388
  27.9 22.9 %copy-start.2 = (bf16[256,32]{0,1:T(8,128)(2,1)S(1)}, bf16[256,32]{0,1:T(8,128)(2,1)}, u32[]{:S(2)}) copy-start(bf16[256,32]{0,1:T(8,128)(2,1)} %param.16) | copy-start | bytes 49156
  27.9 22.9 %copy-start.6 = (f32[32]{0:T(128)S(1)}, f32[32]{0:T(128)}, u32[]{:S(2)}) copy-start(f32[32]{0:T(128)} %param.17) | copy-start | bytes 388
  52.0 0.8 %copy-start.7 = (f32[128]{0:T(128)S(1)}, f32[128]{0:T(128)}, u32[]{:S(2)}) copy-start(f32[128]{0:T(128)} %param.21) | copy-start | bytes 1540
where the time goes:
time: 54.7 us; the launch traced here: 54.4 us
  blocking collectives  33.5 us (61%)
  starting transfers between devices  7.42 us (14%)
  local copies, waits for them, and re-layouts  6.75 us (12%)
  other arithmetic  2.94 us (5%)
  matrix products  2.91 us (5%)
  between operations  0.9 us (2%)
    all_gather x1, blocking collectives, per_device(): lax.all_gather(right_flat, 'row', axis=1, tiled=True)  21 us
    unnamed x1, blocking collectives  12.4 us
    all_to_all x1, starting transfers between devices, per_device(): lax.all_to_all(alignment, 'row', split_axis=1, concat_axis=0, tiled=True)  7.42 us
    unnamed x20, local copies, waits for them, and re-layouts  4.12 us
    dot_general x1, matrix products, pair_tile(): jnp.dot(outer_sum, out_weight, preferred_element_type=jnp.float32)  1.49 us
    dot_general x1, local copies, waits for them, and re-layouts, pair_tile(): lax.dot_general(left_flat, column_piece, (((0,), (0,)), ((), ())), prefer...  1.11 us
  transfers between devices with their start and end apart: 1, of which 0 were waited for; matrix products, arithmetic and copies ran while one was open for 8% of the time, Pallas kernels for 0%

commit v1 on v0

v1 whole, which is shorter than its diff:
```python
import functools

import jax
import jax.numpy as jnp
from jax import lax
from jax.experimental import pallas as pl
from jax.experimental.pallas import tpu as pltpu
from jax.sharding import PartitionSpec as P

F32 = jnp.float32
BF16 = jnp.bfloat16
FLAG_ROWS = 8


def _iota(shape, dim):
    return lax.broadcasted_iota(jnp.int32, shape, dim)


def _dot_t(lhs, rhs, **kw):
    return lax.dot_general(
        lhs, rhs, (((1,), (1,)), ((), ())), preferred_element_type=F32, **kw
    )


def _column(row):
    length = row.shape[1]
    square = (length, length)
    picked = jnp.where(
        _iota(square, 0) == _iota(square, 1), jnp.broadcast_to(row, square), 0.0
    )
    return jnp.sum(picked, axis=1, keepdims=True)


def _vmem(n):
    return [pl.BlockSpec(memory_space=pltpu.VMEM)] * n


def _project_kernel(
    x_ref, flags_ref, crop_ref, gain_ref, shift_ref, wl_ref, wr_ref, lb_ref, rb_ref, out_ref
):
    seqs, residues, _ = x_ref.shape
    channels = wl_ref.shape[0]
    pair = 2 * seqs
    lanes = pair * channels
    first = (lax.axis_index("row") % 2) * seqs
    spread = _iota((lanes, channels), 0)
    which = _iota((lanes, channels), 1)
    pick_r = jnp.where(spread // pair == which, 1.0, 0.0)
    pick_l = jnp.where(spread % channels == which, 1.0, 0.0)
    exact = dict(precision=lax.Precision.HIGHEST)
    wr_rep = jnp.dot(pick_r.astype(BF16), wr_ref[...], preferred_element_type=F32).astype(BF16)
    wl_rep = jnp.concatenate([wl_ref[...]] * pair, axis=0)
    rb_rep = _dot_t(jnp.broadcast_to(rb_ref[...], (8, channels)), pick_r, **exact)[0:1]
    lb_rep = _dot_t(jnp.broadcast_to(lb_ref[...], (8, channels)), pick_l, **exact)[0:1]
    crop = _column(crop_ref[...].astype(F32))
    lane = _iota((1, lanes), 1)
    seq_r = lane % pair - first
    seq_l = lane // channels - first
    right = jnp.zeros((residues, lanes), F32)
    left = jnp.zeros((residues, lanes), F32)
    flag_r = jnp.zeros((1, lanes), F32)
    flag_l = jnp.zeros((1, lanes), F32)
    flag_row = jnp.zeros((1, lanes), F32)
    for s in range(seqs):
        values = x_ref[s].astype(F32)
        values = values - jnp.mean(values, axis=-1, keepdims=True)
        variance = jnp.mean(values * values, axis=-1, keepdims=True)
        normed = values * lax.rsqrt(variance + 1e-05) * gain_ref[...] + shift_ref[...]
        high = normed.astype(BF16)
        low = (normed - high.astype(F32)).astype(BF16)
        flag = flags_ref[s].astype(F32)
        right = jnp.where(seq_r == s, _dot_t(high, wr_rep) + _dot_t(low, wr_rep), right)
        left = jnp.where(seq_l == s, _dot_t(high, wl_rep) + _dot_t(low, wl_rep), left)
        flag_r = jnp.where(seq_r == s, flag, flag_r)
        flag_l = jnp.where(seq_l == s, flag, flag_l)
        flag_row = jnp.where(lane - first == s, flag, flag_row)
    out_ref[0:residues] = ((right + rb_rep) * (flag_r * crop)).astype(BF16)
    out_ref[residues : 2 * residues] = ((left + lb_rep) * (flag_l * crop)).astype(BF16)
    rows = _iota((2 * FLAG_ROWS, lanes), 0)
    out_ref[2 * residues :] = jnp.where(rows == 0, flag_row, 0.0).astype(BF16)


def _pack_kernel(steps, rows_chip, own_ref, other_ref, *out_refs):
    residues = own_ref.shape[0] // 2 - FLAG_ROWS
    total = rows_chip + FLAG_ROWS
    index = lax.axis_index("row")
    chip, core = index // 2, index % 2
    right = own_ref[0:residues] + other_ref[0:residues]
    flags = own_ref[2 * residues :] + other_ref[2 * residues :]
    for out_ref, (far, near) in zip(out_refs, ((0, 0),) + steps):
        target = chip ^ jnp.where(core == 1, far, near)
        start = pl.multiple_of(residues + target * rows_chip, rows_chip)
        out_ref[0:residues] = right
        slab = own_ref[pl.ds(start, rows_chip)] + other_ref[pl.ds(start, rows_chip)]
        tail = jnp.concatenate([slab.astype(F32), flags.astype(F32)], axis=0)
        out_ref[residues : residues + total] = tail[0:total].astype(BF16)


def _weight_kernel(channels, w_ref, out_ref, wide_ref):
    width = w_ref.shape[1]
    wide_ref[...] = w_ref[...].astype(F32)
    for e in range(channels):
        block = wide_ref[pl.ds(e, channels, stride=channels), :]
        out_ref[:, e * width : (e + 1) * width] = block.astype(BF16)


def _partial(parcels, w_ref, a_ref):
    channels = w_ref.shape[0]
    lanes = parcels[0].shape[1]
    pair = lanes // channels
    width = w_ref.shape[1] // channels
    residues = parcels[0].shape[0] - 2 * pair - FLAG_ROWS
    core = lax.axis_index("row") % 2
    mine = _iota((pair, lanes), 1) // channels == _iota((pair, lanes), 0)
    rows = []
    for ref in parcels:
        slab = ref[residues : residues + 2 * pair].astype(F32)
        slab = jnp.where(core == 1, slab[pair:], slab[:pair])
        for i in range(pair):
            rows.append(jnp.where(mine, jnp.broadcast_to(slab[i : i + 1], (pair, lanes)), 0.0))
    spread = jnp.concatenate(rows, axis=0).astype(BF16)
    for e in range(0, channels, 2):
        block = w_ref[:, e * width : (e + 2) * width]
        product = jnp.dot(
            spread, jnp.concatenate([block] * pair, axis=0), preferred_element_type=F32
        )
        for n in range(len(parcels)):
            for i in range(pair):
                at = (n * pair + i) * pair
                both = jnp.concatenate(
                    [product[at : at + pair, :width], product[at : at + pair, width:]], axis=0
                )
                a_ref[
                    n * lanes + e * pair : n * lanes + (e + 2) * pair,
                    i * width : (i + 1) * width,
                ] = both.astype(BF16)
    total = None
    for n, ref in enumerate(parcels):
        part = jnp.dot(
            ref[0:residues], a_ref[n * lanes : (n + 1) * lanes], preferred_element_type=F32
        )
        total = part if total is None else total + part
    return total


def _live(parcels):
    total = None
    for ref in parcels:
        rows = ref.shape[0]
        part = ref[rows - 2 * FLAG_ROWS :].astype(F32)[FLAG_ROWS:]
        total = part if total is None else total + part
    return total


def _first_kernel(count, w_ref, *refs):
    parcels, (sum_ref, live_ref, a_ref) = refs[:count], refs[count:]
    sum_ref[...] = _partial(parcels, w_ref, a_ref)
    live_ref[...] = _live(parcels)


def _last_kernel(count, w_ref, sum_in, live_in, crop_ref, bias_ref, *refs):
    parcels, (out_ref, a_ref) = refs[:count], refs[count:]
    rows_here, _, width = out_ref.shape
    projected = sum_in[...] + _partial(parcels, w_ref, a_ref)
    live = jnp.sum(live_in[...] + _live(parcels))
    crop = crop_ref[...].astype(F32)
    column = _column(crop)
    first = lax.axis_index("row") * rows_here
    lane = _iota(crop.shape, 1)
    for i in range(rows_here):
        crop_i = jnp.sum(jnp.where(lane == first + i, crop, 0.0))
        divisor = jnp.maximum(live * crop_i * column, 1.0)
        tile = projected[:, i * width : (i + 1) * width] / divisor + bias_ref[...]
        out_ref[i] = tile.astype(BF16)


def per_device(
    alignment,
    seq_flags,
    crop_flags,
    norm_gain,
    norm_bias,
    left_weight,
    left_bias,
    right_weight,
    right_bias,
    out_weight,
    out_bias,
):
    seqs, residues, _ = alignment.shape
    channels = left_weight.shape[1]
    width = out_weight.shape[1]
    devices = lax.axis_size("row")
    rows_here = residues // devices
    rows_chip = 2 * rows_here
    chips = devices // 2
    lanes = 2 * seqs * channels
    steps = tuple((k, (k + 1) % chips) for k in range(1, chips, 2))
    cores = [(d, d ^ 1) for d in range(devices)]
    crop = crop_flags.reshape(1, residues)
    limit = pltpu.CompilerParams(vmem_limit_bytes=48 * 1024 * 1024)

    projected = pl.pallas_call(
        _project_kernel,
        out_shape=jax.ShapeDtypeStruct((2 * residues + 2 * FLAG_ROWS, lanes), BF16),
        in_specs=_vmem(1) + [pl.BlockSpec(memory_space=pltpu.SMEM)] + _vmem(7),
        out_specs=_vmem(1)[0],
        compiler_params=limit,
        name="project",
    )(
        alignment,
        seq_flags,
        crop,
        norm_gain.reshape(1, -1),
        norm_bias.reshape(1, -1),
        left_weight.T,
        right_weight.T,
        left_bias.reshape(1, -1),
        right_bias.reshape(1, -1),
    )
    other = lax.ppermute(projected, "row", cores)
    parcel = jax.ShapeDtypeStruct((residues + rows_chip + FLAG_ROWS, lanes), BF16)
    own, *parcels = pl.pallas_call(
        functools.partial(_pack_kernel, steps, rows_chip),
        out_shape=[parcel] * (1 + len(steps)),
        in_specs=_vmem(2),
        out_specs=_vmem(1 + len(steps)),
        compiler_params=limit,
        name="pack",
    )(projected, other)
    received = []
    for (far, near), piece in zip(steps, parcels):
        pairs = [(2 * q + 1, 2 * (q ^ far) + 1) for q in range(chips)]
        if near:
            pairs += [(2 * q, 2 * (q ^ near)) for q in range(chips)]
        received.append(lax.ppermute(piece, "row", pairs))
    handed = [lax.ppermute(piece, "row", cores) for piece in received]

    weight = pl.pallas_call(
        functools.partial(_weight_kernel, channels),
        out_shape=jax.ShapeDtypeStruct((channels, channels * width), BF16),
        in_specs=_vmem(1),
        out_specs=_vmem(1)[0],
        scratch_shapes=[pltpu.VMEM(out_weight.shape, F32)],
        compiler_params=limit,
        name="weight",
    )(out_weight)
    here = [own] + received
    partial_sum, live = pl.pallas_call(
        functools.partial(_first_kernel, len(here)),
        out_shape=[
            jax.ShapeDtypeStruct((residues, rows_here * width), F32),
            jax.ShapeDtypeStruct((FLAG_ROWS, lanes), F32),
        ],
        in_specs=_vmem(1 + len(here)),
        out_specs=_vmem(2),
        scratch_shapes=[pltpu.VMEM((len(here) * lanes, rows_here * width), BF16)],
        compiler_params=limit,
        name="first",
    )(weight, *here)
    return pl.pallas_call(
        functools.partial(_last_kernel, len(handed)),
        out_shape=jax.ShapeDtypeStruct((rows_here, residues, width), BF16),
        in_specs=_vmem(5 + len(handed)),
        out_specs=_vmem(1)[0],
        scratch_shapes=[pltpu.VMEM((len(handed) * lanes, rows_here * width), BF16)],
        compiler_params=limit,
        name="last",
    )(weight, partial_sum, live, crop, out_bias.reshape(1, -1), *handed)


def solution(mesh):
    return jax.shard_map(
        per_device,
        mesh=mesh,
        in_specs=(
            P(("grp", "row"), None, None),
            P(("grp", "row")),
            P("grp"),
            P(),
            P(),
            P(),
            P(),
            P(),
            P(),
            P(),
            P(),
        ),
        out_specs=P(("grp", "row"), None, None),
        check_vma=False,
    )
```

time: 54.7 us -> 26 us (0.48)
  blocking collectives: 33.5 us -> 0 us
  starting transfers between devices: 7.42 us -> 13.2 us
  Pallas kernels: 0 us -> 5.12 us
  waiting for transfers between devices: 0.01 us -> 3.5 us
  local copies, waits for them, and re-layouts: 6.75 us -> 3.78 us
  other arithmetic: 2.94 us -> 0 us
  matrix products: 2.91 us -> 0 us
  between operations: 0.9 us -> 0.11 us
    all_gather x1 -> x0, blocking collectives: 21 us -> none  [per_device(): lax.all_gather(right_flat, 'row', axis=1, tiled=True)]
    ppermute x0 -> x9, starting transfers between devices: none -> 13.2 us  [the longest x4 6.38 us: per_device(): handed = [lax.ppermute(piece, 'row', cores) for piece in received]]
    unnamed x1 -> x0, blocking collectives: 12.4 us -> none
    all_to_all x1 -> x0, starting transfers between devices: 7.42 us -> none  [per_device(): lax.all_to_all(alignment, 'row', split_axis=1, concat_axis=0, tiled=True)]
    pallas_call x0 -> x5, Pallas kernels: none -> 5.12 us  [the longest x1 1.83 us: per_device(): pl.pallas_call(functools.partial(_last_kernel, len(handed)), out_shape=ja...]
    ppermute x0 -> x9, waiting for transfers between devices: none -> 3.5 us  [the longest x4 2.5 us: per_device(): received.append(lax.ppermute(piece, 'row', pairs))]
    dot_general x4 -> x0, matrix products: 2.91 us -> none  [the longest x1 1.49 us: pair_tile(): jnp.dot(outer_sum, out_weight, preferred_element_type=jnp.float32)]
    convert_element_type x4 -> x0, local copies, waits for them, and re-layouts: 1.14 us -> none  [the longest x1 0.82 us: pair_tile(): outer_sum.reshape(rows_here * width_cols, channels * channels)]
  transfers between devices with their start and end apart: 1 -> 9, of which waited for: 0 -> 2; matrix products, arithmetic and copies ran while one was open for 8% -> 0% of each run, Pallas kernels for 0% -> 6%
where the time goes in v1:
time: 26 us; the launch traced here: 25.7 us
  starting transfers between devices  13.2 us (51%)
  Pallas kernels  5.12 us (20%)
  local copies, waits for them, and re-layouts  3.78 us (15%)
  waiting for transfers between devices  3.5 us (13%)
    ppermute x4, starting transfers between devices, per_device(): handed = [lax.ppermute(piece, 'row', cores) for piece in received]  6.38 us
    ppermute x4, starting transfers between devices, per_device(): received.append(lax.ppermute(piece, 'row', pairs))  6.23 us
    unnamed x22, local copies, waits for them, and re-layouts  3.78 us
    ppermute x4, waiting for transfers between devices, per_device(): received.append(lax.ppermute(piece, 'row', pairs))  2.5 us
    pallas_call x1, Pallas kernels, per_device(): pl.pallas_call(functools.partial(_last_kernel, len(handed)), out_shape=ja...  1.83 us
    pallas_call x1, Pallas kernels, per_device(): pl.pallas_call(_project_kernel, out_shape=jax.ShapeDtypeStruct((2 * resid...  1.63 us
    pallas_call x1, Pallas kernels, per_device(): pl.pallas_call(functools.partial(_first_kernel, len(here)), out_shape=[ja...  1.28 us
    ppermute x1, waiting for transfers between devices, per_device(): other = lax.ppermute(projected, 'row', cores)  1 us
  transfers between devices with their start and end apart: 9, of which 2 were waited for; matrix products, arithmetic and copies ran while one was open for 0% of the time, Pallas kernels for 6%

profile of v1, /device:TPU:0, one launch (start us, length us, event | category | flops | bytes accessed | tf_op | source)
XLA Modules:
  0.0 25.7 jit_solution(9647383548827136097)
XLA Ops:
  0.0 0.6 %copy-done.9 = f32[32]{0:T(128)S(1)} copy-done((f32[32]{0:T(128)S(1)}, f32[32]{0:T(128)}, u32[]{:S(2)}) %copy-start.9) | copy-done | bytes 152
  0.7 0.0 copy-done.6
  0.7 0.0 copy-done.8
  0.7 0.0 copy-done.4
  0.7 0.0 copy-done.5
  0.8 0.9 %copy-done = bf16[4,128,256]{2,1,0:T(8,128)(2,1)S(1)} copy-done((bf16[4,128,256]{2,1,0:T(8,128)(2,1)S(1)}, bf16[4,128,256]{2,1,0:T(8,128)(2,1)}, u32[]{:S(2)}) %copy-start) | copy-done | bytes 262168
  1.7 0.7 %copy-done.2 = bf16[256,32]{0,1:T(8,128)(2,1)S(1)} copy-done((bf16[256,32]{0,1:T(8,128)(2,1)S(1)}, bf16[256,32]{0,1:T(8,128)(2,1)}, u32[]{:S(2)}) %copy-start.2) | copy-done | bytes 16408
  2.4 0.7 %copy-done.3 = bf16[256,32]{0,1:T(8,128)(2,1)S(1)} copy-done((bf16[256,32]{0,1:T(8,128)(2,1)S(1)}, bf16[256,32]{0,1:T(8,128)(2,1)}, u32[]{:S(2)}) %copy-start.3) | copy-done | bytes 16408
  3.1 1.6 %project.1.own_ref = bf16[272,256]{1,0:T(8,128)(2,1)S(1)} custom-call(bf16[4,128,256]{2,1,0:T(8,128)(2,1)S(1)} %copy-done, s32[4]{0:T(128)S(1)} %copy-done.7, s32[1,128]{1,0:T(1,128)S(1)} %bitcast.10, f32[1,256]{1,0:T(1,128)S(1)} %bitcast.12, f32[1,256]{1,0:T(1,128)S(1)} %bitcast.13, bf16[32,256]{1,0:T(8,128)(2,1)S(1)} %bitcast.8, ...), custom_call_target="tpu_custom_call" | custom-call | tf_op jit(solution)/shard_map/project/pallas_call | solution.py:203
  4.8 0.6 %collective-permute-start = (bf16[272,256]{1,0:T(8,128)(2,1)S(1)}, bf16[272,256]{1,0:T(8,128)(2,1)S(1)}, u32[]{:S(2)}, u32[]{:S(2)}) collective-permute-start(bf16[272,256]{1,0:T(8,128)(2,1)S(1)} %project.1.own_ref), channel_id=1, source_target_pairs={{0,1},{1,0},{2,3},{3,2},{4,5},{5,4},{6,7},{7,6},{8,9},{9,8},{10,11... | collective-permute-start | bytes 417800 | tf_op jit(solution)/shard_map/ppermute | solution.py:221
  5.3 1.0 %collective-permute-done.other_ref = bf16[272,256]{1,0:T(8,128)(2,1)S(1)} collective-permute-done((bf16[272,256]{1,0:T(8,128)(2,1)S(1)}, bf16[272,256]{1,0:T(8,128)(2,1)S(1)}, u32[]{:S(2)}, u32[]{:S(2)}) %collective-permute-start) | collective-permute-done | bytes 139296 | tf_op jit(solution)/shard_map/ppermute | solution.py:221
  6.4 3.0 %collective-permute-start.1 = (bf16[152,256]{1,0:T(8,128)(2,1)S(1)}, bf16[152,256]{1,0:T(8,128)(2,1)S(1)}, u32[]{:S(2)}, u32[]{:S(2)}) collective-permute-start(bf16[152,256]{1,0:T(8,128)(2,1)S(1)} %get-tuple-element.13), channel_id=1, source_target_pairs={{1,3},{3,1},{5,7},{7,5},{9,11},{11,9},{13,15},{15,13},{0,4},{2,6},... | collective-permute-start | bytes 233480 | tf_op jit(solution)/shard_map/ppermute | solution.py:236
  9.4 2.6 %collective-permute-start.2 = (bf16[152,256]{1,0:T(8,128)(2,1)S(1)}, bf16[152,256]{1,0:T(8,128)(2,1)S(1)}, u32[]{:S(2)}, u32[]{:S(2)}) collective-permute-start(bf16[152,256]{1,0:T(8,128)(2,1)S(1)} %get-tuple-element.14), channel_id=1, source_target_pairs={{1,7},{3,5},{5,3},{7,1},{9,15},{11,13},{13,11},{15,9},{0,8},{2,10}... | collective-permute-start | bytes 233480 | tf_op jit(solution)/shard_map/ppermute | solution.py:236
  11.9 0.0 collective-permute-start.3
  12.0 0.7 %collective-permute-start.4 = (bf16[152,256]{1,0:T(8,128)(2,1)S(1)}, bf16[152,256]{1,0:T(8,128)(2,1)S(1)}, u32[]{:S(2)}, u32[]{:S(2)}) collective-permute-start(bf16[152,256]{1,0:T(8,128)(2,1)S(1)} %get-tuple-element.16), channel_id=1, source_target_pairs={{1,15},{3,13},{5,11},{7,9},{9,7},{11,5},{13,3},{15,1},{17,31},{19,... | collective-permute-start | bytes 233480 | tf_op jit(solution)/shard_map/ppermute | solution.py:236
  12.6 0.0 collective-permute-done.1.refs_1_
  12.6 3.0 %collective-permute-start.5 = (bf16[152,256]{1,0:T(8,128)(2,1)S(1)}, bf16[152,256]{1,0:T(8,128)(2,1)S(1)}, u32[]{:S(2)}, u32[]{:S(2)}) collective-permute-start(bf16[152,256]{1,0:T(8,128)(2,1)S(1)} %collective-permute-done.1.refs_1_), channel_id=1, source_target_pairs={{0,1},{1,0},{2,3},{3,2},{4,5},{5,4},{6,7},{7,6},{8,9},{9,8},{10,11... | collective-permute-start | bytes 233480 | tf_op jit(solution)/shard_map/ppermute | solution.py:237
  15.7 0.0 collective-permute-done.2.refs_2_
  15.7 0.1 collective-permute-start.6
  15.8 2.5 %collective-permute-done.3.refs_3_ = bf16[152,256]{1,0:T(8,128)(2,1)S(1)} collective-permute-done((bf16[152,256]{1,0:T(8,128)(2,1)S(1)}, bf16[152,256]{1,0:T(8,128)(2,1)S(1)}, u32[]{:S(2)}, u32[]{:S(2)}) %collective-permute-start.3) | collective-permute-done | bytes 77856 | tf_op jit(solution)/shard_map/ppermute | solution.py:236
  18.2 0.0 collective-permute-start.7
  18.3 0.0 collective-permute-done.4.refs_4_
  18.3 3.2 %collective-permute-start.8 = (bf16[152,256]{1,0:T(8,128)(2,1)S(1)}, bf16[152,256]{1,0:T(8,128)(2,1)S(1)}, u32[]{:S(2)}, u32[]{:S(2)}) collective-permute-start(bf16[152,256]{1,0:T(8,128)(2,1)S(1)} %collective-permute-done.4.refs_4_), channel_id=1, source_target_pairs={{0,1},{1,0},{2,3},{3,2},{4,5},{5,4},{6,7},{7,6},{8,9},{9,8},{10,11... | collective-permute-start | bytes 233480 | tf_op jit(solution)/shard_map/ppermute | solution.py:237
  21.5 0.3 %weight.1.w_ref = bf16[32,4096]{1,0:T(8,128)(2,1)S(1)} custom-call(bf16[1024,128]{1,0:T(8,128)(2,1)S(1)} %copy-done.1), custom_call_target="tpu_custom_call" | custom-call | tf_op jit(solution)/shard_map/weight/pallas_call | solution.py:239
  21.9 1.3 %first.1 = (f32[128,1024]{1,0:T(8,128)S(1)}, f32[8,256]{1,0:T(8,128)S(1)}) custom-call(bf16[32,4096]{1,0:T(8,128)(2,1)S(1)} %weight.1.w_ref, bf16[152,256]{1,0:T(8,128)(2,1)S(1)} %get-tuple-element.12.refs_0_, bf16[152,256]{1,0:T(8,128)(2,1)S(1)} %collective-permute-done.1.refs_1_, bf16[152,256]{1,0:T(8,128)(2,1)S(1)} %collective-permute-done.2.refs_2_, ...), custom_call_target="tpu_custom_call" | custom-call | tf_op jit(solution)/shard_map/first/pallas_call | solution.py:249
  23.1 0.0 collective-permute-done.5.refs_0_
  23.2 0.0 collective-permute-done.6.refs_1_
  23.2 0.0 collective-permute-done.7.refs_2_
  23.2 0.0 collective-permute-done.8.refs_3_
  23.2 0.0 copy-start.10
  23.2 0.6 %copy-done.10 = f32[128]{0:T(128)S(1)} copy-done((f32[128]{0:T(128)S(1)}, f32[128]{0:T(128)}, u32[]{:S(2)}) %copy-start.10) | copy-done | bytes 536
  23.8 1.8 %last.1 = bf16[8,128,128]{2,1,0:T(8,128)(2,1)} custom-call(bf16[32,4096]{1,0:T(8,128)(2,1)S(1)} %weight.1.w_ref, f32[128,1024]{1,0:T(8,128)S(1)} %get-tuple-element.17.sum_in, f32[8,256]{1,0:T(8,128)S(1)} %get-tuple-element.18.live_in, s32[1,128]{1,0:T(1,128)S(1)} %bitcast.11, f32[1,128]{1,0:T(1,128)S(1)} %bitcast.16, ...), custom_call_target="tpu_custom_call" | custom-call | tf_op jit(solution)/shard_map/last/pallas_call | solution.py:261
  (13 shorter events, 0.1 us)
Async XLA Ops:
  0.0 0.7 %copy-start.9 = (f32[32]{0:T(128)S(1)}, f32[32]{0:T(128)}, u32[]{:S(2)}) copy-start(f32[32]{0:T(128)} %param.19) | copy-start | bytes 388
  0.0 0.7 %copy-start.6 = (f32[256]{0:T(256)S(1)}, f32[256]{0:T(256)}, u32[]{:S(2)}) copy-start(f32[256]{0:T(256)} %param.15) | copy-start | bytes 3076
  0.0 0.7 %copy-start.7 = (s32[4]{0:T(128)S(1)}, s32[4]{0:T(128)}, u32[]{:S(2)}) copy-start(s32[4]{0:T(128)} %flags_ref.1) | copy-start | bytes 52
  0.0 0.7 %copy-start.8 = (f32[32]{0:T(128)S(1)}, f32[32]{0:T(128)}, u32[]{:S(2)}) copy-start(f32[32]{0:T(128)} %param.17) | copy-start | bytes 388
  0.0 0.7 %copy-start.4 = (s32[128]{0:T(128)S(1)}, s32[128]{0:T(128)}, u32[]{:S(2)}) copy-start(s32[128]{0:T(128)} %param.13) | copy-start | bytes 1540
  0.0 0.7 %copy-start.5 = (f32[256]{0:T(256)S(1)}, f32[256]{0:T(256)}, u32[]{:S(2)}) copy-start(f32[256]{0:T(256)} %param.14) | copy-start | bytes 3076
  0.8 0.9 %copy-start = (bf16[4,128,256]{2,1,0:T(8,128)(2,1)S(1)}, bf16[4,128,256]{2,1,0:T(8,128)(2,1)}, u32[]{:S(2)}) copy-start(bf16[4,128,256]{2,1,0:T(8,128)(2,1)} %x_ref.1) | copy-start | bytes 786436
  1.7 0.7 %copy-start.2 = (bf16[256,32]{0,1:T(8,128)(2,1)S(1)}, bf16[256,32]{0,1:T(8,128)(2,1)}, u32[]{:S(2)}) copy-start(bf16[256,32]{0,1:T(8,128)(2,1)} %param.16) | copy-start | bytes 49156
  2.4 0.7 %copy-start.3 = (bf16[256,32]{0,1:T(8,128)(2,1)S(1)}, bf16[256,32]{0,1:T(8,128)(2,1)}, u32[]{:S(2)}) copy-start(bf16[256,32]{0,1:T(8,128)(2,1)} %param.18) | copy-start | bytes 49156
  3.1 18.4 %copy-start.1 = (bf16[1024,128]{1,0:T(8,128)(2,1)S(1)}, bf16[1024,128]{1,0:T(8,128)(2,1)}, u32[]{:S(2)}) copy-start(bf16[1024,128]{1,0:T(8,128)(2,1)} %w_ref.1) | copy-start | bytes 786436
  4.8 1.6 %collective-permute-start = (bf16[272,256]{1,0:T(8,128)(2,1)S(1)}, bf16[272,256]{1,0:T(8,128)(2,1)S(1)}, u32[]{:S(2)}, u32[]{:S(2)}) collective-permute-start(bf16[272,256]{1,0:T(8,128)(2,1)S(1)} %project.1.own_ref), channel_id=1, source_target_pairs={{0,1},{1,0},{2,3},{3,2},{4,5},{5,4},{6,7},{7,6},{8,9},{9,8},{10,11... | collective-permute-start | bytes 417800 | tf_op jit(solution)/shard_map/ppermute | solution.py:221
  6.4 6.2 %collective-permute-start.1 = (bf16[152,256]{1,0:T(8,128)(2,1)S(1)}, bf16[152,256]{1,0:T(8,128)(2,1)S(1)}, u32[]{:S(2)}, u32[]{:S(2)}) collective-permute-start(bf16[152,256]{1,0:T(8,128)(2,1)S(1)} %get-tuple-element.13), channel_id=1, source_target_pairs={{1,3},{3,1},{5,7},{7,5},{9,11},{11,9},{13,15},{15,13},{0,4},{2,6},... | collective-permute-start | bytes 233480 | tf_op jit(solution)/shard_map/ppermute | solution.py:236
  9.4 6.3 %collective-permute-start.2 = (bf16[152,256]{1,0:T(8,128)(2,1)S(1)}, bf16[152,256]{1,0:T(8,128)(2,1)S(1)}, u32[]{:S(2)}, u32[]{:S(2)}) collective-permute-start(bf16[152,256]{1,0:T(8,128)(2,1)S(1)} %get-tuple-element.14), channel_id=1, source_target_pairs={{1,7},{3,5},{5,3},{7,1},{9,15},{11,13},{13,11},{15,9},{0,8},{2,10}... | collective-permute-start | bytes 233480 | tf_op jit(solution)/shard_map/ppermute | solution.py:236
  11.9 6.3 %collective-permute-start.3 = (bf16[152,256]{1,0:T(8,128)(2,1)S(1)}, bf16[152,256]{1,0:T(8,128)(2,1)S(1)}, u32[]{:S(2)}, u32[]{:S(2)}) collective-permute-start(bf16[152,256]{1,0:T(8,128)(2,1)S(1)} %get-tuple-element.15), channel_id=1, source_target_pairs={{1,11},{3,9},{5,15},{7,13},{9,3},{11,1},{13,7},{15,5},{0,12},{2,14... | collective-permute-start | bytes 233480 | tf_op jit(solution)/shard_map/ppermute | solution.py:236
  12.0 6.3 %collective-permute-start.4 = (bf16[152,256]{1,0:T(8,128)(2,1)S(1)}, bf16[152,256]{1,0:T(8,128)(2,1)S(1)}, u32[]{:S(2)}, u32[]{:S(2)}) collective-permute-start(bf16[152,256]{1,0:T(8,128)(2,1)S(1)} %get-tuple-element.16), channel_id=1, source_target_pairs={{1,15},{3,13},{5,11},{7,9},{9,7},{11,5},{13,3},{15,1},{17,31},{19,... | collective-permute-start | bytes 233480 | tf_op jit(solution)/shard_map/ppermute | solution.py:236
  12.6 10.5 %collective-permute-start.5 = (bf16[152,256]{1,0:T(8,128)(2,1)S(1)}, bf16[152,256]{1,0:T(8,128)(2,1)S(1)}, u32[]{:S(2)}, u32[]{:S(2)}) collective-permute-start(bf16[152,256]{1,0:T(8,128)(2,1)S(1)} %collective-permute-done.1.refs_1_), channel_id=1, source_target_pairs={{0,1},{1,0},{2,3},{3,2},{4,5},{5,4},{6,7},{7,6},{8,9},{9,8},{10,11... | collective-permute-start | bytes 233480 | tf_op jit(solution)/shard_map/ppermute | solution.py:237
  15.7 7.5 %collective-permute-start.6 = (bf16[152,256]{1,0:T(8,128)(2,1)S(1)}, bf16[152,256]{1,0:T(8,128)(2,1)S(1)}, u32[]{:S(2)}, u32[]{:S(2)}) collective-permute-start(bf16[152,256]{1,0:T(8,128)(2,1)S(1)} %collective-permute-done.2.refs_2_), channel_id=1, source_target_pairs={{0,1},{1,0},{2,3},{3,2},{4,5},{5,4},{6,7},{7,6},{8,9},{9,8},{10,11... | collective-permute-start | bytes 233480 | tf_op jit(solution)/shard_map/ppermute | solution.py:237
  18.2 4.9 %collective-permute-start.7 = (bf16[152,256]{1,0:T(8,128)(2,1)S(1)}, bf16[152,256]{1,0:T(8,128)(2,1)S(1)}, u32[]{:S(2)}, u32[]{:S(2)}) collective-permute-start(bf16[152,256]{1,0:T(8,128)(2,1)S(1)} %collective-permute-done.3.refs_3_), channel_id=1, source_target_pairs={{0,1},{1,0},{2,3},{3,2},{4,5},{5,4},{6,7},{7,6},{8,9},{9,8},{10,11... | collective-permute-start | bytes 233480 | tf_op jit(solution)/shard_map/ppermute | solution.py:237
  18.3 4.9 %collective-permute-start.8 = (bf16[152,256]{1,0:T(8,128)(2,1)S(1)}, bf16[152,256]{1,0:T(8,128)(2,1)S(1)}, u32[]{:S(2)}, u32[]{:S(2)}) collective-permute-start(bf16[152,256]{1,0:T(8,128)(2,1)S(1)} %collective-permute-done.4.refs_4_), channel_id=1, source_target_pairs={{0,1},{1,0},{2,3},{3,2},{4,5},{5,4},{6,7},{7,6},{8,9},{9,8},{10,11... | collective-permute-start | bytes 233480 | tf_op jit(solution)/shard_map/ppermute | solution.py:237
  23.2 0.7 %copy-start.10 = (f32[128]{0:T(128)S(1)}, f32[128]{0:T(128)}, u32[]{:S(2)}) copy-start(f32[128]{0:T(128)} %param.21) | copy-start | bytes 1540

commit v2 on v1

v2 whole, which is shorter than its diff:
```python
import functools

import jax
import jax.numpy as jnp
from jax import lax
from jax.experimental import pallas as pl
from jax.experimental.pallas import tpu as pltpu
from jax.sharding import PartitionSpec as P


F32 = jnp.float32
BF16 = jnp.bfloat16
FLAG_ROWS = 8


def _iota(shape, dim):
    return lax.broadcasted_iota(jnp.int32, shape, dim)


def _column(row):
    length = row.shape[1]
    square = (length, length)
    picked = jnp.where(
        _iota(square, 0) == _iota(square, 1), jnp.broadcast_to(row, square), 0.0
    )
    return jnp.sum(picked, axis=1, keepdims=True)


def _stay(array):
    return pltpu.with_memory_space_constraint(array, pltpu.HBM)


def _vmem(n):
    return [pl.BlockSpec(memory_space=pltpu.VMEM)] * n


def _project_kernel(
    x_hbm,
    flags_hbm,
    crop_hbm,
    gain_hbm,
    shift_hbm,
    wl_hbm,
    wr_hbm,
    lb_hbm,
    rb_hbm,
    out_ref,
    x_ref,
    flags_ref,
    crop_ref,
    gain_ref,
    shift_ref,
    wl_ref,
    wr_ref,
    lb_ref,
    rb_ref,
    x_sems,
    sems,
):
    seqs, residues, _ = x_ref.shape
    channels = wl_ref.shape[0]
    small = [
        pltpu.make_async_copy(src, dst, sems.at[n])
        for n, (src, dst) in enumerate(
            [
                (wr_hbm, wr_ref),
                (wl_hbm, wl_ref),
                (gain_hbm, gain_ref),
                (shift_hbm, shift_ref),
                (crop_hbm, crop_ref),
                (flags_hbm, flags_ref),
                (lb_hbm, lb_ref),
                (rb_hbm, rb_ref),
            ]
        )
    ]
    loads = [
        pltpu.make_async_copy(x_hbm.at[s], x_ref.at[s], x_sems.at[s]) for s in range(seqs)
    ]
    for copy in loads + small:
        copy.start()
    pair = 2 * seqs
    lanes = pair * channels
    first = (lax.axis_index("row") % 2) * seqs
    which = _iota((channels, lanes), 0)
    spread = _iota((channels, lanes), 1)
    pick_r = jnp.where(spread // pair == which, 1.0, 0.0)
    pick_l = jnp.where(spread % channels == which, 1.0, 0.0)
    exact = dict(precision=lax.Precision.HIGHEST, preferred_element_type=F32)
    lane = _iota((1, lanes), 1)
    seq_r = lane % pair - first
    seq_l = lane // channels - first
    for copy in small:
        copy.wait()
    turned = (((0,), (0,)), ((), ()))
    wr_rep = lax.dot_general(
        wr_ref[...], pick_r.astype(BF16), turned, preferred_element_type=F32
    ).astype(BF16)
    wl_rep = lax.dot_general(
        wl_ref[...], pick_l.astype(BF16), turned, preferred_element_type=F32
    ).astype(BF16)
    rb_rep = jnp.dot(jnp.broadcast_to(rb_ref[...], (8, channels)), pick_r, **exact)[0:1]
    lb_rep = jnp.dot(jnp.broadcast_to(lb_ref[...], (8, channels)), pick_l, **exact)[0:1]
    crop = _column(crop_ref[...].astype(F32))
    right = jnp.zeros((residues, lanes), F32)
    left = jnp.zeros((residues, lanes), F32)
    flag_r = jnp.zeros((1, lanes), F32)
    flag_l = jnp.zeros((1, lanes), F32)
    flag_row = jnp.zeros((1, lanes), F32)
    flags = flags_ref[...].astype(F32)
    for s in range(seqs):
        flag = jnp.broadcast_to(flags[:, s : s + 1], (1, lanes))
        flag_r = jnp.where(seq_r == s, flag, flag_r)
        flag_l = jnp.where(seq_l == s, flag, flag_l)
        flag_row = jnp.where(lane - first == s, flag, flag_row)
    for s in range(seqs):
        loads[s].wait()
        values = x_ref[s].astype(F32)
        values = values - jnp.mean(values, axis=-1, keepdims=True)
        variance = jnp.mean(values * values, axis=-1, keepdims=True)
        normed = values * lax.rsqrt(variance + 1e-05) * gain_ref[...] + shift_ref[...]
        high = normed.astype(BF16)
        low = (normed - high.astype(F32)).astype(BF16)
        to_right = jnp.dot(high, wr_rep, preferred_element_type=F32) + jnp.dot(
            low, wr_rep, preferred_element_type=F32
        )
        to_left = jnp.dot(high, wl_rep, preferred_element_type=F32) + jnp.dot(
            low, wl_rep, preferred_element_type=F32
        )
        right = jnp.where(seq_r == s, to_right, right)
        left = jnp.where(seq_l == s, to_left, left)
    out_ref[0:residues] = ((right + rb_rep) * (flag_r * crop)).astype(BF16)
    out_ref[residues : 2 * residues] = ((left + lb_rep) * (flag_l * crop)).astype(BF16)
    rows = _iota((2 * FLAG_ROWS, lanes), 0)
    out_ref[2 * residues :] = jnp.where(rows == 0, flag_row, 0.0).astype(BF16)


def _pack_kernel(steps, rows_chip, own_ref, other_ref, *out_refs):
    residues = own_ref.shape[0] // 2 - FLAG_ROWS
    total = rows_chip + FLAG_ROWS
    index = lax.axis_index("row")
    chip, core = index // 2, index % 2
    right = own_ref[0:residues] + other_ref[0:residues]
    flags = own_ref[2 * residues :] + other_ref[2 * residues :]
    for out_ref, (far, near) in zip(out_refs, ((0, 0),) + steps):
        target = chip ^ jnp.where(core == 1, far, near)
        start = pl.multiple_of(residues + target * rows_chip, rows_chip)
        out_ref[0:residues] = right
        slab = own_ref[pl.ds(start, rows_chip)] + other_ref[pl.ds(start, rows_chip)]
        tail = jnp.concatenate([slab.astype(F32), flags.astype(F32)], axis=0)
        out_ref[residues : residues + total] = tail[0:total].astype(BF16)


def _read(slot, rows):
    if not isinstance(slot, tuple):
        return slot[rows]
    north, south = slot
    return jnp.where(lax.axis_index("row") % 2 == 1, north[rows], south[rows])


def _rows(slot):
    return (slot[0] if isinstance(slot, tuple) else slot).shape


def _partial(slots, w_ref, a_ref):
    channels = w_ref.shape[0]
    height, lanes = _rows(slots[0])
    pair = lanes // channels
    width = w_ref.shape[1] // channels
    residues = height - 2 * pair - FLAG_ROWS
    core = lax.axis_index("row") % 2
    mine = _iota((pair, lanes), 1) // channels == _iota((pair, lanes), 0)
    rows = []
    for slot in slots:
        slab = _read(slot, slice(residues, residues + 2 * pair)).astype(F32)
        slab = jnp.where(core == 1, slab[pair:], slab[:pair])
        for i in range(pair):
            rows.append(jnp.where(mine, jnp.broadcast_to(slab[i : i + 1], (pair, lanes)), 0.0))
    spread = jnp.concatenate(rows, axis=0).astype(BF16)
    for e in range(0, channels, 2):
        block = w_ref[:, e * width : (e + 2) * width]
        product = jnp.dot(
            spread, jnp.concatenate([block] * pair, axis=0), preferred_element_type=F32
        )
        for n in range(len(slots)):
            for i in range(pair):
                at = (n * pair + i) * pair
                both = jnp.concatenate(
                    [product[at : at + pair, :width], product[at : at + pair, width:]], axis=0
                )
                a_ref[
                    n * lanes + e * pair : n * lanes + (e + 2) * pair,
                    i * width : (i + 1) * width,
                ] = both.astype(BF16)
    total = None
    for n, slot in enumerate(slots):
        part = jnp.dot(
            _read(slot, slice(0, residues)),
            a_ref[n * lanes : (n + 1) * lanes],
            preferred_element_type=F32,
        )
        total = part if total is None else total + part
    return total


def _live(slots):
    total = None
    for slot in slots:
        rows = _rows(slot)[0]
        part = _read(slot, slice(rows - 2 * FLAG_ROWS, rows)).astype(F32)[FLAG_ROWS:]
        total = part if total is None else total + part
    return total


def _first_kernel(channels, w_hbm, own_ref, w_ref, sum_ref, live_ref, raw_ref, wide_ref, a_ref, sem):
    copy = pltpu.make_async_copy(w_hbm, raw_ref, sem)
    copy.start()
    copy.wait()
    width = raw_ref.shape[1]
    wide_ref[...] = raw_ref[...].astype(F32)
    for e in range(channels):
        block = wide_ref[pl.ds(e, channels, stride=channels), :]
        w_ref[:, e * width : (e + 1) * width] = block.astype(BF16)
    sum_ref[...] = _partial([own_ref], w_ref, a_ref)
    live_ref[...] = _live([own_ref])


def _more_kernel(count, w_ref, sum_in, live_in, *refs):
    parcels, (sum_ref, live_ref, a_ref) = refs[:count], refs[count:]
    sum_ref[...] = sum_in[...] + _partial(parcels, w_ref, a_ref)
    live_ref[...] = live_in[...] + _live(parcels)


def _last_kernel(
    w_ref,
    sum_in,
    live_in,
    crop_hbm,
    bias_hbm,
    north_ref,
    south_ref,
    out_hbm,
    a_ref,
    crop_ref,
    bias_ref,
    out_ref,
    sems,
    out_sems,
):
    loads = [
        pltpu.make_async_copy(crop_hbm, crop_ref, sems.at[0]),
        pltpu.make_async_copy(bias_hbm, bias_ref, sems.at[1]),
    ]
    for copy in loads:
        copy.start()
    slots = [(north_ref, south_ref)]
    rows_here, _, width = out_ref.shape
    live = jnp.sum(live_in[...] + _live(slots))
    projected = sum_in[...] + _partial(slots, w_ref, a_ref)
    for copy in loads:
        copy.wait()
    crop = crop_ref[...].astype(F32)
    column = _column(crop)
    first = lax.axis_index("row") * rows_here
    lane = _iota(crop.shape, 1)
    stores = []
    for i in range(rows_here):
        crop_i = jnp.sum(jnp.where(lane == first + i, crop, 0.0), axis=1, keepdims=True)
        inverse = 1.0 / jnp.maximum(live * crop_i * column, 1.0)
        tile = projected[:, i * width : (i + 1) * width] * inverse + bias_ref[...]
        out_ref[i] = tile.astype(BF16)
        stores.append(pltpu.make_async_copy(out_ref.at[i], out_hbm.at[i], out_sems.at[i]))
        stores[-1].start()
    for copy in stores:
        copy.wait()


def per_device(
    alignment,
    seq_flags,
    crop_flags,
    norm_gain,
    norm_bias,
    left_weight,
    left_bias,
    right_weight,
    right_bias,
    out_weight,
    out_bias,
):
    seqs, residues, _ = alignment.shape
    channels = left_weight.shape[1]
    width = out_weight.shape[1]
    devices = lax.axis_size("row")
    rows_here = residues // devices
    rows_chip = 2 * rows_here
    chips = devices // 2
    lanes = 2 * seqs * channels
    half, quarter = chips // 2, max(1, chips // 4)
    steps = tuple(
        zip(
            [quarter] + [k for k in range(chips - 1, half, -1) if k != quarter],
            [k for k in range(half, 0, -1) if k != quarter] + [0],
        )
    )
    cores = [(d, d ^ 1) for d in range(devices)]
    crop = crop_flags.reshape(1, residues)
    limit = pltpu.CompilerParams(vmem_limit_bytes=48 * 1024 * 1024)
    anywhere = pl.BlockSpec(memory_space=pltpu.HBM)

    operands = (
        alignment,
        seq_flags.reshape(1, seqs),
        crop,
        norm_gain.reshape(1, -1),
        norm_bias.reshape(1, -1),
        left_weight.T,
        right_weight.T,
        left_bias.reshape(1, -1),
        right_bias.reshape(1, -1),
    )
    projected = pl.pallas_call(
        _project_kernel,
        out_shape=jax.ShapeDtypeStruct((2 * residues + 2 * FLAG_ROWS, lanes), BF16),
        in_specs=[anywhere] * len(operands),
        out_specs=_vmem(1)[0],
        scratch_shapes=[pltpu.VMEM(a.shape, a.dtype) for a in operands]
        + [pltpu.SemaphoreType.DMA((seqs,)), pltpu.SemaphoreType.DMA((len(operands) - 1,))],
        compiler_params=limit,
        name="project",
    )(*map(_stay, operands))
    other = lax.ppermute(projected, "row", cores)
    parcel = jax.ShapeDtypeStruct((residues + rows_chip + FLAG_ROWS, lanes), BF16)
    own, *parcels = pl.pallas_call(
        functools.partial(_pack_kernel, steps, rows_chip),
        out_shape=[parcel] * (1 + len(steps)),
        in_specs=_vmem(2),
        out_specs=_vmem(1 + len(steps)),
        compiler_params=limit,
        name="pack",
    )(projected, other)
    received, handed = [], []
    for (far, near), piece in zip(steps, parcels):
        pairs = [(2 * q + 1, 2 * (q ^ far) + 1) for q in range(chips)]
        back = [(2 * q + 1, 2 * q) for q in range(chips)]
        if near:
            pairs += [(2 * q, 2 * (q ^ near)) for q in range(chips)]
            back += [(2 * q, 2 * q + 1) for q in range(chips)]
        received.append(lax.ppermute(piece, "row", pairs))
        handed.append(lax.ppermute(received[-1], "row", back))

    columns = rows_here * width
    state = [
        jax.ShapeDtypeStruct((residues, columns), F32),
        jax.ShapeDtypeStruct((FLAG_ROWS, lanes), F32),
    ]
    weight, *carry = pl.pallas_call(
        functools.partial(_first_kernel, channels),
        out_shape=[jax.ShapeDtypeStruct((channels, channels * width), BF16)] + state,
        in_specs=[anywhere] + _vmem(1),
        out_specs=_vmem(3),
        scratch_shapes=[
            pltpu.VMEM(out_weight.shape, BF16),
            pltpu.VMEM(out_weight.shape, F32),
            pltpu.VMEM((lanes, columns), BF16),
            pltpu.SemaphoreType.DMA,
        ],
        compiler_params=limit,
        name="first",
    )(_stay(out_weight), own)
    middle = len(steps) // 2
    groups = [received[:middle], received[middle:-1] + handed[:middle], handed[middle:-1]]
    for group in groups:
        carry = pl.pallas_call(
            functools.partial(_more_kernel, len(group)),
            out_shape=state,
            in_specs=_vmem(3 + len(group)),
            out_specs=_vmem(2),
            scratch_shapes=[pltpu.VMEM((len(group) * lanes, columns), BF16)],
            compiler_params=limit,
        )(weight, *carry, *group)
    tile = (rows_here, residues, width)
    return pl.pallas_call(
        _last_kernel,
        out_shape=jax.ShapeDtypeStruct(tile, BF16),
        in_specs=_vmem(3) + [anywhere] * 2 + _vmem(2),
        out_specs=anywhere,
        scratch_shapes=[
            pltpu.VMEM((lanes, columns), BF16),
            pltpu.VMEM(crop.shape, crop.dtype),
            pltpu.VMEM((1, width), F32),
            pltpu.VMEM(tile, BF16),
            pltpu.SemaphoreType.DMA((2,)),
            pltpu.SemaphoreType.DMA((rows_here,)),
        ],
        compiler_params=limit,
        name="last",
    )(
        weight,
        *carry,
        _stay(crop),
        _stay(out_bias.reshape(1, -1)),
        received[-1],
        handed[-1],
    )


def solution(mesh):
    return jax.shard_map(
        per_device,
        mesh=mesh,
        in_specs=(
            P(("grp", "row"), None, None),
            P(("grp", "row")),
            P("grp"),
            P(),
            P(),
            P(),
            P(),
            P(),
            P(),
            P(),
            P(),
        ),
        out_specs=P(("grp", "row"), None, None),
        check_vma=False,
    )
```

time: 26 us -> 25.7 us (0.988)
  the two profiles are of different devices: /device:TPU:0 before, /device:TPU:1 now
where the time goes in v2:
time: 25.7 us; the launch traced here: 25.5 us
  starting transfers between devices  11.7 us (46%)
  Pallas kernels  9.04 us (35%)
  waiting for transfers between devices  4.6 us (18%)
    ppermute x4, starting transfers between devices, per_device(): received.append(lax.ppermute(piece, 'row', pairs))  9.04 us
    ppermute x4, waiting for transfers between devices, per_device(): received.append(lax.ppermute(piece, 'row', pairs))  3.25 us
    pallas_call x1, Pallas kernels, per_device(): pl.pallas_call(_project_kernel, out_shape=jax.ShapeDtypeStruct((2 * resid...  2.84 us
    ppermute x4, starting transfers between devices, per_device(): handed.append(lax.ppermute(received[-1], 'row', back))  2.6 us
    pallas_call x3, Pallas kernels, per_device(): pl.pallas_call(functools.partial(_more_kernel, len(group)), out_shape=sta...  2.33 us
    pallas_call x1, Pallas kernels, per_device(): pl.pallas_call(_last_kernel, out_shape=jax.ShapeDtypeStruct(tile, BF16),...  2.07 us
    pallas_call x1, Pallas kernels, per_device(): pl.pallas_call(functools.partial(_first_kernel, channels), out_shape=[jax...  1.76 us
    ppermute x1, waiting for transfers between devices, per_device(): other = lax.ppermute(projected, 'row', cores)  1.35 us
  transfers between devices with their start and end apart: 9, of which 4 were waited for; matrix products, arithmetic and copies ran while one was open for 0% of the time, Pallas kernels for 16%

profile of v2, /device:TPU:1, one launch (start us, length us, event | category | flops | bytes accessed | tf_op | source)
XLA Modules:
  0.0 25.5 jit_solution(2602318686572426698)
XLA Ops:
  0.0 2.8 %project.1.own_ref = bf16[272,256]{1,0:T(8,128)(2,1)S(1)} custom-call(bf16[4,128,256]{2,1,0:T(8,128)(2,1)} %x_hbm.1, s32[1,4]{1,0:T(1,128)} %bitcast.15, s32[1,128]{1,0:T(1,128)} %bitcast.11, f32[1,256]{1,0:T(1,128)} %bitcast.13, f32[1,256]{1,0:T(1,128)} %bitcast.14, bf16[32,256]{1,0:T(8,128)(2,1)} %bitcast.9, bf16[32,256]{1,0:T(8,128)(2,1)} %bitcast.10, ...), custom_call_target="tpu_custom_call" | custom-call | tf_op jit(solution)/shard_map/project/pallas_call | solution.py:322
  2.9 0.1 collective-permute-start
  2.9 1.3 %collective-permute-done.other_ref = bf16[272,256]{1,0:T(8,128)(2,1)S(1)} collective-permute-done((bf16[272,256]{1,0:T(8,128)(2,1)S(1)}, bf16[272,256]{1,0:T(8,128)(2,1)S(1)}, u32[]{:S(2)}, u32[]{:S(2)}) %collective-permute-start) | collective-permute-done | bytes 139296 | tf_op jit(solution)/shard_map/ppermute | solution.py:332
  4.3 2.5 %collective-permute-start.1 = (bf16[152,256]{1,0:T(8,128)(2,1)S(1)}, bf16[152,256]{1,0:T(8,128)(2,1)S(1)}, u32[]{:S(2)}, u32[]{:S(2)}) collective-permute-start(bf16[152,256]{1,0:T(8,128)(2,1)S(1)} %get-tuple-element.23), channel_id=1, source_target_pairs={{1,5},{3,7},{5,1},{7,3},{9,13},{11,15},{13,9},{15,11},{0,8},{2,10}... | collective-permute-start | bytes 233480 | tf_op jit(solution)/shard_map/ppermute | solution.py:349
  6.8 3.2 %collective-permute-start.2 = (bf16[152,256]{1,0:T(8,128)(2,1)S(1)}, bf16[152,256]{1,0:T(8,128)(2,1)S(1)}, u32[]{:S(2)}, u32[]{:S(2)}) collective-permute-start(bf16[152,256]{1,0:T(8,128)(2,1)S(1)} %get-tuple-element.24), channel_id=1, source_target_pairs={{1,15},{3,13},{5,11},{7,9},{9,7},{11,5},{13,3},{15,1},{0,6},{2,4},... | collective-permute-start | bytes 233480 | tf_op jit(solution)/shard_map/ppermute | solution.py:349
  9.9 1.1 %collective-permute-start.3 = (bf16[152,256]{1,0:T(8,128)(2,1)S(1)}, bf16[152,256]{1,0:T(8,128)(2,1)S(1)}, u32[]{:S(2)}, u32[]{:S(2)}) collective-permute-start(bf16[152,256]{1,0:T(8,128)(2,1)S(1)} %get-tuple-element.27), channel_id=1, source_target_pairs={{1,13},{3,15},{5,9},{7,11},{9,5},{11,7},{13,1},{15,3},{0,2},{2,0},... | collective-permute-start | bytes 233480 | tf_op jit(solution)/shard_map/ppermute | solution.py:349
  11.0 2.3 %collective-permute-start.7 = (bf16[152,256]{1,0:T(8,128)(2,1)S(1)}, bf16[152,256]{1,0:T(8,128)(2,1)S(1)}, u32[]{:S(2)}, u32[]{:S(2)}) collective-permute-start(bf16[152,256]{1,0:T(8,128)(2,1)S(1)} %get-tuple-element.32), channel_id=1, source_target_pairs={{1,11},{3,9},{5,15},{7,13},{9,3},{11,1},{13,7},{15,5},{17,27},{19,... | collective-permute-start | bytes 233480 | tf_op jit(solution)/shard_map/ppermute | solution.py:349
  13.4 0.0 collective-permute-done.1.refs_0_
  13.4 0.1 collective-permute-start.4
  13.5 0.2 collective-permute-done.2.refs_1_
  13.6 0.9 %collective-permute-start.5 = (bf16[152,256]{1,0:T(8,128)(2,1)S(1)}, bf16[152,256]{1,0:T(8,128)(2,1)S(1)}, u32[]{:S(2)}, u32[]{:S(2)}) collective-permute-start(bf16[152,256]{1,0:T(8,128)(2,1)S(1)} %collective-permute-done.2.refs_1_), channel_id=1, source_target_pairs={{1,0},{3,2},{5,4},{7,6},{9,8},{11,10},{13,12},{15,14},{0,1},{2,3},... | collective-permute-start | bytes 233480 | tf_op jit(solution)/shard_map/ppermute | solution.py:350
  14.5 0.5 %collective-permute-done.3.refs_0_ = bf16[152,256]{1,0:T(8,128)(2,1)S(1)} collective-permute-done((bf16[152,256]{1,0:T(8,128)(2,1)S(1)}, bf16[152,256]{1,0:T(8,128)(2,1)S(1)}, u32[]{:S(2)}, u32[]{:S(2)}) %collective-permute-start.3) | collective-permute-done | bytes 77856 | tf_op jit(solution)/shard_map/ppermute | solution.py:349
  15.0 0.4 %collective-permute-start.6 = (bf16[152,256]{1,0:T(8,128)(2,1)S(1)}, bf16[152,256]{1,0:T(8,128)(2,1)S(1)}, u32[]{:S(2)}, u32[]{:S(2)}) collective-permute-start(bf16[152,256]{1,0:T(8,128)(2,1)S(1)} %collective-permute-done.3.refs_0_), channel_id=1, source_target_pairs={{1,0},{3,2},{5,4},{7,6},{9,8},{11,10},{13,12},{15,14},{0,1},{2,3},... | collective-permute-start | bytes 233480 | tf_op jit(solution)/shard_map/ppermute | solution.py:350
  15.4 2.6 %collective-permute-done.7.north_ref = bf16[152,256]{1,0:T(8,128)(2,1)S(1)} collective-permute-done((bf16[152,256]{1,0:T(8,128)(2,1)S(1)}, bf16[152,256]{1,0:T(8,128)(2,1)S(1)}, u32[]{:S(2)}, u32[]{:S(2)}) %collective-permute-start.7) | collective-permute-done | bytes 77856 | tf_op jit(solution)/shard_map/ppermute | solution.py:349
  17.9 1.3 %collective-permute-start.8 = (bf16[152,256]{1,0:T(8,128)(2,1)S(1)}, bf16[152,256]{1,0:T(8,128)(2,1)S(1)}, u32[]{:S(2)}, u32[]{:S(2)}) collective-permute-start(bf16[152,256]{1,0:T(8,128)(2,1)S(1)} %collective-permute-done.7.north_ref), channel_id=1, source_target_pairs={{1,0},{3,2},{5,4},{7,6},{9,8},{11,10},{13,12},{15,14},{17,16},{19,... | collective-permute-start | bytes 233480 | tf_op jit(solution)/shard_map/ppermute | solution.py:350
  19.2 1.8 %first.1 = (bf16[32,4096]{1,0:T(8,128)(2,1)S(1)}, f32[128,1024]{1,0:T(8,128)S(1)}, f32[8,256]{1,0:T(8,128)S(1)}) custom-call(bf16[1024,128]{1,0:T(8,128)(2,1)} %w_hbm.1, bf16[152,256]{1,0:T(8,128)(2,1)S(1)} %get-tuple-element.19.own_ref), custom_call_target="tpu_custom_call" | custom-call | tf_op jit(solution)/shard_map/first/pallas_call | solution.py:357
  21.0 0.7 %shard_map.109 = (f32[128,1024]{1,0:T(8,128)S(1)}, f32[8,256]{1,0:T(8,128)S(1)}) custom-call(bf16[32,4096]{1,0:T(8,128)(2,1)S(1)} %get-tuple-element.20.w_ref, f32[128,1024]{1,0:T(8,128)S(1)} %get-tuple-element.21.sum_in, f32[8,256]{1,0:T(8,128)S(1)} %get-tuple-element.22.live_in, bf16[152,256]{1,0:T(8,128)(2,1)S(1)} %collective-permute-done.1.refs_0_, ...), custom_call_target="tpu_custom_call" | custom-call | tf_op jit(solution)/shard_map/pallas_call | solution.py:374
  21.7 0.0 collective-permute-done.4.refs_1_
  21.7 0.0 collective-permute-done.5.refs_2_
  21.8 0.9 %shard_map.110 = (f32[128,1024]{1,0:T(8,128)S(1)}, f32[8,256]{1,0:T(8,128)S(1)}) custom-call(bf16[32,4096]{1,0:T(8,128)(2,1)S(1)} %get-tuple-element.20.w_ref, f32[128,1024]{1,0:T(8,128)S(1)} %get-tuple-element.25.sum_in, f32[8,256]{1,0:T(8,128)S(1)} %get-tuple-element.26.live_in, bf16[152,256]{1,0:T(8,128)(2,1)S(1)} %collective-permute-done.3.refs_0_, ...), custom_call_target="tpu_custom_call" | custom-call | tf_op jit(solution)/shard_map/pallas_call | solution.py:374
  22.7 0.0 collective-permute-done.6.refs_0_
  22.7 0.7 %shard_map.111 = (f32[128,1024]{1,0:T(8,128)S(1)}, f32[8,256]{1,0:T(8,128)S(1)}) custom-call(bf16[32,4096]{1,0:T(8,128)(2,1)S(1)} %get-tuple-element.20.w_ref, f32[128,1024]{1,0:T(8,128)S(1)} %get-tuple-element.28.sum_in, f32[8,256]{1,0:T(8,128)S(1)} %get-tuple-element.29.live_in, bf16[152,256]{1,0:T(8,128)(2,1)S(1)} %collective-permute-done.6.refs_0_), custom_call_target="tpu_custom_call" | custom-call | tf_op jit(solution)/shard_map/pallas_call | solution.py:374
  23.4 0.0 collective-permute-done.8.south_ref
  23.4 2.1 %last.1 = bf16[8,128,128]{2,1,0:T(8,128)(2,1)} custom-call(bf16[32,4096]{1,0:T(8,128)(2,1)S(1)} %get-tuple-element.20.w_ref, f32[128,1024]{1,0:T(8,128)S(1)} %get-tuple-element.30.sum_in, f32[8,256]{1,0:T(8,128)S(1)} %get-tuple-element.31.live_in, s32[1,128]{1,0:T(1,128)} %bitcast.12, f32[1,128]{1,0:T(1,128)} %bitcast.18, ...), custom_call_target="tpu_custom_call" | custom-call | tf_op jit(solution)/shard_map/last/pallas_call | solution.py:383
  (1 shorter events, 0.0 us)
Async XLA Ops:
  2.9 1.4 %collective-permute-start = (bf16[272,256]{1,0:T(8,128)(2,1)S(1)}, bf16[272,256]{1,0:T(8,128)(2,1)S(1)}, u32[]{:S(2)}, u32[]{:S(2)}) collective-permute-start(bf16[272,256]{1,0:T(8,128)(2,1)S(1)} %project.1.own_ref), channel_id=1, source_target_pairs={{0,1},{1,0},{2,3},{3,2},{4,5},{5,4},{6,7},{7,6},{8,9},{9,8},{10,11... | collective-permute-start | bytes 417800 | tf_op jit(solution)/shard_map/ppermute | solution.py:332
  4.3 9.1 %collective-permute-start.1 = (bf16[152,256]{1,0:T(8,128)(2,1)S(1)}, bf16[152,256]{1,0:T(8,128)(2,1)S(1)}, u32[]{:S(2)}, u32[]{:S(2)}) collective-permute-start(bf16[152,256]{1,0:T(8,128)(2,1)S(1)} %get-tuple-element.23), channel_id=1, source_target_pairs={{1,5},{3,7},{5,1},{7,3},{9,13},{11,15},{13,9},{15,11},{0,8},{2,10}... | collective-permute-start | bytes 233480 | tf_op jit(solution)/shard_map/ppermute | solution.py:349
  6.8 6.8 %collective-permute-start.2 = (bf16[152,256]{1,0:T(8,128)(2,1)S(1)}, bf16[152,256]{1,0:T(8,128)(2,1)S(1)}, u32[]{:S(2)}, u32[]{:S(2)}) collective-permute-start(bf16[152,256]{1,0:T(8,128)(2,1)S(1)} %get-tuple-element.24), channel_id=1, source_target_pairs={{1,15},{3,13},{5,11},{7,9},{9,7},{11,5},{13,3},{15,1},{0,6},{2,4},... | collective-permute-start | bytes 233480 | tf_op jit(solution)/shard_map/ppermute | solution.py:349
  9.9 5.0 %collective-permute-start.3 = (bf16[152,256]{1,0:T(8,128)(2,1)S(1)}, bf16[152,256]{1,0:T(8,128)(2,1)S(1)}, u32[]{:S(2)}, u32[]{:S(2)}) collective-permute-start(bf16[152,256]{1,0:T(8,128)(2,1)S(1)} %get-tuple-element.27), channel_id=1, source_target_pairs={{1,13},{3,15},{5,9},{7,11},{9,5},{11,7},{13,1},{15,3},{0,2},{2,0},... | collective-permute-start | bytes 233480 | tf_op jit(solution)/shard_map/ppermute | solution.py:349
  11.0 6.9 %collective-permute-start.7 = (bf16[152,256]{1,0:T(8,128)(2,1)S(1)}, bf16[152,256]{1,0:T(8,128)(2,1)S(1)}, u32[]{:S(2)}, u32[]{:S(2)}) collective-permute-start(bf16[152,256]{1,0:T(8,128)(2,1)S(1)} %get-tuple-element.32), channel_id=1, source_target_pairs={{1,11},{3,9},{5,15},{7,13},{9,3},{11,1},{13,7},{15,5},{17,27},{19,... | collective-permute-start | bytes 233480 | tf_op jit(solution)/shard_map/ppermute | solution.py:349
  13.4 8.4 %collective-permute-start.4 = (bf16[152,256]{1,0:T(8,128)(2,1)S(1)}, bf16[152,256]{1,0:T(8,128)(2,1)S(1)}, u32[]{:S(2)}, u32[]{:S(2)}) collective-permute-start(bf16[152,256]{1,0:T(8,128)(2,1)S(1)} %collective-permute-done.1.refs_0_), channel_id=1, source_target_pairs={{1,0},{3,2},{5,4},{7,6},{9,8},{11,10},{13,12},{15,14},{0,1},{2,3},... | collective-permute-start | bytes 233480 | tf_op jit(solution)/shard_map/ppermute | solution.py:350
  13.6 8.1 %collective-permute-start.5 = (bf16[152,256]{1,0:T(8,128)(2,1)S(1)}, bf16[152,256]{1,0:T(8,128)(2,1)S(1)}, u32[]{:S(2)}, u32[]{:S(2)}) collective-permute-start(bf16[152,256]{1,0:T(8,128)(2,1)S(1)} %collective-permute-done.2.refs_1_), channel_id=1, source_target_pairs={{1,0},{3,2},{5,4},{7,6},{9,8},{11,10},{13,12},{15,14},{0,1},{2,3},... | collective-permute-start | bytes 233480 | tf_op jit(solution)/shard_map/ppermute | solution.py:350
  15.0 7.7 %collective-permute-start.6 = (bf16[152,256]{1,0:T(8,128)(2,1)S(1)}, bf16[152,256]{1,0:T(8,128)(2,1)S(1)}, u32[]{:S(2)}, u32[]{:S(2)}) collective-permute-start(bf16[152,256]{1,0:T(8,128)(2,1)S(1)} %collective-permute-done.3.refs_0_), channel_id=1, source_target_pairs={{1,0},{3,2},{5,4},{7,6},{9,8},{11,10},{13,12},{15,14},{0,1},{2,3},... | collective-permute-start | bytes 233480 | tf_op jit(solution)/shard_map/ppermute | solution.py:350
  17.9 5.4 %collective-permute-start.8 = (bf16[152,256]{1,0:T(8,128)(2,1)S(1)}, bf16[152,256]{1,0:T(8,128)(2,1)S(1)}, u32[]{:S(2)}, u32[]{:S(2)}) collective-permute-start(bf16[152,256]{1,0:T(8,128)(2,1)S(1)} %collective-permute-done.7.north_ref), channel_id=1, source_target_pairs={{1,0},{3,2},{5,4},{7,6},{9,8},{11,10},{13,12},{15,14},{17,16},{19,... | collective-permute-start | bytes 233480 | tf_op jit(solution)/shard_map/ppermute | solution.py:350

commit v3 on v2

--- a/solution.py
+++ b/solution.py
@@ -77,7 +77,7 @@
     loads = [
         pltpu.make_async_copy(x_hbm.at[s], x_ref.at[s], x_sems.at[s]) for s in range(seqs)
     ]
-    for copy in loads + small:
+    for copy in small + loads:
         copy.start()
     pair = 2 * seqs
     lanes = pair * channels
@@ -162,7 +162,7 @@
     return (slot[0] if isinstance(slot, tuple) else slot).shape
 
 
-def _partial(slots, w_ref, a_ref):
+def _spread(slots, w_ref, a_ref):
     channels = w_ref.shape[0]
     height, lanes = _rows(slots[0])
     pair = lanes // channels
@@ -192,11 +192,15 @@
                     n * lanes + e * pair : n * lanes + (e + 2) * pair,
                     i * width : (i + 1) * width,
                 ] = both.astype(BF16)
+
+
+def _contract(slots, a_ref, residues, columns=slice(None)):
+    lanes = _rows(slots[0])[1]
     total = None
     for n, slot in enumerate(slots):
         part = jnp.dot(
             _read(slot, slice(0, residues)),
-            a_ref[n * lanes : (n + 1) * lanes],
+            a_ref[n * lanes : (n + 1) * lanes, columns],
             preferred_element_type=F32,
         )
         total = part if total is None else total + part
@@ -212,65 +216,75 @@
     return total
 
 
-def _first_kernel(channels, w_hbm, own_ref, w_ref, sum_ref, live_ref, raw_ref, wide_ref, a_ref, sem):
-    copy = pltpu.make_async_copy(w_hbm, raw_ref, sem)
-    copy.start()
-    copy.wait()
+def _prepare_kernel(
+    channels, raw_ref, crop_hbm, bias_hbm, w_ref, column_ref, own_ref, bias_ref, wide_ref, crop_ref, sems
+):
+    loads = [
+        pltpu.make_async_copy(src, dst, sems.at[n])
+        for n, (src, dst) in enumerate([(crop_hbm, crop_ref), (bias_hbm, bias_ref)])
+    ]
+    for copy in loads:
+        copy.start()
     width = raw_ref.shape[1]
     wide_ref[...] = raw_ref[...].astype(F32)
     for e in range(channels):
         block = wide_ref[pl.ds(e, channels, stride=channels), :]
         w_ref[:, e * width : (e + 1) * width] = block.astype(BF16)
-    sum_ref[...] = _partial([own_ref], w_ref, a_ref)
-    live_ref[...] = _live([own_ref])
+    for copy in loads:
+        copy.wait()
+    crop = crop_ref[...].astype(F32)
+    column_ref[...] = jnp.broadcast_to(_column(crop), column_ref.shape)
+    rows_here = own_ref.shape[0]
+    square = (rows_here, crop.shape[1])
+    mine = _iota(square, 1) - lax.axis_index("row") * rows_here == _iota(square, 0)
+    kept = jnp.where(mine, jnp.broadcast_to(crop, square), 0.0)
+    own_ref[...] = jnp.broadcast_to(jnp.sum(kept, axis=1, keepdims=True), own_ref.shape)
+
+
+def _first_kernel(count, w_ref, *refs):
+    slots, (sum_ref, live_ref, a_ref) = refs[:count], refs[count:]
+    _spread(slots, w_ref, a_ref)
+    sum_ref[...] = _contract(slots, a_ref, sum_ref.shape[0])
+    live_ref[...] = _live(slots)
 
 
 def _more_kernel(count, w_ref, sum_in, live_in, *refs):
-    parcels, (sum_ref, live_ref, a_ref) = refs[:count], refs[count:]
-    sum_ref[...] = sum_in[...] + _partial(parcels, w_ref, a_ref)
-    live_ref[...] = live_in[...] + _live(parcels)
+    slots, (sum_ref, live_ref, a_ref) = refs[:count], refs[count:]
+    _spread(slots, w_ref, a_ref)
+    sum_ref[...] = sum_in[...] + _contract(slots, a_ref, sum_ref.shape[0])
+    live_ref[...] = live_in[...] + _live(slots)
 
 
 def _last_kernel(
     w_ref,
+    column_ref,
+    own_ref,
+    bias_ref,
     sum_in,
     live_in,
-    crop_hbm,
-    bias_hbm,
     north_ref,
     south_ref,
     out_hbm,
     a_ref,
-    crop_ref,
-    bias_ref,
     out_ref,
     sems,
-    out_sems,
 ):
-    loads = [
-        pltpu.make_async_copy(crop_hbm, crop_ref, sems.at[0]),
-        pltpu.make_async_copy(bias_hbm, bias_ref, sems.at[1]),
-    ]
-    for copy in loads:
-        copy.start()
     slots = [(north_ref, south_ref)]
     rows_here, _, width = out_ref.shape
-    live = jnp.sum(live_in[...] + _live(slots))
-    projected = sum_in[...] + _partial(slots, w_ref, a_ref)
-    for copy in loads:
-        copy.wait()
-    crop = crop_ref[...].astype(F32)
-    column = _column(crop)
-    first = lax.axis_index("row") * rows_here
-    lane = _iota(crop.shape, 1)
+    flags = live_in[...] + _live(slots)
+    live = jnp.sum(jnp.sum(flags, axis=1, keepdims=True), axis=0, keepdims=True)
+    _spread(slots, w_ref, a_ref)
     stores = []
-    for i in range(rows_here):
-        crop_i = jnp.sum(jnp.where(lane == first + i, crop, 0.0), axis=1, keepdims=True)
-        inverse = 1.0 / jnp.maximum(live * crop_i * column, 1.0)
-        tile = projected[:, i * width : (i + 1) * width] * inverse + bias_ref[...]
-        out_ref[i] = tile.astype(BF16)
-        stores.append(pltpu.make_async_copy(out_ref.at[i], out_hbm.at[i], out_sems.at[i]))
-        stores[-1].start()
+    group = 2 if rows_here % 2 == 0 else 1
+    for first in range(0, rows_here, group):
+        columns = slice(first * width, (first + group) * width)
+        projected = sum_in[:, columns] + _contract(slots, a_ref, sum_in.shape[0], columns)
+        for i in range(first, first + group):
+            divisor = jnp.maximum(live * own_ref[i : i + 1] * column_ref[...], 1.0)
+            part = projected[:, (i - first) * width : (i - first + 1) * width]
+            out_ref[i] = (part / divisor + bias_ref[...]).astype(BF16)
+            stores.append(pltpu.make_async_copy(out_ref.at[i], out_hbm.at[i], sems.at[i]))
+            stores[-1].start()
     for copy in stores:
         copy.wait()
 
@@ -354,55 +368,60 @@
         jax.ShapeDtypeStruct((residues, columns), F32),
         jax.ShapeDtypeStruct((FLAG_ROWS, lanes), F32),
     ]
-    weight, *carry = pl.pallas_call(
-        functools.partial(_first_kernel, channels),
-        out_shape=[jax.ShapeDtypeStruct((channels, channels * width), BF16)] + state,
-        in_specs=[anywhere] + _vmem(1),
-        out_specs=_vmem(3),
+    weight, *spread = pl.pallas_call(
+        functools.partial(_prepare_kernel, channels),
+        out_shape=[
+            jax.ShapeDtypeStruct((channels, channels * width), BF16),
+            jax.ShapeDtypeStruct((residues, width), F32),
+            jax.ShapeDtypeStruct((rows_here, width), F32),
+            jax.ShapeDtypeStruct((1, width), F32),
+        ],
+        in_specs=_vmem(1) + [anywhere] * 2,
+        out_specs=_vmem(4),
         scratch_shapes=[
-            pltpu.VMEM(out_weight.shape, BF16),
             pltpu.VMEM(out_weight.shape, F32),
-            pltpu.VMEM((lanes, columns), BF16),
-            pltpu.SemaphoreType.DMA,
+            pltpu.VMEM(crop.shape, crop.dtype),
+            pltpu.SemaphoreType.DMA((2,)),
         ],
         compiler_params=limit,
-        name="first",
-    )(_stay(out_weight), own)
+        name="prepare",
+    )(out_weight, _stay(crop), _stay(out_bias.reshape(1, -1)))
+
     middle = len(steps) // 2
-    groups = [received[:middle], received[middle:-1] + handed[:middle], handed[middle:-1]]
-    for group in groups:
-        carry = pl.pallas_call(
-            functools.partial(_more_kernel, len(group)),
-            out_shape=state,
-            in_specs=_vmem(3 + len(group)),
-            out_specs=_vmem(2),
-            scratch_shapes=[pltpu.VMEM((len(group) * lanes, columns), BF16)],
-            compiler_params=limit,
-        )(weight, *carry, *group)
+    early = [own] + received[:-1] + handed[:middle]
+    carry = pl.pallas_call(
+        functools.partial(_first_kernel, len(early)),
+        out_shape=state,
+        in_specs=_vmem(1 + len(early)),
+        out_specs=_vmem(2),
+        scratch_shapes=[pltpu.VMEM((len(early) * lanes, columns), BF16)],
+        compiler_params=limit,
+        name="early",
+    )(weight, *early)
+    late = handed[middle:-1]
+    carry = pl.pallas_call(
+        functools.partial(_more_kernel, len(late)),
+        out_shape=state,
+        in_specs=_vmem(3 + len(late)),
+        out_specs=_vmem(2),
+        scratch_shapes=[pltpu.VMEM((len(late) * lanes, columns), BF16)],
+        compiler_params=limit,
+        name="late",
+    )(weight, *carry, *late)
     tile = (rows_here, residues, width)
     return pl.pallas_call(
         _last_kernel,
         out_shape=jax.ShapeDtypeStruct(tile, BF16),
-        in_specs=_vmem(3) + [anywhere] * 2 + _vmem(2),
+        in_specs=_vmem(8),
         out_specs=anywhere,
         scratch_shapes=[
             pltpu.VMEM((lanes, columns), BF16),
-            pltpu.VMEM(crop.shape, crop.dtype),
-            pltpu.VMEM((1, width), F32),
             pltpu.VMEM(tile, BF16),
-            pltpu.SemaphoreType.DMA((2,)),
             pltpu.SemaphoreType.DMA((rows_here,)),
         ],
         compiler_params=limit,
         name="last",
-    )(
-        weight,
-        *carry,
-        _stay(crop),
-        _stay(out_bias.reshape(1, -1)),
-        received[-1],
-        handed[-1],
-    )
+    )(weight, *spread, *carry, received[-1], handed[-1])
 
 
 def solution(mesh):

time: 25.7 us -> 23.9 us (0.930)
  Pallas kernels: 9.04 us -> 7.24 us
    pallas_call x4 -> x3, Pallas kernels: 4.09 us -> 2.95 us  [the longest x1 1.47 us: per_device(): pl.pallas_call(functools.partial(_first_kernel, len(early)), out_shape=st...]
    pallas_call x1, Pallas kernels: 2.07 us -> 1.41 us  [per_device(): pl.pallas_call(_last_kernel, out_shape=jax.ShapeDtypeStruct(tile, BF16),...]
  transfers between devices with their start and end apart: 9 -> 9, of which waited for: 4 -> 4; matrix products, arithmetic and copies ran while one was open for 0% -> 0% of each run, Pallas kernels for 16% -> 12%
where the time goes in v3:
time: 23.9 us; the launch traced here: 23.7 us
  starting transfers between devices  11.8 us (49%)
  Pallas kernels  7.24 us (30%)
  waiting for transfers between devices  4.58 us (19%)
    ppermute x4, starting transfers between devices, per_device(): received.append(lax.ppermute(piece, 'row', pairs))  9.06 us
    ppermute x4, waiting for transfers between devices, per_device(): received.append(lax.ppermute(piece, 'row', pairs))  3.23 us
    pallas_call x1, Pallas kernels, per_device(): pl.pallas_call(_project_kernel, out_shape=jax.ShapeDtypeStruct((2 * resid...  2.85 us
    ppermute x4, starting transfers between devices, per_device(): handed.append(lax.ppermute(received[-1], 'row', back))  2.61 us
    pallas_call x1, Pallas kernels, per_device(): pl.pallas_call(functools.partial(_first_kernel, len(early)), out_shape=st...  1.47 us
    pallas_call x1, Pallas kernels, per_device(): pl.pallas_call(_last_kernel, out_shape=jax.ShapeDtypeStruct(tile, BF16),...  1.41 us
    ppermute x1, waiting for transfers between devices, per_device(): other = lax.ppermute(projected, 'row', cores)  1.34 us
    pallas_call x1, Pallas kernels, per_device(): pl.pallas_call(functools.partial(_prepare_kernel, channels), out_shape=[j...  0.79 us
  transfers between devices with their start and end apart: 9, of which 4 were waited for; matrix products, arithmetic and copies ran while one was open for 0% of the time, Pallas kernels for 12%

profile of v3, /device:TPU:1, one launch (start us, length us, event | category | flops | bytes accessed | tf_op | source)
XLA Modules:
  0.0 23.7 jit_solution(6083419916503384016)
XLA Ops:
  0.0 0.0 copy-start
  0.0 2.9 %project.1.own_ref = bf16[272,256]{1,0:T(8,128)(2,1)S(1)} custom-call(bf16[4,128,256]{2,1,0:T(8,128)(2,1)} %x_hbm.1, s32[1,4]{1,0:T(1,128)} %bitcast.15, s32[1,128]{1,0:T(1,128)} %bitcast.11, f32[1,256]{1,0:T(1,128)} %bitcast.13, f32[1,256]{1,0:T(1,128)} %bitcast.14, bf16[32,256]{1,0:T(8,128)(2,1)} %bitcast.9, bf16[32,256]{1,0:T(8,128)(2,1)} %bitcast.10, ...), custom_call_target="tpu_custom_call" | custom-call | tf_op jit(solution)/shard_map/project/pallas_call | solution.py:336
  2.9 0.1 collective-permute-start
  2.9 1.3 %collective-permute-done.other_ref = bf16[272,256]{1,0:T(8,128)(2,1)S(1)} collective-permute-done((bf16[272,256]{1,0:T(8,128)(2,1)S(1)}, bf16[272,256]{1,0:T(8,128)(2,1)S(1)}, u32[]{:S(2)}, u32[]{:S(2)}) %collective-permute-start) | collective-permute-done | bytes 139296 | tf_op jit(solution)/shard_map/ppermute | solution.py:346
  4.3 2.5 %collective-permute-start.1 = (bf16[152,256]{1,0:T(8,128)(2,1)S(1)}, bf16[152,256]{1,0:T(8,128)(2,1)S(1)}, u32[]{:S(2)}, u32[]{:S(2)}) collective-permute-start(bf16[152,256]{1,0:T(8,128)(2,1)S(1)} %get-tuple-element.23), channel_id=1, source_target_pairs={{1,5},{3,7},{5,1},{7,3},{9,13},{11,15},{13,9},{15,11},{0,8},{2,10}... | collective-permute-start | bytes 233480 | tf_op jit(solution)/shard_map/ppermute | solution.py:363
  6.8 3.2 %collective-permute-start.2 = (bf16[152,256]{1,0:T(8,128)(2,1)S(1)}, bf16[152,256]{1,0:T(8,128)(2,1)S(1)}, u32[]{:S(2)}, u32[]{:S(2)}) collective-permute-start(bf16[152,256]{1,0:T(8,128)(2,1)S(1)} %get-tuple-element.24), channel_id=1, source_target_pairs={{1,15},{3,13},{5,11},{7,9},{9,7},{11,5},{13,3},{15,1},{0,6},{2,4},... | collective-permute-start | bytes 233480 | tf_op jit(solution)/shard_map/ppermute | solution.py:363
  10.0 1.1 %collective-permute-start.3 = (bf16[152,256]{1,0:T(8,128)(2,1)S(1)}, bf16[152,256]{1,0:T(8,128)(2,1)S(1)}, u32[]{:S(2)}, u32[]{:S(2)}) collective-permute-start(bf16[152,256]{1,0:T(8,128)(2,1)S(1)} %get-tuple-element.25), channel_id=1, source_target_pairs={{1,13},{3,15},{5,9},{7,11},{9,5},{11,7},{13,1},{15,3},{0,2},{2,0},... | collective-permute-start | bytes 233480 | tf_op jit(solution)/shard_map/ppermute | solution.py:363
  11.0 2.3 %collective-permute-start.7 = (bf16[152,256]{1,0:T(8,128)(2,1)S(1)}, bf16[152,256]{1,0:T(8,128)(2,1)S(1)}, u32[]{:S(2)}, u32[]{:S(2)}) collective-permute-start(bf16[152,256]{1,0:T(8,128)(2,1)S(1)} %get-tuple-element.30), channel_id=1, source_target_pairs={{1,11},{3,9},{5,15},{7,13},{9,3},{11,1},{13,7},{15,5},{17,27},{19,... | collective-permute-start | bytes 233480 | tf_op jit(solution)/shard_map/ppermute | solution.py:363
  13.4 0.0 collective-permute-done.1.refs_1_
  13.4 0.1 collective-permute-start.4
  13.5 0.1 collective-permute-done.2.refs_2_
  13.6 0.9 %collective-permute-start.5 = (bf16[152,256]{1,0:T(8,128)(2,1)S(1)}, bf16[152,256]{1,0:T(8,128)(2,1)S(1)}, u32[]{:S(2)}, u32[]{:S(2)}) collective-permute-start(bf16[152,256]{1,0:T(8,128)(2,1)S(1)} %collective-permute-done.2.refs_2_), channel_id=1, source_target_pairs={{1,0},{3,2},{5,4},{7,6},{9,8},{11,10},{13,12},{15,14},{0,1},{2,3},... | collective-permute-start | bytes 233480 | tf_op jit(solution)/shard_map/ppermute | solution.py:364
  14.5 0.5 %collective-permute-done.3.refs_3_ = bf16[152,256]{1,0:T(8,128)(2,1)S(1)} collective-permute-done((bf16[152,256]{1,0:T(8,128)(2,1)S(1)}, bf16[152,256]{1,0:T(8,128)(2,1)S(1)}, u32[]{:S(2)}, u32[]{:S(2)}) %collective-permute-start.3) | collective-permute-done | bytes 77856 | tf_op jit(solution)/shard_map/ppermute | solution.py:363
  15.0 0.4 %collective-permute-start.6 = (bf16[152,256]{1,0:T(8,128)(2,1)S(1)}, bf16[152,256]{1,0:T(8,128)(2,1)S(1)}, u32[]{:S(2)}, u32[]{:S(2)}) collective-permute-start(bf16[152,256]{1,0:T(8,128)(2,1)S(1)} %collective-permute-done.3.refs_3_), channel_id=1, source_target_pairs={{1,0},{3,2},{5,4},{7,6},{9,8},{11,10},{13,12},{15,14},{0,1},{2,3},... | collective-permute-start | bytes 233480 | tf_op jit(solution)/shard_map/ppermute | solution.py:364
  15.4 2.6 %collective-permute-done.7.north_ref = bf16[152,256]{1,0:T(8,128)(2,1)S(1)} collective-permute-done((bf16[152,256]{1,0:T(8,128)(2,1)S(1)}, bf16[152,256]{1,0:T(8,128)(2,1)S(1)}, u32[]{:S(2)}, u32[]{:S(2)}) %collective-permute-start.7) | collective-permute-done | bytes 77856 | tf_op jit(solution)/shard_map/ppermute | solution.py:363
  18.0 1.3 %collective-permute-start.8 = (bf16[152,256]{1,0:T(8,128)(2,1)S(1)}, bf16[152,256]{1,0:T(8,128)(2,1)S(1)}, u32[]{:S(2)}, u32[]{:S(2)}) collective-permute-start(bf16[152,256]{1,0:T(8,128)(2,1)S(1)} %collective-permute-done.7.north_ref), channel_id=1, source_target_pairs={{1,0},{3,2},{5,4},{7,6},{9,8},{11,10},{13,12},{15,14},{17,16},{19,... | collective-permute-start | bytes 233480 | tf_op jit(solution)/shard_map/ppermute | solution.py:364
  19.3 0.0 copy-done
  19.3 0.8 %prepare.1 = (bf16[32,4096]{1,0:T(8,128)(2,1)S(1)}, f32[128,128]{1,0:T(8,128)S(1)}, f32[8,128]{1,0:T(8,128)S(1)}, f32[1,128]{1,0:T(1,128)S(1)}) custom-call(bf16[1024,128]{1,0:T(8,128)(2,1)S(1)} %copy-done, s32[1,128]{1,0:T(1,128)} %bitcast.12, f32[1,128]{1,0:T(1,128)} %bitcast.18), custom_call_target="tpu_custom_call" | custom-call | tf_op jit(solution)/shard_map/prepare/pallas_call | solution.py:371
  20.1 0.0 collective-permute-done.4.refs_4_
  20.1 0.0 collective-permute-done.5.refs_5_
  20.1 1.5 %early.1 = (f32[128,1024]{1,0:T(8,128)S(1)}, f32[8,256]{1,0:T(8,128)S(1)}) custom-call(bf16[32,4096]{1,0:T(8,128)(2,1)S(1)} %get-tuple-element.18.w_ref, bf16[152,256]{1,0:T(8,128)(2,1)S(1)} %get-tuple-element.22.refs_0_, bf16[152,256]{1,0:T(8,128)(2,1)S(1)} %collective-permute-done.1.refs_1_, bf16[152,256]{1,0:T(8,128)(2,1)S(1)} %collective-permute-done.2.refs_2_, ...), custom_call_target="tpu_custom_call" | custom-call | tf_op jit(solution)/shard_map/early/pallas_call | solution.py:392
  21.6 0.0 collective-permute-done.6.refs_0_
  21.6 0.7 %late.1 = (f32[128,1024]{1,0:T(8,128)S(1)}, f32[8,256]{1,0:T(8,128)S(1)}) custom-call(bf16[32,4096]{1,0:T(8,128)(2,1)S(1)} %get-tuple-element.18.w_ref, f32[128,1024]{1,0:T(8,128)S(1)} %get-tuple-element.26.sum_in, f32[8,256]{1,0:T(8,128)S(1)} %get-tuple-element.27.live_in, bf16[152,256]{1,0:T(8,128)(2,1)S(1)} %collective-permute-done.6.refs_0_), custom_call_target="tpu_custom_call" | custom-call | tf_op jit(solution)/shard_map/late/pallas_call | solution.py:402
  22.3 0.0 collective-permute-done.8.south_ref
  22.3 1.4 %last.1 = bf16[8,128,128]{2,1,0:T(8,128)(2,1)} custom-call(bf16[32,4096]{1,0:T(8,128)(2,1)S(1)} %get-tuple-element.18.w_ref, f32[128,128]{1,0:T(8,128)S(1)} %get-tuple-element.19.column_ref, f32[8,128]{1,0:T(8,128)S(1)} %get-tuple-element.20.own_ref, f32[1,128]{1,0:T(1,128)S(1)} %get-tuple-element.21.bias_ref, f32[128,1024]{1,0:T(8,128)S(1)} %get-tuple-element.28.sum_in, ...), custom_call_target="tpu_custom_call" | custom-call | tf_op jit(solution)/shard_map/last/pallas_call | solution.py:412
  (1 shorter events, 0.0 us)
Async XLA Ops:
  0.0 19.3 %copy-start = (bf16[1024,128]{1,0:T(8,128)(2,1)S(1)}, bf16[1024,128]{1,0:T(8,128)(2,1)}, u32[]{:S(2)}) copy-start(bf16[1024,128]{1,0:T(8,128)(2,1)} %raw_ref.1) | copy-start | bytes 786436
  2.9 1.4 %collective-permute-start = (bf16[272,256]{1,0:T(8,128)(2,1)S(1)}, bf16[272,256]{1,0:T(8,128)(2,1)S(1)}, u32[]{:S(2)}, u32[]{:S(2)}) collective-permute-start(bf16[272,256]{1,0:T(8,128)(2,1)S(1)} %project.1.own_ref), channel_id=1, source_target_pairs={{0,1},{1,0},{2,3},{3,2},{4,5},{5,4},{6,7},{7,6},{8,9},{9,8},{10,11... | collective-permute-start | bytes 417800 | tf_op jit(solution)/shard_map/ppermute | solution.py:346
  4.3 9.1 %collective-permute-start.1 = (bf16[152,256]{1,0:T(8,128)(2,1)S(1)}, bf16[152,256]{1,0:T(8,128)(2,1)S(1)}, u32[]{:S(2)}, u32[]{:S(2)}) collective-permute-start(bf16[152,256]{1,0:T(8,128)(2,1)S(1)} %get-tuple-element.23), channel_id=1, source_target_pairs={{1,5},{3,7},{5,1},{7,3},{9,13},{11,15},{13,9},{15,11},{0,8},{2,10}... | collective-permute-start | bytes 233480 | tf_op jit(solution)/shard_map/ppermute | solution.py:363
  6.8 6.8 %collective-permute-start.2 = (bf16[152,256]{1,0:T(8,128)(2,1)S(1)}, bf16[152,256]{1,0:T(8,128)(2,1)S(1)}, u32[]{:S(2)}, u32[]{:S(2)}) collective-permute-start(bf16[152,256]{1,0:T(8,128)(2,1)S(1)} %get-tuple-element.24), channel_id=1, source_target_pairs={{1,15},{3,13},{5,11},{7,9},{9,7},{11,5},{13,3},{15,1},{0,6},{2,4},... | collective-permute-start | bytes 233480 | tf_op jit(solution)/shard_map/ppermute | solution.py:363
  10.0 5.0 %collective-permute-start.3 = (bf16[152,256]{1,0:T(8,128)(2,1)S(1)}, bf16[152,256]{1,0:T(8,128)(2,1)S(1)}, u32[]{:S(2)}, u32[]{:S(2)}) collective-permute-start(bf16[152,256]{1,0:T(8,128)(2,1)S(1)} %get-tuple-element.25), channel_id=1, source_target_pairs={{1,13},{3,15},{5,9},{7,11},{9,5},{11,7},{13,1},{15,3},{0,2},{2,0},... | collective-permute-start | bytes 233480 | tf_op jit(solution)/shard_map/ppermute | solution.py:363
  11.0 6.9 %collective-permute-start.7 = (bf16[152,256]{1,0:T(8,128)(2,1)S(1)}, bf16[152,256]{1,0:T(8,128)(2,1)S(1)}, u32[]{:S(2)}, u32[]{:S(2)}) collective-permute-start(bf16[152,256]{1,0:T(8,128)(2,1)S(1)} %get-tuple-element.30), channel_id=1, source_target_pairs={{1,11},{3,9},{5,15},{7,13},{9,3},{11,1},{13,7},{15,5},{17,27},{19,... | collective-permute-start | bytes 233480 | tf_op jit(solution)/shard_map/ppermute | solution.py:363
  13.4 6.7 %collective-permute-start.4 = (bf16[152,256]{1,0:T(8,128)(2,1)S(1)}, bf16[152,256]{1,0:T(8,128)(2,1)S(1)}, u32[]{:S(2)}, u32[]{:S(2)}) collective-permute-start(bf16[152,256]{1,0:T(8,128)(2,1)S(1)} %collective-permute-done.1.refs_1_), channel_id=1, source_target_pairs={{1,0},{3,2},{5,4},{7,6},{9,8},{11,10},{13,12},{15,14},{0,1},{2,3},... | collective-permute-start | bytes 233480 | tf_op jit(solution)/shard_map/ppermute | solution.py:364
  13.6 6.4 %collective-permute-start.5 = (bf16[152,256]{1,0:T(8,128)(2,1)S(1)}, bf16[152,256]{1,0:T(8,128)(2,1)S(1)}, u32[]{:S(2)}, u32[]{:S(2)}) collective-permute-start(bf16[152,256]{1,0:T(8,128)(2,1)S(1)} %collective-permute-done.2.refs_2_), channel_id=1, source_target_pairs={{1,0},{3,2},{5,4},{7,6},{9,8},{11,10},{13,12},{15,14},{0,1},{2,3},... | collective-permute-start | bytes 233480 | tf_op jit(solution)/shard_map/ppermute | solution.py:364
  15.0 6.6 %collective-permute-start.6 = (bf16[152,256]{1,0:T(8,128)(2,1)S(1)}, bf16[152,256]{1,0:T(8,128)(2,1)S(1)}, u32[]{:S(2)}, u32[]{:S(2)}) collective-permute-start(bf16[152,256]{1,0:T(8,128)(2,1)S(1)} %collective-permute-done.3.refs_3_), channel_id=1, source_target_pairs={{1,0},{3,2},{5,4},{7,6},{9,8},{11,10},{13,12},{15,14},{0,1},{2,3},... | collective-permute-start | bytes 233480 | tf_op jit(solution)/shard_map/ppermute | solution.py:364
  18.0 4.3 %collective-permute-start.8 = (bf16[152,256]{1,0:T(8,128)(2,1)S(1)}, bf16[152,256]{1,0:T(8,128)(2,1)S(1)}, u32[]{:S(2)}, u32[]{:S(2)}) collective-permute-start(bf16[152,256]{1,0:T(8,128)(2,1)S(1)} %collective-permute-done.7.north_ref), channel_id=1, source_target_pairs={{1,0},{3,2},{5,4},{7,6},{9,8},{11,10},{13,12},{15,14},{17,16},{19,... | collective-permute-start | bytes 233480 | tf_op jit(solution)/shard_map/ppermute | solution.py:364

commit v4 on v3

--- a/solution.py
+++ b/solution.py
@@ -93,12 +93,14 @@
     for copy in small:
         copy.wait()
     turned = (((0,), (0,)), ((), ()))
-    wr_rep = lax.dot_general(
-        wr_ref[...], pick_r.astype(BF16), turned, preferred_element_type=F32
+    weights = jnp.concatenate(
+        [
+            lax.dot_general(ref[...], pick.astype(BF16), turned, preferred_element_type=F32)
+            for ref, pick in ((wr_ref, pick_r), (wl_ref, pick_l))
+        ],
+        axis=1,
     ).astype(BF16)
-    wl_rep = lax.dot_general(
-        wl_ref[...], pick_l.astype(BF16), turned, preferred_element_type=F32
-    ).astype(BF16)
+    weights = jnp.concatenate([weights, weights], axis=0)
     rb_rep = jnp.dot(jnp.broadcast_to(rb_ref[...], (8, channels)), pick_r, **exact)[0:1]
     lb_rep = jnp.dot(jnp.broadcast_to(lb_ref[...], (8, channels)), pick_l, **exact)[0:1]
     crop = _column(crop_ref[...].astype(F32))
@@ -113,22 +115,22 @@
         flag_r = jnp.where(seq_r == s, flag, flag_r)
         flag_l = jnp.where(seq_l == s, flag, flag_l)
         flag_row = jnp.where(lane - first == s, flag, flag_row)
+    for copy in loads:
+        copy.wait()
+    rows = []
     for s in range(seqs):
-        loads[s].wait()
         values = x_ref[s].astype(F32)
         values = values - jnp.mean(values, axis=-1, keepdims=True)
         variance = jnp.mean(values * values, axis=-1, keepdims=True)
         normed = values * lax.rsqrt(variance + 1e-05) * gain_ref[...] + shift_ref[...]
         high = normed.astype(BF16)
         low = (normed - high.astype(F32)).astype(BF16)
-        to_right = jnp.dot(high, wr_rep, preferred_element_type=F32) + jnp.dot(
-            low, wr_rep, preferred_element_type=F32
-        )
-        to_left = jnp.dot(high, wl_rep, preferred_element_type=F32) + jnp.dot(
-            low, wl_rep, preferred_element_type=F32
-        )
-        right = jnp.where(seq_r == s, to_right, right)
-        left = jnp.where(seq_l == s, to_left, left)
+        rows.append(jnp.concatenate([high, low], axis=1))
+    product = jnp.dot(jnp.concatenate(rows, axis=0), weights, preferred_element_type=F32)
+    for s in range(seqs):
+        part = product[s * residues : (s + 1) * residues]
+        right = jnp.where(seq_r == s, part[:, :lanes], right)
+        left = jnp.where(seq_l == s, part[:, lanes:], left)
     out_ref[0:residues] = ((right + rb_rep) * (flag_r * crop)).astype(BF16)
     out_ref[residues : 2 * residues] = ((left + lb_rep) * (flag_l * crop)).astype(BF16)
     rows = _iota((2 * FLAG_ROWS, lanes), 0)
@@ -137,44 +139,34 @@
 
 def _pack_kernel(steps, rows_chip, own_ref, other_ref, *out_refs):
     residues = own_ref.shape[0] // 2 - FLAG_ROWS
-    total = rows_chip + FLAG_ROWS
+    half, rows_here = residues // 2, rows_chip // 2
     index = lax.axis_index("row")
     chip, core = index // 2, index % 2
     right = own_ref[0:residues] + other_ref[0:residues]
-    flags = own_ref[2 * residues :] + other_ref[2 * residues :]
+    flags = (own_ref[2 * residues :] + other_ref[2 * residues :]).astype(F32)[:FLAG_ROWS]
     for out_ref, (far, near) in zip(out_refs, ((0, 0),) + steps):
         target = chip ^ jnp.where(core == 1, far, near)
         start = pl.multiple_of(residues + target * rows_chip, rows_chip)
-        out_ref[0:residues] = right
         slab = own_ref[pl.ds(start, rows_chip)] + other_ref[pl.ds(start, rows_chip)]
-        tail = jnp.concatenate([slab.astype(F32), flags.astype(F32)], axis=0)
-        out_ref[residues : residues + total] = tail[0:total].astype(BF16)
-
-
-def _read(slot, rows):
-    if not isinstance(slot, tuple):
-        return slot[rows]
-    north, south = slot
-    return jnp.where(lax.axis_index("row") % 2 == 1, north[rows], south[rows])
-
-
-def _rows(slot):
-    return (slot[0] if isinstance(slot, tuple) else slot).shape
-
-
-def _spread(slots, w_ref, a_ref):
+        slab = slab.astype(F32)
+        if out_ref.shape[0] > residues:
+            out_ref[0:residues] = right
+            out_ref[residues:] = jnp.concatenate([slab, flags], axis=0).astype(BF16)
+        else:
+            out_ref[0:half] = jnp.where(core == 1, right[:half], right[half:])
+            slab = jnp.where(core == 1, slab[rows_here:], slab[:rows_here])
+            out_ref[half:] = jnp.concatenate([slab, flags], axis=0).astype(BF16)
+
+
+def _spread(slabs, w_ref, targets):
     channels = w_ref.shape[0]
-    height, lanes = _rows(slots[0])
+    rows_here, lanes = slabs[0].shape
     pair = lanes // channels
     width = w_ref.shape[1] // channels
-    residues = height - 2 * pair - FLAG_ROWS
-    core = lax.axis_index("row") % 2
     mine = _iota((pair, lanes), 1) // channels == _iota((pair, lanes), 0)
     rows = []
-    for slot in slots:
-        slab = _read(slot, slice(residues, residues + 2 * pair)).astype(F32)
-        slab = jnp.where(core == 1, slab[pair:], slab[:pair])
-        for i in range(pair):
+    for slab in slabs:
+        for i in range(rows_here):
             rows.append(jnp.where(mine, jnp.broadcast_to(slab[i : i + 1], (pair, lanes)), 0.0))
     spread = jnp.concatenate(rows, axis=0).astype(BF16)
     for e in range(0, channels, 2):
@@ -182,36 +174,38 @@
         product = jnp.dot(
             spread, jnp.concatenate([block] * pair, axis=0), preferred_element_type=F32
         )
-        for n in range(len(slots)):
-            for i in range(pair):
-                at = (n * pair + i) * pair
+        for n, (a_ref, base) in enumerate(targets):
+            for i in range(rows_here):
+                at = (n * rows_here + i) * pair
                 both = jnp.concatenate(
                     [product[at : at + pair, :width], product[at : at + pair, width:]], axis=0
                 )
                 a_ref[
-                    n * lanes + e * pair : n * lanes + (e + 2) * pair,
-                    i * width : (i + 1) * width,
+                    base + e * pair : base + (e + 2) * pair, i * width : (i + 1) * width
                 ] = both.astype(BF16)
 
 
-def _contract(slots, a_ref, residues, columns=slice(None)):
-    lanes = _rows(slots[0])[1]
+def _slab(ref, residues):
+    both = ref[residues : ref.shape[0] - FLAG_ROWS].astype(F32)
+    half = both.shape[0] // 2
+    return jnp.where(lax.axis_index("row") % 2 == 1, both[half:], both[:half])
+
+
+def _contract(refs, a_ref, residues):
+    lanes = refs[0].shape[1]
     total = None
-    for n, slot in enumerate(slots):
+    for n, ref in enumerate(refs):
         part = jnp.dot(
-            _read(slot, slice(0, residues)),
-            a_ref[n * lanes : (n + 1) * lanes, columns],
-            preferred_element_type=F32,
+            ref[0:residues], a_ref[n * lanes : (n + 1) * lanes], preferred_element_type=F32
         )
         total = part if total is None else total + part
     return total
 
 
-def _live(slots):
+def _flags(refs):
     total = None
-    for slot in slots:
-        rows = _rows(slot)[0]
-        part = _read(slot, slice(rows - 2 * FLAG_ROWS, rows)).astype(F32)[FLAG_ROWS:]
+    for ref in refs:
+        part = ref[ref.shape[0] - 2 * FLAG_ROWS :].astype(F32)[FLAG_ROWS:]
         total = part if total is None else total + part
     return total
 
@@ -241,44 +235,54 @@
     own_ref[...] = jnp.broadcast_to(jnp.sum(kept, axis=1, keepdims=True), own_ref.shape)
 
 
-def _first_kernel(count, w_ref, *refs):
-    slots, (sum_ref, live_ref, a_ref) = refs[:count], refs[count:]
-    _spread(slots, w_ref, a_ref)
-    sum_ref[...] = _contract(slots, a_ref, sum_ref.shape[0])
-    live_ref[...] = _live(slots)
-
-
-def _more_kernel(count, w_ref, sum_in, live_in, *refs):
-    slots, (sum_ref, live_ref, a_ref) = refs[:count], refs[count:]
-    _spread(slots, w_ref, a_ref)
-    sum_ref[...] = sum_in[...] + _contract(slots, a_ref, sum_ref.shape[0])
-    live_ref[...] = live_in[...] + _live(slots)
+def _early_kernel(count, w_ref, *refs):
+    parcels, (sum_ref, flags_ref, a_ref) = refs[:count], refs[count:]
+    residues, lanes = sum_ref.shape[0], parcels[0].shape[1]
+    slabs = [_slab(ref, residues) for ref in parcels]
+    _spread(slabs, w_ref, [(a_ref, n * lanes) for n in range(count)])
+    sum_ref[...] = _contract(parcels, a_ref, residues)
+    flags_ref[...] = _flags(parcels)
+
+
+def _late_kernel(count, w_ref, sum_in, flags_in, shared_ref, *refs):
+    parcels, (sum_ref, flags_ref, shared_a_ref, a_ref) = refs[:count], refs[count:]
+    residues, lanes = sum_ref.shape[0], parcels[0].shape[1]
+    slabs = [_slab(ref, residues) for ref in parcels]
+    slabs.append(shared_ref[residues // 2 :].astype(F32)[:-FLAG_ROWS])
+    targets = [(a_ref, n * lanes) for n in range(count)] + [(shared_a_ref, 0)]
+    _spread(slabs, w_ref, targets)
+    sum_ref[...] = sum_in[...] + _contract(parcels, a_ref, residues)
+    flags_ref[...] = flags_in[...] + _flags(parcels + (shared_ref,))
 
 
 def _last_kernel(
-    w_ref,
     column_ref,
     own_ref,
     bias_ref,
     sum_in,
-    live_in,
-    north_ref,
-    south_ref,
+    flags_in,
+    a_ref,
+    mine_ref,
+    other_ref,
     out_hbm,
-    a_ref,
     out_ref,
     sems,
 ):
-    slots = [(north_ref, south_ref)]
-    rows_here, _, width = out_ref.shape
-    flags = live_in[...] + _live(slots)
-    live = jnp.sum(jnp.sum(flags, axis=1, keepdims=True), axis=0, keepdims=True)
-    _spread(slots, w_ref, a_ref)
+    rows_here, residues, width = out_ref.shape
+    half = residues // 2
+    core = lax.axis_index("row") % 2
+    mine, other = mine_ref[0:half], other_ref[0:half]
+    right = jnp.concatenate(
+        [jnp.where(core == 1, mine, other), jnp.where(core == 1, other, mine)], axis=0
+    )
+    live = jnp.sum(jnp.sum(flags_in[...], axis=1, keepdims=True), axis=0, keepdims=True)
     stores = []
     group = 2 if rows_here % 2 == 0 else 1
     for first in range(0, rows_here, group):
         columns = slice(first * width, (first + group) * width)
-        projected = sum_in[:, columns] + _contract(slots, a_ref, sum_in.shape[0], columns)
+        projected = sum_in[:, columns] + jnp.dot(
+            right, a_ref[:, columns], preferred_element_type=F32
+        )
         for i in range(first, first + group):
             divisor = jnp.maximum(live * own_ref[i : i + 1] * column_ref[...], 1.0)
             part = projected[:, (i - first) * width : (i - first + 1) * width]
@@ -314,7 +318,7 @@
     steps = tuple(
         zip(
             [quarter] + [k for k in range(chips - 1, half, -1) if k != quarter],
-            [k for k in range(half, 0, -1) if k != quarter] + [0],
+            [k for k in range(half, 0, -1) if k != quarter] + [half + 1],
         )
     )
     cores = [(d, d ^ 1) for d in range(devices)]
@@ -345,9 +349,10 @@
     )(*map(_stay, operands))
     other = lax.ppermute(projected, "row", cores)
     parcel = jax.ShapeDtypeStruct((residues + rows_chip + FLAG_ROWS, lanes), BF16)
+    shared = jax.ShapeDtypeStruct((residues // 2 + rows_here + FLAG_ROWS, lanes), BF16)
     own, *parcels = pl.pallas_call(
         functools.partial(_pack_kernel, steps, rows_chip),
-        out_shape=[parcel] * (1 + len(steps)),
+        out_shape=[parcel] * len(steps) + [shared],
         in_specs=_vmem(2),
         out_specs=_vmem(1 + len(steps)),
         compiler_params=limit,
@@ -356,12 +361,9 @@
     received, handed = [], []
     for (far, near), piece in zip(steps, parcels):
         pairs = [(2 * q + 1, 2 * (q ^ far) + 1) for q in range(chips)]
-        back = [(2 * q + 1, 2 * q) for q in range(chips)]
-        if near:
-            pairs += [(2 * q, 2 * (q ^ near)) for q in range(chips)]
-            back += [(2 * q, 2 * q + 1) for q in range(chips)]
+        pairs += [(2 * q, 2 * (q ^ near)) for q in range(chips)]
         received.append(lax.ppermute(piece, "row", pairs))
-        handed.append(lax.ppermute(received[-1], "row", back))
+        handed.append(lax.ppermute(received[-1], "row", cores))
 
     columns = rows_here * width
     state = [
@@ -387,10 +389,9 @@
         name="prepare",
     )(out_weight, _stay(crop), _stay(out_bias.reshape(1, -1)))
 
-    middle = len(steps) // 2
-    early = [own] + received[:-1] + handed[:middle]
+    early = [own] + received[:-1]
     carry = pl.pallas_call(
-        functools.partial(_first_kernel, len(early)),
+        functools.partial(_early_kernel, len(early)),
         out_shape=state,
         in_specs=_vmem(1 + len(early)),
         out_specs=_vmem(2),
@@ -398,16 +399,16 @@
         compiler_params=limit,
         name="early",
     )(weight, *early)
-    late = handed[middle:-1]
+    late = handed[:-1]
     carry = pl.pallas_call(
-        functools.partial(_more_kernel, len(late)),
-        out_shape=state,
-        in_specs=_vmem(3 + len(late)),
-        out_specs=_vmem(2),
+        functools.partial(_late_kernel, len(late)),
+        out_shape=state + [jax.ShapeDtypeStruct((lanes, columns), BF16)],
+        in_specs=_vmem(4 + len(late)),
+        out_specs=_vmem(3),
         scratch_shapes=[pltpu.VMEM((len(late) * lanes, columns), BF16)],
         compiler_params=limit,
         name="late",
-    )(weight, *carry, *late)
+    )(weight, *carry, received[-1], *late)
     tile = (rows_here, residues, width)
     return pl.pallas_call(
         _last_kernel,
@@ -415,13 +416,12 @@
         in_specs=_vmem(8),
         out_specs=anywhere,
         scratch_shapes=[
-            pltpu.VMEM((lanes, columns), BF16),
             pltpu.VMEM(tile, BF16),
             pltpu.SemaphoreType.DMA((rows_here,)),
         ],
         compiler_params=limit,
         name="last",
-    )(weight, *spread, *carry, received[-1], handed[-1])
+    )(*spread, *carry, received[-1], handed[-1])
 
 
 def solution(mesh):

time: 23.9 us -> 21.4 us (0.90)
  the two profiles are of different devices: /device:TPU:1 before, /device:TPU:0 now
where the time goes in v4:
time: 21.4 us; the launch traced here: 21.3 us
  starting transfers between devices  9.2 us (43%)
  waiting for transfers between devices  6.07 us (28%)
  Pallas kernels  5.91 us (28%)
    ppermute x4, starting transfers between devices, per_device(): received.append(lax.ppermute(piece, 'row', pairs))  8.33 us
    ppermute x4, waiting for transfers between devices, per_device(): received.append(lax.ppermute(piece, 'row', pairs))  5.06 us
    pallas_call x1, Pallas kernels, per_device(): pl.pallas_call(_project_kernel, out_shape=jax.ShapeDtypeStruct((2 * resid...  2 us
    pallas_call x1, Pallas kernels, per_device(): pl.pallas_call(functools.partial(_early_kernel, len(early)), out_shape=st...  1.1 us
    pallas_call x1, Pallas kernels, per_device(): pl.pallas_call(functools.partial(_late_kernel, len(late)), out_shape=stat...  1.03 us
    ppermute x1, waiting for transfers between devices, per_device(): other = lax.ppermute(projected, 'row', cores)  1 us
    pallas_call x1, Pallas kernels, per_device(): pl.pallas_call(_last_kernel, out_shape=jax.ShapeDtypeStruct(tile, BF16),...  0.97 us
    pallas_call x1, Pallas kernels, per_device(): pl.pallas_call(functools.partial(_prepare_kernel, channels), out_shape=[j...  0.78 us
  transfers between devices with their start and end apart: 9, of which 4 were waited for; matrix products, arithmetic and copies ran while one was open for 0% of the time, Pallas kernels for 14%

profile of v4, /device:TPU:0, one launch (start us, length us, event | category | flops | bytes accessed | tf_op | source)
XLA Modules:
  0.0 21.3 jit_solution(6697473074860206689)
XLA Ops:
  0.0 0.0 copy-start
  0.0 2.0 %project.1.own_ref = bf16[272,256]{1,0:T(8,128)(2,1)S(1)} custom-call(bf16[4,128,256]{2,1,0:T(8,128)(2,1)} %x_hbm.1, s32[1,4]{1,0:T(1,128)} %bitcast.15, s32[1,128]{1,0:T(1,128)} %bitcast.11, f32[1,256]{1,0:T(1,128)} %bitcast.13, f32[1,256]{1,0:T(1,128)} %bitcast.14, bf16[32,256]{1,0:T(8,128)(2,1)} %bitcast.9, bf16[32,256]{1,0:T(8,128)(2,1)} %bitcast.10, ...), custom_call_target="tpu_custom_call" | custom-call | tf_op jit(solution)/shard_map/project/pallas_call | solution.py:340
  2.0 0.6 %collective-permute-start = (bf16[272,256]{1,0:T(8,128)(2,1)S(1)}, bf16[272,256]{1,0:T(8,128)(2,1)S(1)}, u32[]{:S(2)}, u32[]{:S(2)}) collective-permute-start(bf16[272,256]{1,0:T(8,128)(2,1)S(1)} %project.1.own_ref), channel_id=1, source_target_pairs={{0,1},{1,0},{2,3},{3,2},{4,5},{5,4},{6,7},{7,6},{8,9},{9,8},{10,11... | collective-permute-start | bytes 417800 | tf_op jit(solution)/shard_map/ppermute | solution.py:350
  2.6 1.0 %collective-permute-done.other_ref = bf16[272,256]{1,0:T(8,128)(2,1)S(1)} collective-permute-done((bf16[272,256]{1,0:T(8,128)(2,1)S(1)}, bf16[272,256]{1,0:T(8,128)(2,1)S(1)}, u32[]{:S(2)}, u32[]{:S(2)}) %collective-permute-start) | collective-permute-done | bytes 139296 | tf_op jit(solution)/shard_map/ppermute | solution.py:350
  3.6 4.0 %collective-permute-start.1 = (bf16[152,256]{1,0:T(8,128)(2,1)S(1)}, bf16[152,256]{1,0:T(8,128)(2,1)S(1)}, u32[]{:S(2)}, u32[]{:S(2)}) collective-permute-start(bf16[152,256]{1,0:T(8,128)(2,1)S(1)} %get-tuple-element.24), channel_id=1, source_target_pairs={{1,5},{3,7},{5,1},{7,3},{9,13},{11,15},{13,9},{15,11},{0,8},{2,10}... | collective-permute-start | bytes 233480 | tf_op jit(solution)/shard_map/ppermute | solution.py:365
  7.6 2.5 %collective-permute-start.2 = (bf16[152,256]{1,0:T(8,128)(2,1)S(1)}, bf16[152,256]{1,0:T(8,128)(2,1)S(1)}, u32[]{:S(2)}, u32[]{:S(2)}) collective-permute-start(bf16[152,256]{1,0:T(8,128)(2,1)S(1)} %get-tuple-element.25), channel_id=1, source_target_pairs={{1,15},{3,13},{5,11},{7,9},{9,7},{11,5},{13,3},{15,1},{0,6},{2,4},... | collective-permute-start | bytes 233480 | tf_op jit(solution)/shard_map/ppermute | solution.py:365
  10.1 0.5 %collective-permute-start.3 = (bf16[152,256]{1,0:T(8,128)(2,1)S(1)}, bf16[152,256]{1,0:T(8,128)(2,1)S(1)}, u32[]{:S(2)}, u32[]{:S(2)}) collective-permute-start(bf16[152,256]{1,0:T(8,128)(2,1)S(1)} %get-tuple-element.26), channel_id=1, source_target_pairs={{1,13},{3,15},{5,9},{7,11},{9,5},{11,7},{13,1},{15,3},{0,2},{2,0},... | collective-permute-start | bytes 233480 | tf_op jit(solution)/shard_map/ppermute | solution.py:365
  10.6 1.3 %collective-permute-start.4 = (bf16[80,256]{1,0:T(8,128)(2,1)S(1)}, bf16[80,256]{1,0:T(8,128)(2,1)S(1)}, u32[]{:S(2)}, u32[]{:S(2)}) collective-permute-start(bf16[80,256]{1,0:T(8,128)(2,1)S(1)} %get-tuple-element.29), channel_id=1, source_target_pairs={{1,11},{3,9},{5,15},{7,13},{9,3},{11,1},{13,7},{15,5},{0,10},{2,8}... | collective-permute-start | bytes 122888 | tf_op jit(solution)/shard_map/ppermute | solution.py:365
  11.9 0.0 collective-permute-done.1.refs_1_
  11.9 0.0 collective-permute-start.5
  11.9 1.7 %collective-permute-done.2.refs_2_ = bf16[152,256]{1,0:T(8,128)(2,1)S(1)} collective-permute-done((bf16[152,256]{1,0:T(8,128)(2,1)S(1)}, bf16[152,256]{1,0:T(8,128)(2,1)S(1)}, u32[]{:S(2)}, u32[]{:S(2)}) %collective-permute-start.2) | collective-permute-done | bytes 77856 | tf_op jit(solution)/shard_map/ppermute | solution.py:365
  13.6 0.0 collective-permute-start.6
  13.6 0.9 %collective-permute-done.3.refs_3_ = bf16[152,256]{1,0:T(8,128)(2,1)S(1)} collective-permute-done((bf16[152,256]{1,0:T(8,128)(2,1)S(1)}, bf16[152,256]{1,0:T(8,128)(2,1)S(1)}, u32[]{:S(2)}, u32[]{:S(2)}) %collective-permute-start.3) | collective-permute-done | bytes 77856 | tf_op jit(solution)/shard_map/ppermute | solution.py:365
  14.5 0.2 collective-permute-start.7
  14.7 2.5 %collective-permute-done.4.shared_ref.mine_ref = bf16[80,256]{1,0:T(8,128)(2,1)S(1)} collective-permute-done((bf16[80,256]{1,0:T(8,128)(2,1)S(1)}, bf16[80,256]{1,0:T(8,128)(2,1)S(1)}, u32[]{:S(2)}, u32[]{:S(2)}) %collective-permute-start.4) | collective-permute-done | bytes 40992 | tf_op jit(solution)/shard_map/ppermute | solution.py:365
  17.2 0.1 collective-permute-start.8
  17.3 0.0 copy-done
  17.3 0.8 %prepare.1 = (bf16[32,4096]{1,0:T(8,128)(2,1)S(1)}, f32[128,128]{1,0:T(8,128)S(1)}, f32[8,128]{1,0:T(8,128)S(1)}, f32[1,128]{1,0:T(1,128)S(1)}) custom-call(bf16[1024,128]{1,0:T(8,128)(2,1)S(1)} %copy-done, s32[1,128]{1,0:T(1,128)} %bitcast.12, f32[1,128]{1,0:T(1,128)} %bitcast.18), custom_call_target="tpu_custom_call" | custom-call | tf_op jit(solution)/shard_map/prepare/pallas_call | solution.py:373
  18.1 1.1 %early.1 = (f32[128,1024]{1,0:T(8,128)S(1)}, f32[8,256]{1,0:T(8,128)S(1)}) custom-call(bf16[32,4096]{1,0:T(8,128)(2,1)S(1)} %get-tuple-element.22.w_ref, bf16[152,256]{1,0:T(8,128)(2,1)S(1)} %get-tuple-element.23.refs_0_, bf16[152,256]{1,0:T(8,128)(2,1)S(1)} %collective-permute-done.1.refs_1_, bf16[152,256]{1,0:T(8,128)(2,1)S(1)} %collective-permute-done.2.refs_2_, ...), custom_call_target="tpu_custom_call" | custom-call | tf_op jit(solution)/shard_map/early/pallas_call | solution.py:393
  19.2 0.0 collective-permute-done.5.refs_0_
  19.2 0.0 collective-permute-done.6.refs_1_
  19.2 0.0 collective-permute-done.7.refs_2_
  19.2 1.0 %late.1 = (f32[128,1024]{1,0:T(8,128)S(1)}, f32[8,256]{1,0:T(8,128)S(1)}, bf16[256,1024]{1,0:T(8,128)(2,1)S(1)}) custom-call(bf16[32,4096]{1,0:T(8,128)(2,1)S(1)} %get-tuple-element.22.w_ref, f32[128,1024]{1,0:T(8,128)S(1)} %get-tuple-element.27.sum_in, f32[8,256]{1,0:T(8,128)S(1)} %get-tuple-element.28.flags_in, ...), custom_call_target="tpu_custom_call" | custom-call | tf_op jit(solution)/shard_map/late/pallas_call | solution.py:403
  20.3 0.0 collective-permute-done.8.other_ref
  20.3 1.0 %last.1 = bf16[8,128,128]{2,1,0:T(8,128)(2,1)} custom-call(f32[128,128]{1,0:T(8,128)S(1)} %get-tuple-element.19.column_ref, f32[8,128]{1,0:T(8,128)S(1)} %get-tuple-element.20.own_ref, f32[1,128]{1,0:T(1,128)S(1)} %get-tuple-element.21.bias_ref, f32[128,1024]{1,0:T(8,128)S(1)} %get-tuple-element.30.sum_in, f32[8,256]{1,0:T(8,128)S(1)} %get-tuple-element.31.flags_in, ...), custom_call_target="tpu_custom_call" | custom-call | tf_op jit(solution)/shard_map/last/pallas_call | solution.py:413
  (1 shorter events, 0.0 us)
Async XLA Ops:
  0.0 17.3 %copy-start = (bf16[1024,128]{1,0:T(8,128)(2,1)S(1)}, bf16[1024,128]{1,0:T(8,128)(2,1)}, u32[]{:S(2)}) copy-start(bf16[1024,128]{1,0:T(8,128)(2,1)} %raw_ref.1) | copy-start | bytes 786436
  2.0 1.6 %collective-permute-start = (bf16[272,256]{1,0:T(8,128)(2,1)S(1)}, bf16[272,256]{1,0:T(8,128)(2,1)S(1)}, u32[]{:S(2)}, u32[]{:S(2)}) collective-permute-start(bf16[272,256]{1,0:T(8,128)(2,1)S(1)} %project.1.own_ref), channel_id=1, source_target_pairs={{0,1},{1,0},{2,3},{3,2},{4,5},{5,4},{6,7},{7,6},{8,9},{9,8},{10,11... | collective-permute-start | bytes 417800 | tf_op jit(solution)/shard_map/ppermute | solution.py:350
  3.6 8.3 %collective-permute-start.1 = (bf16[152,256]{1,0:T(8,128)(2,1)S(1)}, bf16[152,256]{1,0:T(8,128)(2,1)S(1)}, u32[]{:S(2)}, u32[]{:S(2)}) collective-permute-start(bf16[152,256]{1,0:T(8,128)(2,1)S(1)} %get-tuple-element.24), channel_id=1, source_target_pairs={{1,5},{3,7},{5,1},{7,3},{9,13},{11,15},{13,9},{15,11},{0,8},{2,10}... | collective-permute-start | bytes 233480 | tf_op jit(solution)/shard_map/ppermute | solution.py:365
  7.6 6.0 %collective-permute-start.2 = (bf16[152,256]{1,0:T(8,128)(2,1)S(1)}, bf16[152,256]{1,0:T(8,128)(2,1)S(1)}, u32[]{:S(2)}, u32[]{:S(2)}) collective-permute-start(bf16[152,256]{1,0:T(8,128)(2,1)S(1)} %get-tuple-element.25), channel_id=1, source_target_pairs={{1,15},{3,13},{5,11},{7,9},{9,7},{11,5},{13,3},{15,1},{0,6},{2,4},... | collective-permute-start | bytes 233480 | tf_op jit(solution)/shard_map/ppermute | solution.py:365
  10.1 4.4 %collective-permute-start.3 = (bf16[152,256]{1,0:T(8,128)(2,1)S(1)}, bf16[152,256]{1,0:T(8,128)(2,1)S(1)}, u32[]{:S(2)}, u32[]{:S(2)}) collective-permute-start(bf16[152,256]{1,0:T(8,128)(2,1)S(1)} %get-tuple-element.26), channel_id=1, source_target_pairs={{1,13},{3,15},{5,9},{7,11},{9,5},{11,7},{13,1},{15,3},{0,2},{2,0},... | collective-permute-start | bytes 233480 | tf_op jit(solution)/shard_map/ppermute | solution.py:365
  10.6 6.6 %collective-permute-start.4 = (bf16[80,256]{1,0:T(8,128)(2,1)S(1)}, bf16[80,256]{1,0:T(8,128)(2,1)S(1)}, u32[]{:S(2)}, u32[]{:S(2)}) collective-permute-start(bf16[80,256]{1,0:T(8,128)(2,1)S(1)} %get-tuple-element.29), channel_id=1, source_target_pairs={{1,11},{3,9},{5,15},{7,13},{9,3},{11,1},{13,7},{15,5},{0,10},{2,8}... | collective-permute-start | bytes 122888 | tf_op jit(solution)/shard_map/ppermute | solution.py:365
  11.9 7.3 %collective-permute-start.5 = (bf16[152,256]{1,0:T(8,128)(2,1)S(1)}, bf16[152,256]{1,0:T(8,128)(2,1)S(1)}, u32[]{:S(2)}, u32[]{:S(2)}) collective-permute-start(bf16[152,256]{1,0:T(8,128)(2,1)S(1)} %collective-permute-done.1.refs_1_), channel_id=1, source_target_pairs={{0,1},{1,0},{2,3},{3,2},{4,5},{5,4},{6,7},{7,6},{8,9},{9,8},{10,11... | collective-permute-start | bytes 233480 | tf_op jit(solution)/shard_map/ppermute | solution.py:366
  13.6 5.6 %collective-permute-start.6 = (bf16[152,256]{1,0:T(8,128)(2,1)S(1)}, bf16[152,256]{1,0:T(8,128)(2,1)S(1)}, u32[]{:S(2)}, u32[]{:S(2)}) collective-permute-start(bf16[152,256]{1,0:T(8,128)(2,1)S(1)} %collective-permute-done.2.refs_2_), channel_id=1, source_target_pairs={{0,1},{1,0},{2,3},{3,2},{4,5},{5,4},{6,7},{7,6},{8,9},{9,8},{10,11... | collective-permute-start | bytes 233480 | tf_op jit(solution)/shard_map/ppermute | solution.py:366
  14.5 4.7 %collective-permute-start.7 = (bf16[152,256]{1,0:T(8,128)(2,1)S(1)}, bf16[152,256]{1,0:T(8,128)(2,1)S(1)}, u32[]{:S(2)}, u32[]{:S(2)}) collective-permute-start(bf16[152,256]{1,0:T(8,128)(2,1)S(1)} %collective-permute-done.3.refs_3_), channel_id=1, source_target_pairs={{0,1},{1,0},{2,3},{3,2},{4,5},{5,4},{6,7},{7,6},{8,9},{9,8},{10,11... | collective-permute-start | bytes 233480 | tf_op jit(solution)/shard_map/ppermute | solution.py:366
  17.2 3.1 %collective-permute-start.8 = (bf16[80,256]{1,0:T(8,128)(2,1)S(1)}, bf16[80,256]{1,0:T(8,128)(2,1)S(1)}, u32[]{:S(2)}, u32[]{:S(2)}) collective-permute-start(bf16[80,256]{1,0:T(8,128)(2,1)S(1)} %collective-permute-done.4.shared_ref.mine_ref), channel_id=1, source_target_pairs={{0,1},{1,0},{2,3},{3,2},{4,5},{5,4},{6,7},{7,6},{8,9},{9,8},{10,11... | collective-permute-start | bytes 122888 | tf_op jit(solution)/shard_map/ppermute | solution.py:366

commit v5 on v4

--- a/solution.py
+++ b/solution.py
@@ -24,6 +24,14 @@
         _iota(square, 0) == _iota(square, 1), jnp.broadcast_to(row, square), 0.0
     )
     return jnp.sum(picked, axis=1, keepdims=True)
+
+
+def _pick_lanes(row, pick):
+    high = row.astype(BF16).astype(F32)
+    middle = (row - high).astype(BF16).astype(F32)
+    parts = jnp.concatenate([high, middle, row - high - middle, jnp.zeros_like(row)], axis=0)
+    parts = jnp.concatenate([parts, jnp.zeros_like(parts)], axis=0).astype(BF16)
+    return jnp.sum(jnp.dot(parts, pick, preferred_element_type=F32), axis=0, keepdims=True)
 
 
 def _stay(array):
@@ -75,7 +83,7 @@
         )
     ]
     loads = [
-        pltpu.make_async_copy(x_hbm.at[s], x_ref.at[s], x_sems.at[s]) for s in range(seqs)
+        pltpu.make_async_copy(x_hbm, x_ref, x_sems.at[0])
     ]
     for copy in small + loads:
         copy.start()
@@ -84,9 +92,8 @@
     first = (lax.axis_index("row") % 2) * seqs
     which = _iota((channels, lanes), 0)
     spread = _iota((channels, lanes), 1)
-    pick_r = jnp.where(spread // pair == which, 1.0, 0.0)
-    pick_l = jnp.where(spread % channels == which, 1.0, 0.0)
-    exact = dict(precision=lax.Precision.HIGHEST, preferred_element_type=F32)
+    pick_r = jnp.where(spread // pair == which, 1.0, 0.0).astype(BF16)
+    pick_l = jnp.where(spread % channels == which, 1.0, 0.0).astype(BF16)
     lane = _iota((1, lanes), 1)
     seq_r = lane % pair - first
     seq_l = lane // channels - first
@@ -95,14 +102,14 @@
     turned = (((0,), (0,)), ((), ()))
     weights = jnp.concatenate(
         [
-            lax.dot_general(ref[...], pick.astype(BF16), turned, preferred_element_type=F32)
+            lax.dot_general(ref[...], pick, turned, preferred_element_type=F32)
             for ref, pick in ((wr_ref, pick_r), (wl_ref, pick_l))
         ],
         axis=1,
     ).astype(BF16)
     weights = jnp.concatenate([weights, weights], axis=0)
-    rb_rep = jnp.dot(jnp.broadcast_to(rb_ref[...], (8, channels)), pick_r, **exact)[0:1]
-    lb_rep = jnp.dot(jnp.broadcast_to(lb_ref[...], (8, channels)), pick_l, **exact)[0:1]
+    rb_rep = _pick_lanes(rb_ref[...], pick_r)
+    lb_rep = _pick_lanes(lb_ref[...], pick_l)
     crop = _column(crop_ref[...].astype(F32))
     right = jnp.zeros((residues, lanes), F32)
     left = jnp.zeros((residues, lanes), F32)
@@ -276,6 +283,7 @@
         [jnp.where(core == 1, mine, other), jnp.where(core == 1, other, mine)], axis=0
     )
     live = jnp.sum(jnp.sum(flags_in[...], axis=1, keepdims=True), axis=0, keepdims=True)
+    inside = jnp.where(column_ref[...] > 0.0, 1.0 / jnp.maximum(live, 1.0), 1.0)
     stores = []
     group = 2 if rows_here % 2 == 0 else 1
     for first in range(0, rows_here, group):
@@ -284,9 +292,9 @@
             right, a_ref[:, columns], preferred_element_type=F32
         )
         for i in range(first, first + group):
-            divisor = jnp.maximum(live * own_ref[i : i + 1] * column_ref[...], 1.0)
+            scale = jnp.where(own_ref[i : i + 1] > 0.0, inside, 1.0)
             part = projected[:, (i - first) * width : (i - first + 1) * width]
-            out_ref[i] = (part / divisor + bias_ref[...]).astype(BF16)
+            out_ref[i] = (part * scale + bias_ref[...]).astype(BF16)
             stores.append(pltpu.make_async_copy(out_ref.at[i], out_hbm.at[i], sems.at[i]))
             stores[-1].start()
     for copy in stores:
@@ -314,13 +322,9 @@
     rows_chip = 2 * rows_here
     chips = devices // 2
     lanes = 2 * seqs * channels
-    half, quarter = chips // 2, max(1, chips // 4)
-    steps = tuple(
-        zip(
-            [quarter] + [k for k in range(chips - 1, half, -1) if k != quarter],
-            [k for k in range(half, 0, -1) if k != quarter] + [half + 1],
-        )
-    )
+    half = chips // 2
+    steps = [(k, k + 1) for k in range(chips - 2, 1, -2) if k != half]
+    steps = tuple(steps + [(half, 1), (half + 1, half + 1)])
     cores = [(d, d ^ 1) for d in range(devices)]
     crop = crop_flags.reshape(1, residues)
     limit = pltpu.CompilerParams(vmem_limit_bytes=48 * 1024 * 1024)
@@ -343,7 +347,7 @@
         in_specs=[anywhere] * len(operands),
         out_specs=_vmem(1)[0],
         scratch_shapes=[pltpu.VMEM(a.shape, a.dtype) for a in operands]
-        + [pltpu.SemaphoreType.DMA((seqs,)), pltpu.SemaphoreType.DMA((len(operands) - 1,))],
+        + [pltpu.SemaphoreType.DMA((1,)), pltpu.SemaphoreType.DMA((len(operands) - 1,))],
         compiler_params=limit,
         name="project",
     )(*map(_stay, operands))

time: 21.4 us -> 20.4 us (0.953)
  waiting for transfers between devices: 6.07 us -> 5.2 us
    ppermute x4, waiting for transfers between devices: 5.06 us -> 4.19 us  [per_device(): received.append(lax.ppermute(piece, 'row', pairs))]
    ppermute x4, starting transfers between devices: 8.33 us -> 8.07 us  [per_device(): received.append(lax.ppermute(piece, 'row', pairs))]
where the time goes in v5:
time: 20.4 us; the launch traced here: 20.2 us
  starting transfers between devices  9.15 us (45%)
  Pallas kernels  5.77 us (28%)
  waiting for transfers between devices  5.2 us (25%)
    ppermute x4, starting transfers between devices, per_device(): received.append(lax.ppermute(piece, 'row', pairs))  8.07 us
    ppermute x4, waiting for transfers between devices, per_device(): received.append(lax.ppermute(piece, 'row', pairs))  4.19 us
    pallas_call x1, Pallas kernels, per_device(): pl.pallas_call(_project_kernel, out_shape=jax.ShapeDtypeStruct((2 * resid...  1.87 us
    pallas_call x1, Pallas kernels, per_device(): pl.pallas_call(functools.partial(_early_kernel, len(early)), out_shape=st...  1.1 us
    pallas_call x1, Pallas kernels, per_device(): pl.pallas_call(functools.partial(_late_kernel, len(late)), out_shape=stat...  1.03 us
    ppermute x1, waiting for transfers between devices, per_device(): other = lax.ppermute(projected, 'row', cores)  1 us
    pallas_call x1, Pallas kernels, per_device(): pl.pallas_call(_last_kernel, out_shape=jax.ShapeDtypeStruct(tile, BF16),...  0.96 us
    pallas_call x1, Pallas kernels, per_device(): pl.pallas_call(functools.partial(_prepare_kernel, channels), out_shape=[j...  0.78 us
  transfers between devices with their start and end apart: 9, of which 4 were waited for; matrix products, arithmetic and copies ran while one was open for 0% of the time, Pallas kernels for 14%

profile of v5, /device:TPU:0, one launch (start us, length us, event | category | flops | bytes accessed | tf_op | source)
XLA Modules:
  0.0 20.2 jit_solution(2213937394139131944)
XLA Ops:
  0.0 0.0 copy-start
  0.0 1.9 %project.1.own_ref = bf16[272,256]{1,0:T(8,128)(2,1)S(1)} custom-call(bf16[4,128,256]{2,1,0:T(8,128)(2,1)} %x_hbm.1, s32[1,4]{1,0:T(1,128)} %bitcast.15, s32[1,128]{1,0:T(1,128)} %bitcast.11, f32[1,256]{1,0:T(1,128)} %bitcast.13, f32[1,256]{1,0:T(1,128)} %bitcast.14, bf16[32,256]{1,0:T(8,128)(2,1)} %bitcast.9, bf16[32,256]{1,0:T(8,128)(2,1)} %bitcast.10, ...), custom_call_target="tpu_custom_call" | custom-call | tf_op jit(solution)/shard_map/project/pallas_call | solution.py:344
  1.9 0.6 %collective-permute-start = (bf16[272,256]{1,0:T(8,128)(2,1)S(1)}, bf16[272,256]{1,0:T(8,128)(2,1)S(1)}, u32[]{:S(2)}, u32[]{:S(2)}) collective-permute-start(bf16[272,256]{1,0:T(8,128)(2,1)S(1)} %project.1.own_ref), channel_id=1, source_target_pairs={{0,1},{1,0},{2,3},{3,2},{4,5},{5,4},{6,7},{7,6},{8,9},{9,8},{10,11... | collective-permute-start | bytes 417800 | tf_op jit(solution)/shard_map/ppermute | solution.py:354
  2.4 1.0 %collective-permute-done.other_ref = bf16[272,256]{1,0:T(8,128)(2,1)S(1)} collective-permute-done((bf16[272,256]{1,0:T(8,128)(2,1)S(1)}, bf16[272,256]{1,0:T(8,128)(2,1)S(1)}, u32[]{:S(2)}, u32[]{:S(2)}) %collective-permute-start) | collective-permute-done | bytes 139296 | tf_op jit(solution)/shard_map/ppermute | solution.py:354
  3.5 6.0 %collective-permute-start.1 = (bf16[152,256]{1,0:T(8,128)(2,1)S(1)}, bf16[152,256]{1,0:T(8,128)(2,1)S(1)}, u32[]{:S(2)}, u32[]{:S(2)}) collective-permute-start(bf16[152,256]{1,0:T(8,128)(2,1)S(1)} %get-tuple-element.24), channel_id=1, source_target_pairs={{1,13},{3,15},{5,9},{7,11},{9,5},{11,7},{13,1},{15,3},{0,14},{2,12... | collective-permute-start | bytes 233480 | tf_op jit(solution)/shard_map/ppermute | solution.py:369
  9.4 0.0 collective-permute-start.2
  9.4 1.0 %collective-permute-start.3 = (bf16[152,256]{1,0:T(8,128)(2,1)S(1)}, bf16[152,256]{1,0:T(8,128)(2,1)S(1)}, u32[]{:S(2)}, u32[]{:S(2)}) collective-permute-start(bf16[152,256]{1,0:T(8,128)(2,1)S(1)} %get-tuple-element.26), channel_id=1, source_target_pairs={{1,9},{3,11},{5,13},{7,15},{9,1},{11,3},{13,5},{15,7},{0,2},{2,0},... | collective-permute-start | bytes 233480 | tf_op jit(solution)/shard_map/ppermute | solution.py:369
  10.4 1.1 %collective-permute-start.4 = (bf16[80,256]{1,0:T(8,128)(2,1)S(1)}, bf16[80,256]{1,0:T(8,128)(2,1)S(1)}, u32[]{:S(2)}, u32[]{:S(2)}) collective-permute-start(bf16[80,256]{1,0:T(8,128)(2,1)S(1)} %get-tuple-element.29), channel_id=1, source_target_pairs={{1,11},{3,9},{5,15},{7,13},{9,3},{11,1},{13,7},{15,5},{0,10},{2,8}... | collective-permute-start | bytes 122888 | tf_op jit(solution)/shard_map/ppermute | solution.py:369
  11.5 1.2 %collective-permute-done.1.refs_1_ = bf16[152,256]{1,0:T(8,128)(2,1)S(1)} collective-permute-done((bf16[152,256]{1,0:T(8,128)(2,1)S(1)}, bf16[152,256]{1,0:T(8,128)(2,1)S(1)}, u32[]{:S(2)}, u32[]{:S(2)}) %collective-permute-start.1) | collective-permute-done | bytes 77856 | tf_op jit(solution)/shard_map/ppermute | solution.py:369
  12.7 0.0 collective-permute-start.5
  12.7 2.4 %collective-permute-done.2.refs_2_ = bf16[152,256]{1,0:T(8,128)(2,1)S(1)} collective-permute-done((bf16[152,256]{1,0:T(8,128)(2,1)S(1)}, bf16[152,256]{1,0:T(8,128)(2,1)S(1)}, u32[]{:S(2)}, u32[]{:S(2)}) %collective-permute-start.2) | collective-permute-done | bytes 77856 | tf_op jit(solution)/shard_map/ppermute | solution.py:369
  15.1 0.0 collective-permute-start.6
  15.1 0.0 collective-permute-done.3.refs_3_
  15.1 0.5 %collective-permute-start.7 = (bf16[152,256]{1,0:T(8,128)(2,1)S(1)}, bf16[152,256]{1,0:T(8,128)(2,1)S(1)}, u32[]{:S(2)}, u32[]{:S(2)}) collective-permute-start(bf16[152,256]{1,0:T(8,128)(2,1)S(1)} %collective-permute-done.3.refs_3_), channel_id=1, source_target_pairs={{0,1},{1,0},{2,3},{3,2},{4,5},{5,4},{6,7},{7,6},{8,9},{9,8},{10,11... | collective-permute-start | bytes 233480 | tf_op jit(solution)/shard_map/ppermute | solution.py:370
  15.6 0.6 %collective-permute-done.4.shared_ref.mine_ref = bf16[80,256]{1,0:T(8,128)(2,1)S(1)} collective-permute-done((bf16[80,256]{1,0:T(8,128)(2,1)S(1)}, bf16[80,256]{1,0:T(8,128)(2,1)S(1)}, u32[]{:S(2)}, u32[]{:S(2)}) %collective-permute-start.4) | collective-permute-done | bytes 40992 | tf_op jit(solution)/shard_map/ppermute | solution.py:369
  16.2 0.0 collective-permute-start.8
  16.3 0.0 copy-done
  16.3 0.8 %prepare.1 = (bf16[32,4096]{1,0:T(8,128)(2,1)S(1)}, f32[128,128]{1,0:T(8,128)S(1)}, f32[8,128]{1,0:T(8,128)S(1)}, f32[1,128]{1,0:T(1,128)S(1)}) custom-call(bf16[1024,128]{1,0:T(8,128)(2,1)S(1)} %copy-done, s32[1,128]{1,0:T(1,128)} %bitcast.12, f32[1,128]{1,0:T(1,128)} %bitcast.18), custom_call_target="tpu_custom_call" | custom-call | tf_op jit(solution)/shard_map/prepare/pallas_call | solution.py:377
  17.0 1.1 %early.1 = (f32[128,1024]{1,0:T(8,128)S(1)}, f32[8,256]{1,0:T(8,128)S(1)}) custom-call(bf16[32,4096]{1,0:T(8,128)(2,1)S(1)} %get-tuple-element.22.w_ref, bf16[152,256]{1,0:T(8,128)(2,1)S(1)} %get-tuple-element.23.refs_0_, bf16[152,256]{1,0:T(8,128)(2,1)S(1)} %collective-permute-done.1.refs_1_, bf16[152,256]{1,0:T(8,128)(2,1)S(1)} %collective-permute-done.2.refs_2_, ...), custom_call_target="tpu_custom_call" | custom-call | tf_op jit(solution)/shard_map/early/pallas_call | solution.py:397
  18.1 0.0 collective-permute-done.5.refs_0_
  18.2 0.0 collective-permute-done.6.refs_1_
  18.2 0.0 collective-permute-done.7.refs_2_
  18.2 1.0 %late.1 = (f32[128,1024]{1,0:T(8,128)S(1)}, f32[8,256]{1,0:T(8,128)S(1)}, bf16[256,1024]{1,0:T(8,128)(2,1)S(1)}) custom-call(bf16[32,4096]{1,0:T(8,128)(2,1)S(1)} %get-tuple-element.22.w_ref, f32[128,1024]{1,0:T(8,128)S(1)} %get-tuple-element.27.sum_in, f32[8,256]{1,0:T(8,128)S(1)} %get-tuple-element.28.flags_in, ...), custom_call_target="tpu_custom_call" | custom-call | tf_op jit(solution)/shard_map/late/pallas_call | solution.py:407
  19.2 0.0 collective-permute-done.8.other_ref
  19.2 1.0 %last.1 = bf16[8,128,128]{2,1,0:T(8,128)(2,1)} custom-call(f32[128,128]{1,0:T(8,128)S(1)} %get-tuple-element.19.column_ref, f32[8,128]{1,0:T(8,128)S(1)} %get-tuple-element.20.own_ref, f32[1,128]{1,0:T(1,128)S(1)} %get-tuple-element.21.bias_ref, f32[128,1024]{1,0:T(8,128)S(1)} %get-tuple-element.30.sum_in, f32[8,256]{1,0:T(8,128)S(1)} %get-tuple-element.31.flags_in, ...), custom_call_target="tpu_custom_call" | custom-call | tf_op jit(solution)/shard_map/last/pallas_call | solution.py:417
  (1 shorter events, 0.0 us)
Async XLA Ops:
  0.0 16.3 %copy-start = (bf16[1024,128]{1,0:T(8,128)(2,1)S(1)}, bf16[1024,128]{1,0:T(8,128)(2,1)}, u32[]{:S(2)}) copy-start(bf16[1024,128]{1,0:T(8,128)(2,1)} %raw_ref.1) | copy-start | bytes 786436
  1.9 1.6 %collective-permute-start = (bf16[272,256]{1,0:T(8,128)(2,1)S(1)}, bf16[272,256]{1,0:T(8,128)(2,1)S(1)}, u32[]{:S(2)}, u32[]{:S(2)}) collective-permute-start(bf16[272,256]{1,0:T(8,128)(2,1)S(1)} %project.1.own_ref), channel_id=1, source_target_pairs={{0,1},{1,0},{2,3},{3,2},{4,5},{5,4},{6,7},{7,6},{8,9},{9,8},{10,11... | collective-permute-start | bytes 417800 | tf_op jit(solution)/shard_map/ppermute | solution.py:354
  3.5 9.2 %collective-permute-start.1 = (bf16[152,256]{1,0:T(8,128)(2,1)S(1)}, bf16[152,256]{1,0:T(8,128)(2,1)S(1)}, u32[]{:S(2)}, u32[]{:S(2)}) collective-permute-start(bf16[152,256]{1,0:T(8,128)(2,1)S(1)} %get-tuple-element.24), channel_id=1, source_target_pairs={{1,13},{3,15},{5,9},{7,11},{9,5},{11,7},{13,1},{15,3},{0,14},{2,12... | collective-permute-start | bytes 233480 | tf_op jit(solution)/shard_map/ppermute | solution.py:369
  9.4 5.7 %collective-permute-start.2 = (bf16[152,256]{1,0:T(8,128)(2,1)S(1)}, bf16[152,256]{1,0:T(8,128)(2,1)S(1)}, u32[]{:S(2)}, u32[]{:S(2)}) collective-permute-start(bf16[152,256]{1,0:T(8,128)(2,1)S(1)} %get-tuple-element.25), channel_id=1, source_target_pairs={{1,5},{3,7},{5,1},{7,3},{9,13},{11,15},{13,9},{15,11},{0,6},{2,4},... | collective-permute-start | bytes 233480 | tf_op jit(solution)/shard_map/ppermute | solution.py:369
  9.4 5.7 %collective-permute-start.3 = (bf16[152,256]{1,0:T(8,128)(2,1)S(1)}, bf16[152,256]{1,0:T(8,128)(2,1)S(1)}, u32[]{:S(2)}, u32[]{:S(2)}) collective-permute-start(bf16[152,256]{1,0:T(8,128)(2,1)S(1)} %get-tuple-element.26), channel_id=1, source_target_pairs={{1,9},{3,11},{5,13},{7,15},{9,1},{11,3},{13,5},{15,7},{0,2},{2,0},... | collective-permute-start | bytes 233480 | tf_op jit(solution)/shard_map/ppermute | solution.py:369
  10.4 5.8 %collective-permute-start.4 = (bf16[80,256]{1,0:T(8,128)(2,1)S(1)}, bf16[80,256]{1,0:T(8,128)(2,1)S(1)}, u32[]{:S(2)}, u32[]{:S(2)}) collective-permute-start(bf16[80,256]{1,0:T(8,128)(2,1)S(1)} %get-tuple-element.29), channel_id=1, source_target_pairs={{1,11},{3,9},{5,15},{7,13},{9,3},{11,1},{13,7},{15,5},{0,10},{2,8}... | collective-permute-start | bytes 122888 | tf_op jit(solution)/shard_map/ppermute | solution.py:369
  12.7 5.5 %collective-permute-start.5 = (bf16[152,256]{1,0:T(8,128)(2,1)S(1)}, bf16[152,256]{1,0:T(8,128)(2,1)S(1)}, u32[]{:S(2)}, u32[]{:S(2)}) collective-permute-start(bf16[152,256]{1,0:T(8,128)(2,1)S(1)} %collective-permute-done.1.refs_1_), channel_id=1, source_target_pairs={{0,1},{1,0},{2,3},{3,2},{4,5},{5,4},{6,7},{7,6},{8,9},{9,8},{10,11... | collective-permute-start | bytes 233480 | tf_op jit(solution)/shard_map/ppermute | solution.py:370
  15.1 3.0 %collective-permute-start.6 = (bf16[152,256]{1,0:T(8,128)(2,1)S(1)}, bf16[152,256]{1,0:T(8,128)(2,1)S(1)}, u32[]{:S(2)}, u32[]{:S(2)}) collective-permute-start(bf16[152,256]{1,0:T(8,128)(2,1)S(1)} %collective-permute-done.2.refs_2_), channel_id=1, source_target_pairs={{0,1},{1,0},{2,3},{3,2},{4,5},{5,4},{6,7},{7,6},{8,9},{9,8},{10,11... | collective-permute-start | bytes 233480 | tf_op jit(solution)/shard_map/ppermute | solution.py:370
  15.1 3.0 %collective-permute-start.7 = (bf16[152,256]{1,0:T(8,128)(2,1)S(1)}, bf16[152,256]{1,0:T(8,128)(2,1)S(1)}, u32[]{:S(2)}, u32[]{:S(2)}) collective-permute-start(bf16[152,256]{1,0:T(8,128)(2,1)S(1)} %collective-permute-done.3.refs_3_), channel_id=1, source_target_pairs={{0,1},{1,0},{2,3},{3,2},{4,5},{5,4},{6,7},{7,6},{8,9},{9,8},{10,11... | collective-permute-start | bytes 233480 | tf_op jit(solution)/shard_map/ppermute | solution.py:370
  16.2 3.0 %collective-permute-start.8 = (bf16[80,256]{1,0:T(8,128)(2,1)S(1)}, bf16[80,256]{1,0:T(8,128)(2,1)S(1)}, u32[]{:S(2)}, u32[]{:S(2)}) collective-permute-start(bf16[80,256]{1,0:T(8,128)(2,1)S(1)} %collective-permute-done.4.shared_ref.mine_ref), channel_id=1, source_target_pairs={{0,1},{1,0},{2,3},{3,2},{4,5},{5,4},{6,7},{7,6},{8,9},{9,8},{10,11... | collective-permute-start | bytes 122888 | tf_op jit(solution)/shard_map/ppermute | solution.py:370

commit v6 on v5

--- a/solution.py
+++ b/solution.py
@@ -251,6 +251,15 @@
     flags_ref[...] = _flags(parcels)
 
 
+def _middle_kernel(count, w_ref, sum_in, flags_in, *refs):
+    parcels, (sum_ref, flags_ref, a_ref) = refs[:count], refs[count:]
+    residues, lanes = sum_ref.shape[0], parcels[0].shape[1]
+    slabs = [_slab(ref, residues) for ref in parcels]
+    _spread(slabs, w_ref, [(a_ref, n * lanes) for n in range(count)])
+    sum_ref[...] = sum_in[...] + _contract(parcels, a_ref, residues)
+    flags_ref[...] = flags_in[...] + _flags(parcels)
+
+
 def _late_kernel(count, w_ref, sum_in, flags_in, shared_ref, *refs):
     parcels, (sum_ref, flags_ref, shared_a_ref, a_ref) = refs[:count], refs[count:]
     residues, lanes = sum_ref.shape[0], parcels[0].shape[1]
@@ -393,7 +402,8 @@
         name="prepare",
     )(out_weight, _stay(crop), _stay(out_bias.reshape(1, -1)))
 
-    early = [own] + received[:-1]
+    order = arrival(len(steps))
+    early = [own] + [received[n] for n in order[:-3]]
     carry = pl.pallas_call(
         functools.partial(_early_kernel, len(early)),
         out_shape=state,
@@ -403,16 +413,28 @@
         compiler_params=limit,
         name="early",
     )(weight, *early)
-    late = handed[:-1]
+    groups = {
+        "second": [received[order[-3]]] + [handed[n] for n in order[:-3]],
+        "middle": [received[order[-2]], handed[order[-3]]],
+    }
+    for group in groups.values():
+        carry = pl.pallas_call(
+            functools.partial(_middle_kernel, len(group)),
+            out_shape=state,
+            in_specs=_vmem(3 + len(group)),
+            out_specs=_vmem(2),
+            scratch_shapes=[pltpu.VMEM((len(group) * lanes, columns), BF16)],
+            compiler_params=limit,
+        )(weight, *carry, *group)
     carry = pl.pallas_call(
-        functools.partial(_late_kernel, len(late)),
+        functools.partial(_late_kernel, 1),
         out_shape=state + [jax.ShapeDtypeStruct((lanes, columns), BF16)],
-        in_specs=_vmem(4 + len(late)),
+        in_specs=_vmem(5),
         out_specs=_vmem(3),
-        scratch_shapes=[pltpu.VMEM((len(late) * lanes, columns), BF16)],
+        scratch_shapes=[pltpu.VMEM((lanes, columns), BF16)],
         compiler_params=limit,
         name="late",
-    )(weight, *carry, received[-1], *late)
+    )(weight, *carry, received[-1], handed[order[-2]])
     tile = (rows_here, residues, width)
     return pl.pallas_call(
         _last_kernel,
@@ -428,6 +450,10 @@
     )(*spread, *carry, received[-1], handed[-1])
 
 
+def arrival(count):
+    return [0] + list(range(2, count - 1)) + [1, count - 1]
+
+
 def solution(mesh):
     return jax.shard_map(
         per_device,

time: 20.4 us -> 21.1 us (1.034)
  Pallas kernels: 5.77 us -> 6.45 us
  waiting for transfers between devices: 5.2 us -> 5.72 us
  starting transfers between devices: 9.15 us -> 8.73 us
    pallas_call x1 -> x3, Pallas kernels: 1.03 us -> 2.08 us  [the longest x2 1.45 us: per_device(): pl.pallas_call(functools.partial(_middle_kernel, len(group)), out_shape=s...]
    ppermute x4, waiting for transfers between devices: 4.19 us -> 4.72 us  [per_device(): received.append(lax.ppermute(piece, 'row', pairs))]
    ppermute x4, starting transfers between devices: 0.52 us -> 0.09 us  [per_device(): handed.append(lax.ppermute(received[-1], 'row', cores))]
    pallas_call x1, Pallas kernels: 1.1 us -> 0.73 us  [per_device(): pl.pallas_call(functools.partial(_early_kernel, len(early)), out_shape=st...]
  transfers between devices with their start and end apart: 9 -> 9, of which waited for: 4 -> 5; matrix products, arithmetic and copies ran while one was open for 0% -> 0% of each run, Pallas kernels for 14% -> 17%
where the time goes in v6:
time: 21.1 us; the launch traced here: 21 us
  starting transfers between devices  8.73 us (41%)
  Pallas kernels  6.45 us (31%)
  waiting for transfers between devices  5.72 us (27%)
    ppermute x4, starting transfers between devices, per_device(): received.append(lax.ppermute(piece, 'row', pairs))  8.07 us
    ppermute x4, waiting for transfers between devices, per_device(): received.append(lax.ppermute(piece, 'row', pairs))  4.72 us
    pallas_call x1, Pallas kernels, per_device(): pl.pallas_call(_project_kernel, out_shape=jax.ShapeDtypeStruct((2 * resid...  1.87 us
    pallas_call x2, Pallas kernels, per_device(): pl.pallas_call(functools.partial(_middle_kernel, len(group)), out_shape=s...  1.45 us
    ppermute x1, waiting for transfers between devices, per_device(): other = lax.ppermute(projected, 'row', cores)  1 us
    pallas_call x1, Pallas kernels, per_device(): pl.pallas_call(_last_kernel, out_shape=jax.ShapeDtypeStruct(tile, BF16),...  0.96 us
    pallas_call x1, Pallas kernels, per_device(): pl.pallas_call(functools.partial(_prepare_kernel, channels), out_shape=[j...  0.78 us
    pallas_call x1, Pallas kernels, per_device(): pl.pallas_call(functools.partial(_early_kernel, len(early)), out_shape=st...  0.73 us
  transfers between devices with their start and end apart: 9, of which 5 were waited for; matrix products, arithmetic and copies ran while one was open for 0% of the time, Pallas kernels for 17%

profile of v6, /device:TPU:0, one launch (start us, length us, event | category | flops | bytes accessed | tf_op | source)
XLA Modules:
  0.0 21.0 jit_solution(1127952566324610986)
XLA Ops:
  0.0 0.0 copy-start
  0.0 1.9 %project.1.own_ref = bf16[272,256]{1,0:T(8,128)(2,1)S(1)} custom-call(bf16[4,128,256]{2,1,0:T(8,128)(2,1)} %x_hbm.1, s32[1,4]{1,0:T(1,128)} %bitcast.15, s32[1,128]{1,0:T(1,128)} %bitcast.11, f32[1,256]{1,0:T(1,128)} %bitcast.13, f32[1,256]{1,0:T(1,128)} %bitcast.14, bf16[32,256]{1,0:T(8,128)(2,1)} %bitcast.9, bf16[32,256]{1,0:T(8,128)(2,1)} %bitcast.10, ...), custom_call_target="tpu_custom_call" | custom-call | tf_op jit(solution)/shard_map/project/pallas_call | solution.py:353
  1.9 0.6 %collective-permute-start = (bf16[272,256]{1,0:T(8,128)(2,1)S(1)}, bf16[272,256]{1,0:T(8,128)(2,1)S(1)}, u32[]{:S(2)}, u32[]{:S(2)}) collective-permute-start(bf16[272,256]{1,0:T(8,128)(2,1)S(1)} %project.1.own_ref), channel_id=1, source_target_pairs={{0,1},{1,0},{2,3},{3,2},{4,5},{5,4},{6,7},{7,6},{8,9},{9,8},{10,11... | collective-permute-start | bytes 417800 | tf_op jit(solution)/shard_map/ppermute | solution.py:363
  2.4 1.0 %collective-permute-done.other_ref = bf16[272,256]{1,0:T(8,128)(2,1)S(1)} collective-permute-done((bf16[272,256]{1,0:T(8,128)(2,1)S(1)}, bf16[272,256]{1,0:T(8,128)(2,1)S(1)}, u32[]{:S(2)}, u32[]{:S(2)}) %collective-permute-start) | collective-permute-done | bytes 139296 | tf_op jit(solution)/shard_map/ppermute | solution.py:363
  3.5 6.0 %collective-permute-start.1 = (bf16[152,256]{1,0:T(8,128)(2,1)S(1)}, bf16[152,256]{1,0:T(8,128)(2,1)S(1)}, u32[]{:S(2)}, u32[]{:S(2)}) collective-permute-start(bf16[152,256]{1,0:T(8,128)(2,1)S(1)} %get-tuple-element.28), channel_id=1, source_target_pairs={{1,13},{3,15},{5,9},{7,11},{9,5},{11,7},{13,1},{15,3},{0,14},{2,12... | collective-permute-start | bytes 233480 | tf_op jit(solution)/shard_map/ppermute | solution.py:378
  9.4 0.5 %collective-permute-start.2 = (bf16[152,256]{1,0:T(8,128)(2,1)S(1)}, bf16[152,256]{1,0:T(8,128)(2,1)S(1)}, u32[]{:S(2)}, u32[]{:S(2)}) collective-permute-start(bf16[152,256]{1,0:T(8,128)(2,1)S(1)} %get-tuple-element.31), channel_id=1, source_target_pairs={{1,9},{3,11},{5,13},{7,15},{9,1},{11,3},{13,5},{15,7},{0,2},{2,0},... | collective-permute-start | bytes 233480 | tf_op jit(solution)/shard_map/ppermute | solution.py:378
  9.9 0.5 %collective-permute-start.4 = (bf16[152,256]{1,0:T(8,128)(2,1)S(1)}, bf16[152,256]{1,0:T(8,128)(2,1)S(1)}, u32[]{:S(2)}, u32[]{:S(2)}) collective-permute-start(bf16[152,256]{1,0:T(8,128)(2,1)S(1)} %get-tuple-element.34), channel_id=1, source_target_pairs={{1,5},{3,7},{5,1},{7,3},{9,13},{11,15},{13,9},{15,11},{0,6},{2,4},... | collective-permute-start | bytes 233480 | tf_op jit(solution)/shard_map/ppermute | solution.py:378
  10.4 1.1 %collective-permute-start.6 = (bf16[80,256]{1,0:T(8,128)(2,1)S(1)}, bf16[80,256]{1,0:T(8,128)(2,1)S(1)}, u32[]{:S(2)}, u32[]{:S(2)}) collective-permute-start(bf16[80,256]{1,0:T(8,128)(2,1)S(1)} %get-tuple-element.37), channel_id=1, source_target_pairs={{1,11},{3,9},{5,15},{7,13},{9,3},{11,1},{13,7},{15,5},{0,10},{2,8}... | collective-permute-start | bytes 122888 | tf_op jit(solution)/shard_map/ppermute | solution.py:378
  11.5 1.0 %collective-permute-done.1.refs_1_ = bf16[152,256]{1,0:T(8,128)(2,1)S(1)} collective-permute-done((bf16[152,256]{1,0:T(8,128)(2,1)S(1)}, bf16[152,256]{1,0:T(8,128)(2,1)S(1)}, u32[]{:S(2)}, u32[]{:S(2)}) %collective-permute-start.1) | collective-permute-done | bytes 77856 | tf_op jit(solution)/shard_map/ppermute | solution.py:378
  12.6 0.0 collective-permute-start.3
  12.6 1.3 %collective-permute-done.2.refs_0_ = bf16[152,256]{1,0:T(8,128)(2,1)S(1)} collective-permute-done((bf16[152,256]{1,0:T(8,128)(2,1)S(1)}, bf16[152,256]{1,0:T(8,128)(2,1)S(1)}, u32[]{:S(2)}, u32[]{:S(2)}) %collective-permute-start.2) | collective-permute-done | bytes 77856 | tf_op jit(solution)/shard_map/ppermute | solution.py:378
  13.8 0.0 collective-permute-start.5
  13.8 2.0 %collective-permute-done.4.refs_0_ = bf16[152,256]{1,0:T(8,128)(2,1)S(1)} collective-permute-done((bf16[152,256]{1,0:T(8,128)(2,1)S(1)}, bf16[152,256]{1,0:T(8,128)(2,1)S(1)}, u32[]{:S(2)}, u32[]{:S(2)}) %collective-permute-start.4) | collective-permute-done | bytes 77856 | tf_op jit(solution)/shard_map/ppermute | solution.py:378
  15.8 0.0 collective-permute-start.7
  15.8 0.4 %collective-permute-done.6.shared_ref.mine_ref = bf16[80,256]{1,0:T(8,128)(2,1)S(1)} collective-permute-done((bf16[80,256]{1,0:T(8,128)(2,1)S(1)}, bf16[80,256]{1,0:T(8,128)(2,1)S(1)}, u32[]{:S(2)}, u32[]{:S(2)}) %collective-permute-start.6) | collective-permute-done | bytes 40992 | tf_op jit(solution)/shard_map/ppermute | solution.py:378
  16.3 0.1 collective-permute-start.8
  16.4 0.0 copy-done
  16.4 0.8 %prepare.1 = (bf16[32,4096]{1,0:T(8,128)(2,1)S(1)}, f32[128,128]{1,0:T(8,128)S(1)}, f32[8,128]{1,0:T(8,128)S(1)}, f32[1,128]{1,0:T(1,128)S(1)}) custom-call(bf16[1024,128]{1,0:T(8,128)(2,1)S(1)} %copy-done, s32[1,128]{1,0:T(1,128)} %bitcast.12, f32[1,128]{1,0:T(1,128)} %bitcast.18), custom_call_target="tpu_custom_call" | custom-call | tf_op jit(solution)/shard_map/prepare/pallas_call | solution.py:386
  17.1 0.7 %early.1 = (f32[128,1024]{1,0:T(8,128)S(1)}, f32[8,256]{1,0:T(8,128)S(1)}) custom-call(bf16[32,4096]{1,0:T(8,128)(2,1)S(1)} %get-tuple-element.26.w_ref, bf16[152,256]{1,0:T(8,128)(2,1)S(1)} %get-tuple-element.27.refs_0_, bf16[152,256]{1,0:T(8,128)(2,1)S(1)} %collective-permute-done.1.refs_1_), custom_call_target="tpu_custom_call" | custom-call | tf_op jit(solution)/shard_map/early/pallas_call | solution.py:407
  17.9 0.0 collective-permute-done.3.refs_1_
  17.9 0.7 %shard_map.109 = (f32[128,1024]{1,0:T(8,128)S(1)}, f32[8,256]{1,0:T(8,128)S(1)}) custom-call(bf16[32,4096]{1,0:T(8,128)(2,1)S(1)} %get-tuple-element.26.w_ref, f32[128,1024]{1,0:T(8,128)S(1)} %get-tuple-element.29.sum_in, f32[8,256]{1,0:T(8,128)S(1)} %get-tuple-element.30.flags_in, bf16[152,256]{1,0:T(8,128)(2,1)S(1)} %collective-permute-done.2.refs_0_, ...), custom_call_target="tpu_custom_call" | custom-call | tf_op jit(solution)/shard_map/pallas_call | solution.py:421
  18.6 0.0 collective-permute-done.5.refs_1_
  18.6 0.7 %shard_map.110 = (f32[128,1024]{1,0:T(8,128)S(1)}, f32[8,256]{1,0:T(8,128)S(1)}) custom-call(bf16[32,4096]{1,0:T(8,128)(2,1)S(1)} %get-tuple-element.26.w_ref, f32[128,1024]{1,0:T(8,128)S(1)} %get-tuple-element.32.sum_in, f32[8,256]{1,0:T(8,128)S(1)} %get-tuple-element.33.flags_in, bf16[152,256]{1,0:T(8,128)(2,1)S(1)} %collective-permute-done.4.refs_0_, ...), custom_call_target="tpu_custom_call" | custom-call | tf_op jit(solution)/shard_map/pallas_call | solution.py:421
  19.4 0.0 collective-permute-done.7.refs_0_
  19.4 0.6 %late.1 = (f32[128,1024]{1,0:T(8,128)S(1)}, f32[8,256]{1,0:T(8,128)S(1)}, bf16[256,1024]{1,0:T(8,128)(2,1)S(1)}) custom-call(bf16[32,4096]{1,0:T(8,128)(2,1)S(1)} %get-tuple-element.26.w_ref, f32[128,1024]{1,0:T(8,128)S(1)} %get-tuple-element.35.sum_in, f32[8,256]{1,0:T(8,128)S(1)} %get-tuple-element.36.flags_in, ...), custom_call_target="tpu_custom_call" | custom-call | tf_op jit(solution)/shard_map/late/pallas_call | solution.py:429
  20.0 0.0 collective-permute-done.8.other_ref
  20.0 1.0 %last.1 = bf16[8,128,128]{2,1,0:T(8,128)(2,1)} custom-call(f32[128,128]{1,0:T(8,128)S(1)} %get-tuple-element.23.column_ref, f32[8,128]{1,0:T(8,128)S(1)} %get-tuple-element.24.own_ref, f32[1,128]{1,0:T(1,128)S(1)} %get-tuple-element.25.bias_ref, f32[128,1024]{1,0:T(8,128)S(1)} %get-tuple-element.38.sum_in, f32[8,256]{1,0:T(8,128)S(1)} %get-tuple-element.39.flags_in, ...), custom_call_target="tpu_custom_call" | custom-call | tf_op jit(solution)/shard_map/last/pallas_call | solution.py:439
  (1 shorter events, 0.0 us)
Async XLA Ops:
  0.0 16.4 %copy-start = (bf16[1024,128]{1,0:T(8,128)(2,1)S(1)}, bf16[1024,128]{1,0:T(8,128)(2,1)}, u32[]{:S(2)}) copy-start(bf16[1024,128]{1,0:T(8,128)(2,1)} %raw_ref.1) | copy-start | bytes 786436
  1.9 1.6 %collective-permute-start = (bf16[272,256]{1,0:T(8,128)(2,1)S(1)}, bf16[272,256]{1,0:T(8,128)(2,1)S(1)}, u32[]{:S(2)}, u32[]{:S(2)}) collective-permute-start(bf16[272,256]{1,0:T(8,128)(2,1)S(1)} %project.1.own_ref), channel_id=1, source_target_pairs={{0,1},{1,0},{2,3},{3,2},{4,5},{5,4},{6,7},{7,6},{8,9},{9,8},{10,11... | collective-permute-start | bytes 417800 | tf_op jit(solution)/shard_map/ppermute | solution.py:363
  3.5 9.1 %collective-permute-start.1 = (bf16[152,256]{1,0:T(8,128)(2,1)S(1)}, bf16[152,256]{1,0:T(8,128)(2,1)S(1)}, u32[]{:S(2)}, u32[]{:S(2)}) collective-permute-start(bf16[152,256]{1,0:T(8,128)(2,1)S(1)} %get-tuple-element.28), channel_id=1, source_target_pairs={{1,13},{3,15},{5,9},{7,11},{9,5},{11,7},{13,1},{15,3},{0,14},{2,12... | collective-permute-start | bytes 233480 | tf_op jit(solution)/shard_map/ppermute | solution.py:378
  9.4 4.4 %collective-permute-start.2 = (bf16[152,256]{1,0:T(8,128)(2,1)S(1)}, bf16[152,256]{1,0:T(8,128)(2,1)S(1)}, u32[]{:S(2)}, u32[]{:S(2)}) collective-permute-start(bf16[152,256]{1,0:T(8,128)(2,1)S(1)} %get-tuple-element.31), channel_id=1, source_target_pairs={{1,9},{3,11},{5,13},{7,15},{9,1},{11,3},{13,5},{15,7},{0,2},{2,0},... | collective-permute-start | bytes 233480 | tf_op jit(solution)/shard_map/ppermute | solution.py:378
  9.9 5.9 %collective-permute-start.4 = (bf16[152,256]{1,0:T(8,128)(2,1)S(1)}, bf16[152,256]{1,0:T(8,128)(2,1)S(1)}, u32[]{:S(2)}, u32[]{:S(2)}) collective-permute-start(bf16[152,256]{1,0:T(8,128)(2,1)S(1)} %get-tuple-element.34), channel_id=1, source_target_pairs={{1,5},{3,7},{5,1},{7,3},{9,13},{11,15},{13,9},{15,11},{0,6},{2,4},... | collective-permute-start | bytes 233480 | tf_op jit(solution)/shard_map/ppermute | solution.py:378
  10.4 5.8 %collective-permute-start.6 = (bf16[80,256]{1,0:T(8,128)(2,1)S(1)}, bf16[80,256]{1,0:T(8,128)(2,1)S(1)}, u32[]{:S(2)}, u32[]{:S(2)}) collective-permute-start(bf16[80,256]{1,0:T(8,128)(2,1)S(1)} %get-tuple-element.37), channel_id=1, source_target_pairs={{1,11},{3,9},{5,15},{7,13},{9,3},{11,1},{13,7},{15,5},{0,10},{2,8}... | collective-permute-start | bytes 122888 | tf_op jit(solution)/shard_map/ppermute | solution.py:378
  12.6 5.3 %collective-permute-start.3 = (bf16[152,256]{1,0:T(8,128)(2,1)S(1)}, bf16[152,256]{1,0:T(8,128)(2,1)S(1)}, u32[]{:S(2)}, u32[]{:S(2)}) collective-permute-start(bf16[152,256]{1,0:T(8,128)(2,1)S(1)} %collective-permute-done.1.refs_1_), channel_id=1, source_target_pairs={{0,1},{1,0},{2,3},{3,2},{4,5},{5,4},{6,7},{7,6},{8,9},{9,8},{10,11... | collective-permute-start | bytes 233480 | tf_op jit(solution)/shard_map/ppermute | solution.py:379
  13.8 4.8 %collective-permute-start.5 = (bf16[152,256]{1,0:T(8,128)(2,1)S(1)}, bf16[152,256]{1,0:T(8,128)(2,1)S(1)}, u32[]{:S(2)}, u32[]{:S(2)}) collective-permute-start(bf16[152,256]{1,0:T(8,128)(2,1)S(1)} %collective-permute-done.2.refs_0_), channel_id=1, source_target_pairs={{0,1},{1,0},{2,3},{3,2},{4,5},{5,4},{6,7},{7,6},{8,9},{9,8},{10,11... | collective-permute-start | bytes 233480 | tf_op jit(solution)/shard_map/ppermute | solution.py:379
  15.8 3.5 %collective-permute-start.7 = (bf16[152,256]{1,0:T(8,128)(2,1)S(1)}, bf16[152,256]{1,0:T(8,128)(2,1)S(1)}, u32[]{:S(2)}, u32[]{:S(2)}) collective-permute-start(bf16[152,256]{1,0:T(8,128)(2,1)S(1)} %collective-permute-done.4.refs_0_), channel_id=1, source_target_pairs={{0,1},{1,0},{2,3},{3,2},{4,5},{5,4},{6,7},{7,6},{8,9},{9,8},{10,11... | collective-permute-start | bytes 233480 | tf_op jit(solution)/shard_map/ppermute | solution.py:379
  16.3 3.8 %collective-permute-start.8 = (bf16[80,256]{1,0:T(8,128)(2,1)S(1)}, bf16[80,256]{1,0:T(8,128)(2,1)S(1)}, u32[]{:S(2)}, u32[]{:S(2)}) collective-permute-start(bf16[80,256]{1,0:T(8,128)(2,1)S(1)} %collective-permute-done.6.shared_ref.mine_ref), channel_id=1, source_target_pairs={{0,1},{1,0},{2,3},{3,2},{4,5},{5,4},{6,7},{7,6},{8,9},{9,8},{10,11... | collective-permute-start | bytes 122888 | tf_op jit(solution)/shard_map/ppermute | solution.py:379

commit v7 on v6

--- a/solution.py
+++ b/solution.py
@@ -260,54 +260,81 @@
     flags_ref[...] = flags_in[...] + _flags(parcels)
 
 
-def _late_kernel(count, w_ref, sum_in, flags_in, shared_ref, *refs):
-    parcels, (sum_ref, flags_ref, shared_a_ref, a_ref) = refs[:count], refs[count:]
-    residues, lanes = sum_ref.shape[0], parcels[0].shape[1]
-    slabs = [_slab(ref, residues) for ref in parcels]
-    slabs.append(shared_ref[residues // 2 :].astype(F32)[:-FLAG_ROWS])
-    targets = [(a_ref, n * lanes) for n in range(count)] + [(shared_a_ref, 0)]
-    _spread(slabs, w_ref, targets)
-    sum_ref[...] = sum_in[...] + _contract(parcels, a_ref, residues)
-    flags_ref[...] = flags_in[...] + _flags(parcels + (shared_ref,))
-
-
-def _last_kernel(
+def _finish(total, refs, other, live, out_ref, out_hbm, sems):
+    column_ref, own_ref, bias_ref = refs
+    rows_here, half, width = out_ref.shape
+    upper = (lax.axis_index("row") % 2 == 1) != other
+    column = jnp.where(upper, column_ref[0:half], column_ref[half:])
+    offset = pl.multiple_of(jnp.where(upper, 0, half), half)
+    inside = jnp.where(column > 0.0, 1.0 / jnp.maximum(live, 1.0), 1.0)
+    stores = []
+    for i in range(rows_here):
+        scale = jnp.where(own_ref[i : i + 1] > 0.0, inside, 1.0)
+        part = total[:, i * width : (i + 1) * width]
+        out_ref[i] = (part * scale + bias_ref[...]).astype(BF16)
+        stores.append(
+            pltpu.make_async_copy(out_ref.at[i], out_hbm.at[i, pl.ds(offset, half)], sems.at[i])
+        )
+        stores[-1].start()
+    for copy in stores:
+        copy.wait()
+
+
+def _total(flags):
+    return jnp.sum(jnp.sum(flags, axis=1, keepdims=True), axis=0, keepdims=True)
+
+
+def _late_kernel(
+    w_ref,
     column_ref,
     own_ref,
     bias_ref,
     sum_in,
     flags_in,
+    shared_ref,
+    parcel_ref,
+    rest_ref,
+    flags_ref,
+    shared_a_ref,
+    out_hbm,
     a_ref,
-    mine_ref,
+    out_ref,
+    sems,
+):
+    residues = sum_in.shape[0]
+    half = residues // 2
+    north = lax.axis_index("row") % 2 == 1
+    slabs = [_slab(parcel_ref, residues), shared_ref[half:].astype(F32)[:-FLAG_ROWS]]
+    _spread(slabs, w_ref, [(a_ref, 0), (shared_a_ref, 0)])
+    total = sum_in[...] + _contract((parcel_ref,), a_ref, residues)
+    rest_ref[...] = jnp.where(north, total[half:], total[:half])
+    mine = jnp.where(north, total[:half], total[half:])
+    mine = mine + jnp.dot(shared_ref[0:half], shared_a_ref[...], preferred_element_type=F32)
+    flags = flags_in[...] + _flags((parcel_ref, shared_ref))
+    flags_ref[...] = flags
+    refs = (column_ref, own_ref, bias_ref)
+    _finish(mine, refs, False, _total(flags), out_ref, out_hbm, sems)
+
+
+def _last_kernel(
+    column_ref,
+    own_ref,
+    bias_ref,
+    rest_ref,
+    flags_ref,
+    a_ref,
     other_ref,
+    begun_hbm,
     out_hbm,
     out_ref,
     sems,
 ):
-    rows_here, residues, width = out_ref.shape
-    half = residues // 2
-    core = lax.axis_index("row") % 2
-    mine, other = mine_ref[0:half], other_ref[0:half]
-    right = jnp.concatenate(
-        [jnp.where(core == 1, mine, other), jnp.where(core == 1, other, mine)], axis=0
+    half = rest_ref.shape[0]
+    total = rest_ref[...] + jnp.dot(
+        other_ref[0:half], a_ref[...], preferred_element_type=F32
     )
-    live = jnp.sum(jnp.sum(flags_in[...], axis=1, keepdims=True), axis=0, keepdims=True)
-    inside = jnp.where(column_ref[...] > 0.0, 1.0 / jnp.maximum(live, 1.0), 1.0)
-    stores = []
-    group = 2 if rows_here % 2 == 0 else 1
-    for first in range(0, rows_here, group):
-        columns = slice(first * width, (first + group) * width)
-        projected = sum_in[:, columns] + jnp.dot(
-            right, a_ref[:, columns], preferred_element_type=F32
-        )
-        for i in range(first, first + group):
-            scale = jnp.where(own_ref[i : i + 1] > 0.0, inside, 1.0)
-            part = projected[:, (i - first) * width : (i - first + 1) * width]
-            out_ref[i] = (part * scale + bias_ref[...]).astype(BF16)
-            stores.append(pltpu.make_async_copy(out_ref.at[i], out_hbm.at[i], sems.at[i]))
-            stores[-1].start()
-    for copy in stores:
-        copy.wait()
+    refs = (column_ref, own_ref, bias_ref)
+    _finish(total, refs, True, _total(flags_ref[...]), out_ref, out_hbm, sems)
 
 
 def per_device(
@@ -426,28 +453,35 @@
             scratch_shapes=[pltpu.VMEM((len(group) * lanes, columns), BF16)],
             compiler_params=limit,
         )(weight, *carry, *group)
-    carry = pl.pallas_call(
-        functools.partial(_late_kernel, 1),
-        out_shape=state + [jax.ShapeDtypeStruct((lanes, columns), BF16)],
-        in_specs=_vmem(5),
-        out_specs=_vmem(3),
-        scratch_shapes=[pltpu.VMEM((lanes, columns), BF16)],
+    tile = jax.ShapeDtypeStruct((rows_here, residues, width), BF16)
+    stage = [
+        pltpu.VMEM((rows_here, residues // 2, width), BF16),
+        pltpu.SemaphoreType.DMA((rows_here,)),
+    ]
+    *carry, begun = pl.pallas_call(
+        _late_kernel,
+        out_shape=[
+            jax.ShapeDtypeStruct((residues // 2, columns), F32),
+            state[1],
+            jax.ShapeDtypeStruct((lanes, columns), BF16),
+            tile,
+        ],
+        in_specs=_vmem(8),
+        out_specs=_vmem(3) + [anywhere],
+        scratch_shapes=[pltpu.VMEM((lanes, columns), BF16)] + stage,
         compiler_params=limit,
         name="late",
-    )(weight, *carry, received[-1], handed[order[-2]])
-    tile = (rows_here, residues, width)
+    )(weight, *spread, *carry, received[-1], handed[order[-2]])
     return pl.pallas_call(
         _last_kernel,
-        out_shape=jax.ShapeDtypeStruct(tile, BF16),
-        in_specs=_vmem(8),
+        out_shape=tile,
+        in_specs=_vmem(7) + [anywhere],
         out_specs=anywhere,
-        scratch_shapes=[
-            pltpu.VMEM(tile, BF16),
-            pltpu.SemaphoreType.DMA((rows_here,)),
-        ],
+        scratch_shapes=stage,
+        input_output_aliases={7: 0},
         compiler_params=limit,
         name="last",
-    )(*spread, *carry, received[-1], handed[-1])
+    )(*spread, *carry, handed[-1], begun)
 
 
 def arrival(count):

time: 21.1 us -> 21.9 us (1.038)
  Pallas kernels: 6.45 us -> 7.18 us
    pallas_call x2, Pallas kernels: 1.59 us -> 2.31 us  [the longest x1 1.4 us: per_device(): pl.pallas_call(_late_kernel, out_shape=[jax.ShapeDtypeStruct((residues //...]
  transfers between devices with their start and end apart: 9 -> 9, of which waited for: 5 -> 5; matrix products, arithmetic and copies ran while one was open for 0% -> 0% of each run, Pallas kernels for 17% -> 20%
where the time goes in v7:
time: 21.9 us; the launch traced here: 21.7 us
  starting transfers between devices  8.73 us (40%)
  Pallas kernels  7.18 us (33%)
  waiting for transfers between devices  5.72 us (26%)
    ppermute x4, starting transfers between devices, per_device(): received.append(lax.ppermute(piece, 'row', pairs))  8.07 us
    ppermute x4, waiting for transfers between devices, per_device(): received.append(lax.ppermute(piece, 'row', pairs))  4.72 us
    pallas_call x1, Pallas kernels, per_device(): pl.pallas_call(_project_kernel, out_shape=jax.ShapeDtypeStruct((2 * resid...  1.87 us
    pallas_call x2, Pallas kernels, per_device(): pl.pallas_call(functools.partial(_middle_kernel, len(group)), out_shape=s...  1.46 us
    pallas_call x1, Pallas kernels, per_device(): pl.pallas_call(_late_kernel, out_shape=[jax.ShapeDtypeStruct((residues //...  1.4 us
    ppermute x1, waiting for transfers between devices, per_device(): other = lax.ppermute(projected, 'row', cores)  1 us
    pallas_call x1, Pallas kernels, per_device(): pl.pallas_call(_last_kernel, out_shape=tile, in_specs=_vmem(7) + [anywher...  0.91 us
    pallas_call x1, Pallas kernels, per_device(): pl.pallas_call(functools.partial(_prepare_kernel, channels), out_shape=[j...  0.78 us
  transfers between devices with their start and end apart: 9, of which 5 were waited for; matrix products, arithmetic and copies ran while one was open for 0% of the time, Pallas kernels for 20%

profile of v7, /device:TPU:0, one launch (start us, length us, event | category | flops | bytes accessed | tf_op | source)
XLA Modules:
  0.0 21.7 jit_solution(6707553411551966701)
XLA Ops:
  0.0 0.0 copy-start
  0.0 1.9 %project.1.own_ref = bf16[272,256]{1,0:T(8,128)(2,1)S(1)} custom-call(bf16[4,128,256]{2,1,0:T(8,128)(2,1)} %x_hbm.1, s32[1,4]{1,0:T(1,128)} %bitcast.15, s32[1,128]{1,0:T(1,128)} %bitcast.11, f32[1,256]{1,0:T(1,128)} %bitcast.13, f32[1,256]{1,0:T(1,128)} %bitcast.14, bf16[32,256]{1,0:T(8,128)(2,1)} %bitcast.9, bf16[32,256]{1,0:T(8,128)(2,1)} %bitcast.10, ...), custom_call_target="tpu_custom_call" | custom-call | tf_op jit(solution)/shard_map/project/pallas_call | solution.py:380
  1.9 0.6 %collective-permute-start = (bf16[272,256]{1,0:T(8,128)(2,1)S(1)}, bf16[272,256]{1,0:T(8,128)(2,1)S(1)}, u32[]{:S(2)}, u32[]{:S(2)}) collective-permute-start(bf16[272,256]{1,0:T(8,128)(2,1)S(1)} %project.1.own_ref), channel_id=1, source_target_pairs={{0,1},{1,0},{2,3},{3,2},{4,5},{5,4},{6,7},{7,6},{8,9},{9,8},{10,11... | collective-permute-start | bytes 417800 | tf_op jit(solution)/shard_map/ppermute | solution.py:390
  2.4 1.0 %collective-permute-done.other_ref = bf16[272,256]{1,0:T(8,128)(2,1)S(1)} collective-permute-done((bf16[272,256]{1,0:T(8,128)(2,1)S(1)}, bf16[272,256]{1,0:T(8,128)(2,1)S(1)}, u32[]{:S(2)}, u32[]{:S(2)}) %collective-permute-start) | collective-permute-done | bytes 139296 | tf_op jit(solution)/shard_map/ppermute | solution.py:390
  3.5 6.0 %collective-permute-start.1 = (bf16[152,256]{1,0:T(8,128)(2,1)S(1)}, bf16[152,256]{1,0:T(8,128)(2,1)S(1)}, u32[]{:S(2)}, u32[]{:S(2)}) collective-permute-start(bf16[152,256]{1,0:T(8,128)(2,1)S(1)} %get-tuple-element.29), channel_id=1, source_target_pairs={{1,13},{3,15},{5,9},{7,11},{9,5},{11,7},{13,1},{15,3},{0,14},{2,12... | collective-permute-start | bytes 233480 | tf_op jit(solution)/shard_map/ppermute | solution.py:405
  9.4 0.5 %collective-permute-start.2 = (bf16[152,256]{1,0:T(8,128)(2,1)S(1)}, bf16[152,256]{1,0:T(8,128)(2,1)S(1)}, u32[]{:S(2)}, u32[]{:S(2)}) collective-permute-start(bf16[152,256]{1,0:T(8,128)(2,1)S(1)} %get-tuple-element.32), channel_id=1, source_target_pairs={{1,9},{3,11},{5,13},{7,15},{9,1},{11,3},{13,5},{15,7},{0,2},{2,0},... | collective-permute-start | bytes 233480 | tf_op jit(solution)/shard_map/ppermute | solution.py:405
  9.9 0.5 %collective-permute-start.4 = (bf16[152,256]{1,0:T(8,128)(2,1)S(1)}, bf16[152,256]{1,0:T(8,128)(2,1)S(1)}, u32[]{:S(2)}, u32[]{:S(2)}) collective-permute-start(bf16[152,256]{1,0:T(8,128)(2,1)S(1)} %get-tuple-element.35), channel_id=1, source_target_pairs={{1,5},{3,7},{5,1},{7,3},{9,13},{11,15},{13,9},{15,11},{0,6},{2,4},... | collective-permute-start | bytes 233480 | tf_op jit(solution)/shard_map/ppermute | solution.py:405
  10.4 1.1 %collective-permute-start.6 = (bf16[80,256]{1,0:T(8,128)(2,1)S(1)}, bf16[80,256]{1,0:T(8,128)(2,1)S(1)}, u32[]{:S(2)}, u32[]{:S(2)}) collective-permute-start(bf16[80,256]{1,0:T(8,128)(2,1)S(1)} %get-tuple-element.38), channel_id=1, source_target_pairs={{1,11},{3,9},{5,15},{7,13},{9,3},{11,1},{13,7},{15,5},{0,10},{2,8}... | collective-permute-start | bytes 122888 | tf_op jit(solution)/shard_map/ppermute | solution.py:405
  11.5 1.0 %collective-permute-done.1.refs_1_ = bf16[152,256]{1,0:T(8,128)(2,1)S(1)} collective-permute-done((bf16[152,256]{1,0:T(8,128)(2,1)S(1)}, bf16[152,256]{1,0:T(8,128)(2,1)S(1)}, u32[]{:S(2)}, u32[]{:S(2)}) %collective-permute-start.1) | collective-permute-done | bytes 77856 | tf_op jit(solution)/shard_map/ppermute | solution.py:405
  12.6 0.0 collective-permute-start.3
  12.6 1.3 %collective-permute-done.2.refs_0_ = bf16[152,256]{1,0:T(8,128)(2,1)S(1)} collective-permute-done((bf16[152,256]{1,0:T(8,128)(2,1)S(1)}, bf16[152,256]{1,0:T(8,128)(2,1)S(1)}, u32[]{:S(2)}, u32[]{:S(2)}) %collective-permute-start.2) | collective-permute-done | bytes 77856 | tf_op jit(solution)/shard_map/ppermute | solution.py:405
  13.8 0.0 collective-permute-start.5
  13.8 2.0 %collective-permute-done.4.refs_0_ = bf16[152,256]{1,0:T(8,128)(2,1)S(1)} collective-permute-done((bf16[152,256]{1,0:T(8,128)(2,1)S(1)}, bf16[152,256]{1,0:T(8,128)(2,1)S(1)}, u32[]{:S(2)}, u32[]{:S(2)}) %collective-permute-start.4) | collective-permute-done | bytes 77856 | tf_op jit(solution)/shard_map/ppermute | solution.py:405
  15.8 0.0 collective-permute-start.7
  15.8 0.4 %collective-permute-done.6.shared_ref = bf16[80,256]{1,0:T(8,128)(2,1)S(1)} collective-permute-done((bf16[80,256]{1,0:T(8,128)(2,1)S(1)}, bf16[80,256]{1,0:T(8,128)(2,1)S(1)}, u32[]{:S(2)}, u32[]{:S(2)}) %collective-permute-start.6) | collective-permute-done | bytes 40992 | tf_op jit(solution)/shard_map/ppermute | solution.py:405
  16.3 0.1 collective-permute-start.8
  16.4 0.0 copy-done
  16.4 0.8 %prepare.1 = (bf16[32,4096]{1,0:T(8,128)(2,1)S(1)}, f32[128,128]{1,0:T(8,128)S(1)}, f32[8,128]{1,0:T(8,128)S(1)}, f32[1,128]{1,0:T(1,128)S(1)}) custom-call(bf16[1024,128]{1,0:T(8,128)(2,1)S(1)} %copy-done, s32[1,128]{1,0:T(1,128)} %bitcast.12, f32[1,128]{1,0:T(1,128)} %bitcast.18), custom_call_target="tpu_custom_call" | custom-call | tf_op jit(solution)/shard_map/prepare/pallas_call | solution.py:413
  17.1 0.7 %early.1 = (f32[128,1024]{1,0:T(8,128)S(1)}, f32[8,256]{1,0:T(8,128)S(1)}) custom-call(bf16[32,4096]{1,0:T(8,128)(2,1)S(1)} %get-tuple-element.27.w_ref, bf16[152,256]{1,0:T(8,128)(2,1)S(1)} %get-tuple-element.28.refs_0_, bf16[152,256]{1,0:T(8,128)(2,1)S(1)} %collective-permute-done.1.refs_1_), custom_call_target="tpu_custom_call" | custom-call | tf_op jit(solution)/shard_map/early/pallas_call | solution.py:434
  17.9 0.0 collective-permute-done.3.refs_1_
  17.9 0.7 %shard_map.109 = (f32[128,1024]{1,0:T(8,128)S(1)}, f32[8,256]{1,0:T(8,128)S(1)}) custom-call(bf16[32,4096]{1,0:T(8,128)(2,1)S(1)} %get-tuple-element.27.w_ref, f32[128,1024]{1,0:T(8,128)S(1)} %get-tuple-element.30.sum_in, f32[8,256]{1,0:T(8,128)S(1)} %get-tuple-element.31.flags_in, bf16[152,256]{1,0:T(8,128)(2,1)S(1)} %collective-permute-done.2.refs_0_, ...), custom_call_target="tpu_custom_call" | custom-call | tf_op jit(solution)/shard_map/pallas_call | solution.py:448
  18.6 0.0 collective-permute-done.5.refs_1_
  18.6 0.7 %shard_map.110 = (f32[128,1024]{1,0:T(8,128)S(1)}, f32[8,256]{1,0:T(8,128)S(1)}) custom-call(bf16[32,4096]{1,0:T(8,128)(2,1)S(1)} %get-tuple-element.27.w_ref, f32[128,1024]{1,0:T(8,128)S(1)} %get-tuple-element.33.sum_in, f32[8,256]{1,0:T(8,128)S(1)} %get-tuple-element.34.flags_in, bf16[152,256]{1,0:T(8,128)(2,1)S(1)} %collective-permute-done.4.refs_0_, ...), custom_call_target="tpu_custom_call" | custom-call | tf_op jit(solution)/shard_map/pallas_call | solution.py:448
  19.4 0.0 collective-permute-done.7.parcel_ref
  19.4 1.4 %late.1 = (f32[64,1024]{1,0:T(8,128)S(1)}, f32[8,256]{1,0:T(8,128)S(1)}, bf16[256,1024]{1,0:T(8,128)(2,1)S(1)}, bf16[8,128,128]{2,1,0:T(8,128)(2,1)}) custom-call(bf16[32,4096]{1,0:T(8,128)(2,1)S(1)} %get-tuple-element.27.w_ref, f32[128,128]{1,0:T(8,128)S(1)} %get-tuple-element.24.column_ref, f32[8,128]{1,0:T(8,128)S(1)} %get-tuple-element.25.own_ref, ...), custom_call_target="tpu_custom_call" | custom-call | tf_op jit(solution)/shard_map/late/pallas_call | solution.py:461
  20.8 0.0 collective-permute-done.8.other_ref
  20.8 0.9 %last.1 = bf16[8,128,128]{2,1,0:T(8,128)(2,1)} custom-call(f32[128,128]{1,0:T(8,128)S(1)} %get-tuple-element.24.column_ref, f32[8,128]{1,0:T(8,128)S(1)} %get-tuple-element.25.own_ref, f32[1,128]{1,0:T(1,128)S(1)} %get-tuple-element.26.bias_ref, f32[64,1024]{1,0:T(8,128)S(1)} %get-tuple-element.39.rest_ref, ...), custom_call_target="tpu_custom_call", output_to_operand_aliasing={{}: (7, {})} | custom-call | tf_op jit(solution)/shard_map/last/pallas_call | solution.py:475
  (1 shorter events, 0.0 us)
Async XLA Ops:
  0.0 16.4 %copy-start = (bf16[1024,128]{1,0:T(8,128)(2,1)S(1)}, bf16[1024,128]{1,0:T(8,128)(2,1)}, u32[]{:S(2)}) copy-start(bf16[1024,128]{1,0:T(8,128)(2,1)} %raw_ref.1) | copy-start | bytes 786436
  1.9 1.6 %collective-permute-start = (bf16[272,256]{1,0:T(8,128)(2,1)S(1)}, bf16[272,256]{1,0:T(8,128)(2,1)S(1)}, u32[]{:S(2)}, u32[]{:S(2)}) collective-permute-start(bf16[272,256]{1,0:T(8,128)(2,1)S(1)} %project.1.own_ref), channel_id=1, source_target_pairs={{0,1},{1,0},{2,3},{3,2},{4,5},{5,4},{6,7},{7,6},{8,9},{9,8},{10,11... | collective-permute-start | bytes 417800 | tf_op jit(solution)/shard_map/ppermute | solution.py:390
  3.5 9.1 %collective-permute-start.1 = (bf16[152,256]{1,0:T(8,128)(2,1)S(1)}, bf16[152,256]{1,0:T(8,128)(2,1)S(1)}, u32[]{:S(2)}, u32[]{:S(2)}) collective-permute-start(bf16[152,256]{1,0:T(8,128)(2,1)S(1)} %get-tuple-element.29), channel_id=1, source_target_pairs={{1,13},{3,15},{5,9},{7,11},{9,5},{11,7},{13,1},{15,3},{0,14},{2,12... | collective-permute-start | bytes 233480 | tf_op jit(solution)/shard_map/ppermute | solution.py:405
  9.4 4.4 %collective-permute-start.2 = (bf16[152,256]{1,0:T(8,128)(2,1)S(1)}, bf16[152,256]{1,0:T(8,128)(2,1)S(1)}, u32[]{:S(2)}, u32[]{:S(2)}) collective-permute-start(bf16[152,256]{1,0:T(8,128)(2,1)S(1)} %get-tuple-element.32), channel_id=1, source_target_pairs={{1,9},{3,11},{5,13},{7,15},{9,1},{11,3},{13,5},{15,7},{0,2},{2,0},... | collective-permute-start | bytes 233480 | tf_op jit(solution)/shard_map/ppermute | solution.py:405
  9.9 5.9 %collective-permute-start.4 = (bf16[152,256]{1,0:T(8,128)(2,1)S(1)}, bf16[152,256]{1,0:T(8,128)(2,1)S(1)}, u32[]{:S(2)}, u32[]{:S(2)}) collective-permute-start(bf16[152,256]{1,0:T(8,128)(2,1)S(1)} %get-tuple-element.35), channel_id=1, source_target_pairs={{1,5},{3,7},{5,1},{7,3},{9,13},{11,15},{13,9},{15,11},{0,6},{2,4},... | collective-permute-start | bytes 233480 | tf_op jit(solution)/shard_map/ppermute | solution.py:405
  10.4 5.8 %collective-permute-start.6 = (bf16[80,256]{1,0:T(8,128)(2,1)S(1)}, bf16[80,256]{1,0:T(8,128)(2,1)S(1)}, u32[]{:S(2)}, u32[]{:S(2)}) collective-permute-start(bf16[80,256]{1,0:T(8,128)(2,1)S(1)} %get-tuple-element.38), channel_id=1, source_target_pairs={{1,11},{3,9},{5,15},{7,13},{9,3},{11,1},{13,7},{15,5},{0,10},{2,8}... | collective-permute-start | bytes 122888 | tf_op jit(solution)/shard_map/ppermute | solution.py:405
  12.6 5.3 %collective-permute-start.3 = (bf16[152,256]{1,0:T(8,128)(2,1)S(1)}, bf16[152,256]{1,0:T(8,128)(2,1)S(1)}, u32[]{:S(2)}, u32[]{:S(2)}) collective-permute-start(bf16[152,256]{1,0:T(8,128)(2,1)S(1)} %collective-permute-done.1.refs_1_), channel_id=1, source_target_pairs={{0,1},{1,0},{2,3},{3,2},{4,5},{5,4},{6,7},{7,6},{8,9},{9,8},{10,11... | collective-permute-start | bytes 233480 | tf_op jit(solution)/shard_map/ppermute | solution.py:406
  13.8 4.8 %collective-permute-start.5 = (bf16[152,256]{1,0:T(8,128)(2,1)S(1)}, bf16[152,256]{1,0:T(8,128)(2,1)S(1)}, u32[]{:S(2)}, u32[]{:S(2)}) collective-permute-start(bf16[152,256]{1,0:T(8,128)(2,1)S(1)} %collective-permute-done.2.refs_0_), channel_id=1, source_target_pairs={{0,1},{1,0},{2,3},{3,2},{4,5},{5,4},{6,7},{7,6},{8,9},{9,8},{10,11... | collective-permute-start | bytes 233480 | tf_op jit(solution)/shard_map/ppermute | solution.py:406
  15.8 3.5 %collective-permute-start.7 = (bf16[152,256]{1,0:T(8,128)(2,1)S(1)}, bf16[152,256]{1,0:T(8,128)(2,1)S(1)}, u32[]{:S(2)}, u32[]{:S(2)}) collective-permute-start(bf16[152,256]{1,0:T(8,128)(2,1)S(1)} %collective-permute-done.4.refs_0_), channel_id=1, source_target_pairs={{0,1},{1,0},{2,3},{3,2},{4,5},{5,4},{6,7},{7,6},{8,9},{9,8},{10,11... | collective-permute-start | bytes 233480 | tf_op jit(solution)/shard_map/ppermute | solution.py:406
  16.3 4.5 %collective-permute-start.8 = (bf16[80,256]{1,0:T(8,128)(2,1)S(1)}, bf16[80,256]{1,0:T(8,128)(2,1)S(1)}, u32[]{:S(2)}, u32[]{:S(2)}) collective-permute-start(bf16[80,256]{1,0:T(8,128)(2,1)S(1)} %collective-permute-done.6.shared_ref), channel_id=1, source_target_pairs={{0,1},{1,0},{2,3},{3,2},{4,5},{5,4},{6,7},{7,6},{8,9},{9,8},{10,11... | collective-permute-start | bytes 122888 | tf_op jit(solution)/shard_map/ppermute | solution.py:406
